TPU v7x, 128 devices: a whole 4x4x4 slice. The times are simulated.
128 devices in a mesh: dp: 128 (over z, y, x, core).
Axes of the slice: x: 4, y: 4, z: 4, core: 2. Of those that a mesh axis runs over, the one named last changes fastest.
Arguments:
- q_hidden: bfloat16 [512, 48, 1024], P('dp')
- q_mask: int32 [512, 48], P('dp')
- p_hidden: bfloat16 [512, 2, 128, 1024], P('dp')
- p_mask: int32 [512, 2, 128], P('dp')
- w_qkv: bfloat16 [1024, 3, 16, 64], replicated
- b_qkv: float32 [3, 16, 64], replicated
- w_out: bfloat16 [16, 64, 1024], replicated
- b_out: float32 [1024], replicated
- ln1_gain: float32 [1024], replicated
- ln1_shift: float32 [1024], replicated
- w_up: bfloat16 [1024, 4096], replicated
- b_up: float32 [4096], replicated
- w_down: bfloat16 [4096, 1024], replicated
- b_down: float32 [1024], replicated
- ln2_gain: float32 [1024], replicated
- ln2_shift: float32 [1024], replicated
Outputs:
- output 1: float32 [], replicated
- output 2: bfloat16 [512, 48, 1024], P('dp')
- output 3: bfloat16 [512, 2, 128, 1024], P('dp')
- output 4: float32 [1024, 3, 16, 64], replicated
- output 5: float32 [3, 16, 64], replicated
- output 6: float32 [16, 64, 1024], replicated
- output 7: float32 [1024], replicated
- output 8: float32 [1024], replicated
- output 9: float32 [1024], replicated
- output 10: float32 [1024, 4096], replicated
- output 11: float32 [4096], replicated
- output 12: float32 [4096, 1024], replicated
- output 13: float32 [1024], replicated
- output 14: float32 [1024], replicated
- output 15: float32 [1024], replicated
All inputs are finite; a program needn't handle non-finite values.
Results may differ from a plain program's by a relative error of at most 0.0126557.
Values sent between devices are 32-bit elements.
A program may use at most 1 GiB of HBM per device.

v0:
```python
import math
import jax
import jax.numpy as jnp
from jax import lax
from jax.sharding import PartitionSpec as P

INV_TEMP = 100.0
LN_EPS = 1e-12
NEG_FILL = -1e9
FULL_PREC = lax.Precision.HIGHEST


def layer_norm(resid_in, ln_gain, ln_shift):
    row_mean = jnp.mean(resid_in, axis=-1, keepdims=True)
    centered = resid_in - row_mean
    row_var = jnp.mean(centered * centered, axis=-1, keepdims=True)
    return centered * lax.rsqrt(row_var + LN_EPS) * ln_gain + ln_shift


def gelu_grad(pre_act):
    normal_cdf = 0.5 * (1.0 + lax.erf(pre_act * (2.0 ** -0.5)))
    return normal_cdf + pre_act * jnp.exp(-0.5 * pre_act * pre_act) * ((2.0 * math.pi) ** -0.5)


def encoder_fwd(hidden, tok_mask, weights):
    w_qkv, b_qkv, w_out, b_out, ln1_gain, ln1_shift, w_up, b_up, w_down, b_down, ln2_gain, ln2_shift = weights
    attn_scale = w_qkv.shape[-1] ** -0.5
    qkv_proj = (jnp.einsum('ntd,dshe->snthe', hidden, w_qkv, preferred_element_type=jnp.float32)
                + b_qkv[:, None, None]).astype(jnp.bfloat16)
    scores = jnp.einsum('nqhe,nkhe->nhqk', qkv_proj[0], qkv_proj[1], preferred_element_type=jnp.float32) * attn_scale
    key_keep = (tok_mask > 0)[:, None, None, :]
    attn_probs = jax.nn.softmax(jnp.where(key_keep, scores, NEG_FILL), axis=-1).astype(jnp.bfloat16)
    context = jnp.einsum('nhqk,nkhe->nqhe', attn_probs, qkv_proj[2], preferred_element_type=jnp.float32).astype(jnp.bfloat16)
    resid1 = hidden.astype(jnp.float32) + jnp.einsum('nqhe,hed->nqd', context, w_out, preferred_element_type=jnp.float32) + b_out
    normed1 = layer_norm(resid1, ln1_gain, ln1_shift).astype(jnp.bfloat16)
    pre_act = jnp.einsum('ntd,df->ntf', normed1, w_up, preferred_element_type=jnp.float32) + b_up
    ffn_act = jax.nn.gelu(pre_act, approximate=False).astype(jnp.bfloat16)
    resid2 = normed1.astype(jnp.float32) + jnp.einsum('ntf,fd->ntd', ffn_act, w_down, preferred_element_type=jnp.float32) + b_down
    layer_out = layer_norm(resid2, ln2_gain, ln2_shift)
    mask_f = tok_mask.astype(jnp.float32)
    pool_wts = mask_f / jnp.sum(mask_f, axis=1, keepdims=True)
    pooled = jnp.einsum('ntd,nt->nd', layer_out, pool_wts)
    inv_norm = lax.rsqrt(jnp.sum(pooled * pooled, axis=-1, keepdims=True))
    embedding = pooled * inv_norm
    fwd_saved = (hidden, pool_wts, qkv_proj, attn_probs, context, resid1, normed1, pre_act, ffn_act, resid2, embedding, inv_norm)
    return embedding, fwd_saved


def encoder_bwd(d_embedding, fwd_saved, weights):
    w_qkv, b_qkv, w_out, b_out, ln1_gain, ln1_shift, w_up, b_up, w_down, b_down, ln2_gain, ln2_shift = weights
    hidden, pool_wts, qkv_proj, attn_probs, context, resid1, normed1, pre_act, ffn_act, resid2, embedding, inv_norm = fwd_saved
    attn_scale = w_qkv.shape[-1] ** -0.5
    d_pooled = (d_embedding - embedding * jnp.sum(embedding * d_embedding, axis=-1, keepdims=True)) * inv_norm
    d_layer_out = d_pooled[:, None, :] * pool_wts[:, :, None]
    unused_ln2, ln2_pull = jax.vjp(layer_norm, resid2, ln2_gain, ln2_shift)
    d_resid2, d_ln2_gain, d_ln2_shift = ln2_pull(d_layer_out)
    d_b_down = jnp.sum(d_resid2, axis=(0, 1))
    d_resid2_lo = d_resid2.astype(jnp.bfloat16)
    d_w_down = jnp.einsum('ntf,ntd->fd', ffn_act, d_resid2_lo, preferred_element_type=jnp.float32)
    d_ffn_act = jnp.einsum('ntd,fd->ntf', d_resid2_lo, w_down, preferred_element_type=jnp.float32).astype(jnp.bfloat16)
    d_pre_act = d_ffn_act * gelu_grad(pre_act)
    d_b_up = jnp.sum(d_pre_act, axis=(0, 1))
    d_pre_lo = d_pre_act.astype(jnp.bfloat16)
    d_w_up = jnp.einsum('ntd,ntf->df', normed1, d_pre_lo, preferred_element_type=jnp.float32)
    d_normed1 = (jnp.einsum('ntf,df->ntd', d_pre_lo, w_up, preferred_element_type=jnp.float32)
                 + d_resid2).astype(jnp.bfloat16).astype(jnp.float32)
    unused_ln1, ln1_pull = jax.vjp(layer_norm, resid1, ln1_gain, ln1_shift)
    d_resid1, d_ln1_gain, d_ln1_shift = ln1_pull(d_normed1)
    d_b_out = jnp.sum(d_resid1, axis=(0, 1))
    d_resid1_lo = d_resid1.astype(jnp.bfloat16)
    d_w_out = jnp.einsum('nqhe,nqd->hed', context, d_resid1_lo, preferred_element_type=jnp.float32)
    d_context = jnp.einsum('nqd,hed->nqhe', d_resid1_lo, w_out, preferred_element_type=jnp.float32).astype(jnp.bfloat16)
    d_probs = jnp.einsum('nqhe,nkhe->nhqk', d_context, qkv_proj[2], preferred_element_type=jnp.float32)
    d_value = jnp.einsum('nhqk,nqhe->nkhe', attn_probs, d_context, preferred_element_type=jnp.float32).astype(jnp.bfloat16)
    row_dot = jnp.sum(d_probs * attn_probs, axis=-1, keepdims=True)
    d_scores = (attn_probs * (d_probs - row_dot) * attn_scale).astype(jnp.bfloat16)
    d_query = jnp.einsum('nhqk,nkhe->nqhe', d_scores, qkv_proj[1], preferred_element_type=jnp.float32).astype(jnp.bfloat16)
    d_key = jnp.einsum('nhqk,nqhe->nkhe', d_scores, qkv_proj[0], preferred_element_type=jnp.float32).astype(jnp.bfloat16)
    d_proj = jnp.stack([d_query, d_key, d_value])
    d_b_qkv = jnp.sum(d_proj, axis=(1, 2), dtype=jnp.float32)
    d_w_qkv = jnp.einsum('ntd,snthe->dshe', hidden, d_proj, preferred_element_type=jnp.float32)
    d_hidden = (d_resid1 + jnp.einsum('snthe,dshe->ntd', d_proj, w_qkv, preferred_element_type=jnp.float32)).astype(jnp.bfloat16)
    weight_grads = (d_w_qkv, d_b_qkv, d_w_out, d_b_out, d_ln1_gain, d_ln1_shift,
                    d_w_up, d_b_up, d_w_down, d_b_down, d_ln2_gain, d_ln2_shift)
    return d_hidden, weight_grads


def solution(mesh):
    batch_axis = mesh.axis_names[0]
    n_dev = mesh.shape[batch_axis]

    def local_step(q_hidden, q_mask, p_hidden, p_mask, *weights):
        n_local, n_cand, p_len, model_width = p_hidden.shape
        n_total = n_local * n_dev
        grad_scale = INV_TEMP / n_total
        q_embed, q_saved = encoder_fwd(q_hidden, q_mask, weights)
        p_embed, p_saved = encoder_fwd(p_hidden.reshape(n_local * n_cand, p_len, model_width),
                                       p_mask.reshape(n_local * n_cand, p_len), weights)
        all_pass = lax.all_gather(p_embed, batch_axis, axis=0, tiled=True)
        logits = jnp.einsum('id,jd->ij', q_embed, all_pass, preferred_element_type=jnp.float32, precision=FULL_PREC) * INV_TEMP
        pos_pass = p_embed.reshape(n_local, n_cand, model_width)[:, 0]
        positive = jnp.sum(q_embed * pos_pass, axis=-1) * INV_TEMP
        log_norm = jax.nn.logsumexp(logits, axis=-1)
        mean_loss = lax.psum(jnp.sum(log_norm - positive), batch_axis) / n_total
        d_logits = jnp.exp(logits - log_norm[:, None]) * grad_scale
        d_q_embed = jnp.einsum('ij,jd->id', d_logits, all_pass, preferred_element_type=jnp.float32, precision=FULL_PREC) - pos_pass * grad_scale
        d_all_pass = jnp.einsum('ij,id->jd', d_logits, q_embed, preferred_element_type=jnp.float32, precision=FULL_PREC)
        d_p_embed = lax.psum_scatter(d_all_pass, batch_axis, scatter_dimension=0, tiled=True)
        pos_term = jnp.stack([q_embed] + [jnp.zeros_like(q_embed)] * (n_cand - 1), axis=1).reshape(n_local * n_cand, model_width)
        d_p_embed = d_p_embed - pos_term * grad_scale
        d_q_hidden, q_grads = encoder_bwd(d_q_embed, q_saved, weights)
        d_p_hidden, p_grads = encoder_bwd(d_p_embed, p_saved, weights)
        local_grads = [q_part + p_part for q_part, p_part in zip(q_grads, p_grads)]
        total_grads = lax.psum(local_grads, batch_axis)
        return (mean_loss, d_q_hidden, d_p_hidden.reshape(p_hidden.shape)) + tuple(total_grads)

    in_specs = (P(batch_axis),) * 4 + (P(),) * 12
    out_specs = (P(), P(batch_axis), P(batch_axis)) + (P(),) * 12
    return jax.shard_map(local_step, mesh=mesh, in_specs=in_specs, out_specs=out_specs, check_vma=False)
```

profile of v0, /device:TPU:1, one launch (start us, length us, event | category | flops | bytes accessed | tf_op | source)
XLA Modules:
  0.0 1393.0 jit_solution(15831607170298365564)
XLA Ops:
  10.1 9.4 fusion.40
  26.5 9.3 fusion.251
  45.9 17.3 %fusion.83 = (u8[128,4096]{1,0:T(8,128)(4,1)}, u8[128,4096]{1,0:T(8,128)(4,1)}, f32[8,128,4096]{2,1,0:T(8,128)S(1)}) fusion(f32[4096]{0:T(1024)S(1)} %copy-done.57, bf16[8,128,1024]{2,1,0:T(8,128)(2,1)S(1)} %add_convert_fusion.3, bf16[1024,4096]{1,0:T(8,128)(2,1)} %param.26), kind=kOutput, calls=%fused_computation.118 | convolution fusion | flops 8647606272 | bytes 28327936 | tf_op jit(solution)/shard_map/ntd,df->ntf/dot_general | solution.py:36
  63.1 40.5 %fusion.6 = bf16[8,128,4096]{2,1,0:T(8,128)(2,1)} fusion(f32[8,128,4096]{2,1,0:T(8,128)S(1)} %get-tuple-element.63, f32[4096]{0:T(1024)S(1)} %copy-done.57, u8[128,4096]{1,0:T(8,128)(4,1)} %get-tuple-element.16, u8[128,4096]{1,0:T(8,128)(4,1)} %get-tuple-element.15), kind=kLoop, calls=%fused_computation.8 | loop fusion | flops 297795584 | bytes 26230784 | tf_op jit(solution)/shard_map/convert_element_type | solution.py:37
  103.7 13.9 fusion.253
  120.6 9.6 fusion.101
  155.6 35.3 %all-gather.2.cloned.1.call-done = f32[1024,1024]{1,0:T(8,128)} async-done(((f32[8,1024]{1,0:T(8,128)}), f32[1024,1024]{1,0:T(8,128)}) %all-gather.2.cloned.1.call-update) | async-done | bytes 4194320 | tf_op jit(solution)/shard_map/all_gather | solution.py:99
  215.6 7.8 multiply_reduce_fusion.4
  243.1 8.6 fusion.186
  251.7 8.3 fusion.215
  267.1 575.2 %reduce-scatter.2.cloned.1.call-done = f32[8,1024]{1,0:T(8,128)} async-done(((f32[1024,1024]{1,0:T(8,128)}), f32[8,1024]{1,0:T(8,128)}) %reduce-scatter.2.cloned.1.call-update) | async-done | bytes 32784 | tf_op jit(solution)/shard_map/reduce_scatter | solution.py:108
  848.3 21.5 %fusion.263 = (f32[4096]{0:T(1024)S(1)}, bf16[8,128,4096]{2,1,0:T(8,128)(2,1)}) fusion(f32[8,128,4096]{2,1,0:T(8,128)} %copy-done.9, f32[4096]{0:T(1024)S(1)} %copy-done.57, bf16[4096,1024]{1,0:T(8,128)(2,1)} %param.28, f32[8,128]{1,0:T(8,128)S(1)} %negate_multiply_fusion.3, f32[8,128]{1,0:T(8,128)S(1)} %multiply_multiply_fusion.17, ...), kind=kOutput, calls=%fused_computation.337 | convolution fusion | flops 8658087936 | bytes 37838848 | tf_op jit(solution)/shard_map/ntd,fd->ntf/dot_general | solution.py:60
  869.8 17.1 %fusion.68 = (f32[1024]{0:T(1024)S(1)}, f32[8,128]{1,0:T(8,128)S(1)}, f32[1024]{0:T(1024)S(1)}, bf16[8,128,1024]{2,1,0:T(8,128)(2,1)}) fusion(f32[8,128,1024]{2,1,0:T(8,128)S(1)} %copy-done.2, f32[8,128]{1,0:T(8,128)S(1)} %fusion.226, f32[8,128]{1,0:T(8,128)S(1)} %broadcast_multiply_fusion.1, f32[1024]{0:T(1024)S(1)} %copy-done.49, ...), kind=kOutput, calls=%fused_computation.95 | convolution fusion | flops 8609854464 | bytes 27344896 | tf_op jit(solution)/shard_map/ntf,df->ntd/dot_general | solution.py:65
  903.7 12.8 convert_bitcast_fusion.2
  916.5 12.9 convert_bitcast_fusion.1
  929.4 8.4 bitcast_add_fusion.4
  937.8 19.9 %bitcast_add_fusion = f32[4096,1024]{1,0:T(8,128)} fusion(f32[4096,1024,1]{1,0,2:T(8,128)} %fusion.215, bf16[8,128,4096]{2,1,0:T(8,128)(2,1)} %fusion.6, f32[8,128]{1,0:T(8,128)S(1)} %negate_multiply_fusion.3, f32[8,128,1024]{2,1,0:T(8,128)} %copy-done.3, f32[8,128]{1,0:T(8,128)S(1)} %multiply_multiply_fusion.17, f32[8,128]{1,0:T(8,128)S(1)} %get-tuple-element.83, ...), kind=kOutput, calls=%fused_computation.19 | convolution fusion | flops 8603566080 | bytes 46194688 | tf_op jit(solution)/shard_map/ntf,ntd->fd/dot_general | solution.py:59
  957.8 18.6 %bitcast_add_fusion.1 = f32[1024,4096]{1,0:T(8,128)} fusion(f32[1024,4096,1]{1,0,2:T(8,128)} %fusion.186, bf16[8,128,1024]{2,1,0:T(8,128)(2,1)S(1)} %copy-done.20, bf16[8,128,4096]{2,1,0:T(8,128)(2,1)} %get-tuple-element.80), kind=kOutput, calls=%fused_computation.20 | convolution fusion | flops 8594128896 | bytes 44040192 | tf_op jit(solution)/shard_map/ntd,ntf->df/dot_general | solution.py:64
  976.4 13.4 fusion.18
  1007.1 71.7 %all-reduce.1 = (f32[]{:T(128)}, f32[3,16,64]{2,1,0:T(8,128)}, f32[1024]{0:T(1024)}, f32[1024]{0:T(1024)}, f32[1024]{0:T(1024)}, /*index=5*/f32[4096]{0:T(1024)}, f32[1024]{0:T(1024)}, f32[1024]{0:T(1024)}, f32[1024]{0:T(1024)}) all-reduce(f32[]{:T(128)} %subtract_reduce_fusion, ...), channel_id=1, replica_groups=mesh['dp'=128] {'dp'}, use_global_device_ids=true, to_apply=%region_20.21 | all-reduce | flops 13313 | bytes 106504 | tf_op jit(solution)/shard_map/psum | solution.py:104
  1079.4 12.6 fusion.70
  1092.0 256.3 %all-reduce.5.cloned.1.call-done = (f32[1024,3,16,64]{0,3,2,1:T(8,128)}, f32[16,64,1024]{2,1,0:T(8,128)}, f32[1024,4096]{1,0:T(8,128)}, f32[4096,1024]{1,0:T(8,128)}) async-done(((f32[1024,3,16,64]{0,3,2,1:T(8,128)}, f32[16,64,1024]{2,1,0:T(8,128)}, f32[1024,4096]{1,0:T(8,128)}, f32[4096,1024]{1,0:T(8,128)}), (f32[1024,3,16,64]{0,3,2,1:T(8,128)}, f32[16,64,1024]{2,1,0:T(8,128)}, f32[1024,4096]{1,0:T(8,128)}, ...) | async-done | bytes 50331664 | tf_op jit(solution)/shard_map/psum | solution.py:114
  1348.3 12.2 copy.184
  1362.7 13.9 %copy.186 = f32[1024,4096]{1,0:T(8,128)} copy(f32[1024,4096]{1,0:T(8,128)} %get-tuple-element.98) | data formatting | bytes 33554432
  (259 shorter events, 149.4 us)
Async XLA Ops:
  7.2 32.2 %copy-start = (bf16[16,64,1024]{2,1,0:T(8,128)(2,1)S(1)}, bf16[16,64,1024]{2,1,0:T(8,128)(2,1)}, u32[]{:S(2)}) copy-start(bf16[16,64,1024]{2,1,0:T(8,128)(2,1)} %param.22) | copy-start | bytes 6291460
  7.2 183.6 %all-gather.2.cloned.1.call-start = ((), (), s32[]{:S(2)}) async-start(), calls=%async_computation.1 | async-start | bytes 4227072 | tf_op jit(solution)/shard_map/all_gather | solution.py:99
  21.3 16.0 %copy-start.7 = (bf16[8,128,16,64]{1,3,0,2:T(8,128)(2,1)}, bf16[8,128,16,64]{1,3,0,2:T(8,128)(2,1)S(1)}, u32[]{:S(2)}) copy-start(bf16[8,128,16,64]{1,3,0,2:T(8,128)(2,1)S(1)} %get-tuple-element.52) | copy-start | bytes 6291460
  45.9 57.8 %copy-start.19 = (bf16[8,128,1024]{2,1,0:T(8,128)(2,1)}, bf16[8,128,1024]{2,1,0:T(8,128)(2,1)S(1)}, u32[]{:S(2)}) copy-start(bf16[8,128,1024]{2,1,0:T(8,128)(2,1)S(1)} %add_convert_fusion.3) | copy-start | bytes 6291460
  63.1 40.6 %copy-start.9 = (f32[8,128,4096]{2,1,0:T(8,128)}, f32[8,128,4096]{2,1,0:T(8,128)S(1)}, u32[]{:S(2)}) copy-start(f32[8,128,4096]{2,1,0:T(8,128)S(1)} %get-tuple-element.63) | copy-start | bytes 50331652
  63.1 40.6 %copy-start.65 = (f32[1024]{0:T(1024)S(1)}, f32[1024]{0:T(1024)}, u32[]{:S(2)}) copy-start(f32[1024]{0:T(1024)} %param.29) | copy-start | bytes 12292
  103.7 13.9 %copy-start.62 = (f32[8]{0:T(128)S(1)}, f32[8]{0:T(128)}, u32[]{:S(2)}) copy-start(f32[8]{0:T(128)} %div.135) | copy-start | bytes 100
  120.4 721.9 %reduce-scatter.2.cloned.1.call-start = ((), (), s32[]{:S(2)}) async-start(), calls=%async_computation.2 | async-start | bytes 4227072 | tf_op jit(solution)/shard_map/reduce_scatter | solution.py:108
  138.9 13.9 slice-start.4
  139.1 13.7 slice-start.5
  154.8 96.9 %copy-start.12 = (f32[4,48,1024]{2,1,0:T(8,128)}, f32[4,48,1024]{2,1,0:T(8,128)S(1)}, u32[]{:S(2)}) copy-start(f32[4,48,1024]{2,1,0:T(8,128)S(1)} %get-tuple-element.72) | copy-start | bytes 2359300
  202.2 1146.1 %all-reduce.5.cloned.1.call-start = ((), (), s32[]{:S(2)}) async-start(), calls=%async_computation.3 | async-start | bytes 100663296 | tf_op jit(solution)/shard_map/psum | solution.py:114
  223.7 15.0 %copy-start.52 = (f32[4,48]{1,0:T(4,128)}, f32[4,48]{1,0:T(4,128)S(1)}, u32[]{:S(2)}) copy-start(f32[4,48]{1,0:T(4,128)S(1)} %negate_multiply_fusion.4) | copy-start | bytes 2308
  238.7 21.3 %copy-start.28 = (bf16[1,4,48,16,64]{4,2,3,1,0:T(8,128)(2,1)}, bf16[1,4,48,16,64]{4,2,3,1,0:T(8,128)(2,1)S(1)}, u32[]{:S(2)}) copy-start(bf16[1,4,48,16,64]{4,2,3,1,0:T(8,128)(2,1)S(1)} %fusion.147) | copy-start | bytes 1179652
  848.3 21.5 %copy-start.2 = (f32[8,128,1024]{2,1,0:T(8,128)S(1)}, f32[8,128,1024]{2,1,0:T(8,128)}, u32[]{:S(2)}) copy-start(f32[8,128,1024]{2,1,0:T(8,128)} %copy-done.1) | copy-start | bytes 12582916
  869.8 17.1 %copy-start.51 = (f32[8,128]{1,0:T(8,128)S(1)}, f32[8,128]{1,0:T(8,128)}, u32[]{:S(2)}) copy-start(f32[8,128]{1,0:T(8,128)} %copy-done.50) | copy-start | bytes 12292
  937.8 19.9 %copy-start.20 = (bf16[8,128,1024]{2,1,0:T(8,128)(2,1)S(1)}, bf16[8,128,1024]{2,1,0:T(8,128)(2,1)}, u32[]{:S(2)}) copy-start(bf16[8,128,1024]{2,1,0:T(8,128)(2,1)} %copy-done.19) | copy-start | bytes 6291460
  957.8 18.7 %copy-start.15 = (bf16[1,8,128,16,64]{2,4,3,1,0:T(8,128)(2,1)S(1)}, bf16[1,8,128,16,64]{2,4,3,1,0:T(8,128)(2,1)}, u32[]{:S(2)}) copy-start(bf16[1,8,128,16,64]{2,4,3,1,0:T(8,128)(2,1)} %convert_bitcast_fusion) | copy-start | bytes 6291460
  957.8 18.7 %copy-start.39 = (bf16[4,2,128,1024]{3,2,1,0:T(8,128)(2,1)S(1)}, bf16[4,2,128,1024]{3,2,1,0:T(8,128)(2,1)}, u32[]{:S(2)}) copy-start(bf16[4,2,128,1024]{3,2,1,0:T(8,128)(2,1)} %param.18) | copy-start | bytes 6291460
  1348.3 12.2 copy-start.30
  1360.5 16.1 %slice-start = ((s8[16777216]{0:T(1024)(128)(4,1)}), s8[4194304]{0:T(1024)(128)(4,1)S(1)}, s32[]{:S(2)}) async-start(s8[16777216]{0:T(1024)(128)(4,1)} %bitcast.307), calls=%async_computation.4 | async-start | bytes 8388608
  1362.7 14.0 %slice-start.1 = ((s8[16777216]{0:T(1024)(128)(4,1)}), s8[4194304]{0:T(1024)(128)(4,1)S(1)}, s32[]{:S(2)}) async-start(s8[16777216]{0:T(1024)(128)(4,1)} %bitcast.307), calls=%async_computation.5 | async-start | bytes 8388608
  1362.7 14.2 %slice-start.2 = ((s8[16777216]{0:T(1024)(128)(4,1)}), s8[4194304]{0:T(1024)(128)(4,1)S(1)}, s32[]{:S(2)}) async-start(s8[16777216]{0:T(1024)(128)(4,1)} %bitcast.307), calls=%async_computation.6 | async-start | bytes 8388608
  1362.7 16.0 %slice-start.3 = ((s8[16777216]{0:T(1024)(128)(4,1)}), s8[4194304]{0:T(1024)(128)(4,1)S(1)}, s32[]{:S(2)}) async-start(s8[16777216]{0:T(1024)(128)(4,1)} %bitcast.307), calls=%async_computation.7 | async-start | bytes 8388608
  (55 other events, 212.9 us)
Sparse Core Ops, SparseCore 0:
  120.5 70.2 all-gather.1
  202.3 639.9 reduce-scatter.1
  990.0 358.1 all-reduce.4
where the time goes:
time: 1400 us; the launch traced here: 1390 us
  waiting for transfers between devices  867 us (62%)
  matrix products  300 us (21%)
  other arithmetic  86.8 us (6%)
  blocking collectives  71.7 us (5%)
  local copies, waits for them, and re-layouts  50.4 us (4%)
  between operations  17.1 us (1%)
    reduce_scatter x1, waiting for transfers between devices, local_step(): lax.psum_scatter(d_all_pass, batch_axis, scatter_dimension=0, tiled=True)  575 us
    psum x1, waiting for transfers between devices, local_step(): total_grads = lax.psum(local_grads, batch_axis)  256 us
    psum x1, blocking collectives, local_step(): mean_loss = lax.psum(jnp.sum(log_norm - positive), batch_axis) / n_total  71.7 us
    convert_element_type x2, other arithmetic, encoder_fwd(): ffn_act = jax.nn.gelu(pre_act, approximate=False).astype(jnp.bfloat16)  47.8 us
    unnamed x156, local copies, waits for them, and re-layouts  46.4 us
    all_gather x1, waiting for transfers between devices, local_step(): all_pass = lax.all_gather(p_embed, batch_axis, axis=0, tiled=True)  35.3 us
    dot_general x2, matrix products, encoder_bwd(): jnp.einsum('ntd,fd->ntf', d_resid2_lo, w_down, preferred_element_type=jnp...  29 us
    dot_general x2, matrix products, encoder_bwd(): jnp.einsum('ntf,ntd->fd', ffn_act, d_resid2_lo, preferred_element_type=jn...  28.3 us
  transfers between devices with their start and end apart: 3, of which 3 were waited for; matrix products, arithmetic and copies ran while one was open for 9% of the time, Pallas kernels for 0%

commit v1 on v0

v1 whole, which is shorter than its diff:
```python
import functools
import jax
import jax.numpy as jnp
from jax import lax
from jax.experimental import pallas as pl
from jax.experimental.pallas import tpu as pltpu
from jax.sharding import PartitionSpec as P

ZERO, ONE, ALL = 0, 1, ...

F32 = jnp.float32
BF16 = jnp.bfloat16
LOGICAL = pl.DeviceIdType.LOGICAL
RING = 4


def mesh_place(axis):
    me = lax.axis_index(axis)
    core = lax.rem(me, 2)
    chip = me // 2
    return (lax.rem(chip, RING), lax.rem(chip // RING, RING), chip // (RING * RING)), core


def device_at(coords, core):
    return ((coords[2] * RING + coords[ONE]) * RING + coords[ZERO]) * 2 + core


def moved(coords, dim, by):
    out = list(coords)
    out[dim] = lax.rem(coords[dim] + by + 2 * RING, RING)
    return tuple(out)


def wrap(i):
    return lax.rem(i + 4 * RING, RING)


def enter(peers):
    barrier = pltpu.get_barrier_semaphore()
    for peer in peers:
        pl.semaphore_signal(barrier, inc=ONE, device_id=peer, device_id_type=LOGICAL)
    pl.semaphore_wait(barrier, len(peers))


def sum_kernel(axis, piece, u0_ref, u1_ref, u2_ref, small_ref, o_ref, part_ref, small_out, acc, stage, land1, land2, land3,
               small_land, load_sem, swap_send, swap_recv, stage_sem, p1_send, p1_recv, p2_send, p2_recv,
               p3_send, p3_recv, a3_send, a3_recv, a2_send, a2_recv, a1_send, a1_recv, own_sem,
               push_send, push_recv, s_send, s_recv):
    u_refs = (u0_ref, u1_ref, u2_ref)
    sub, chunk, region = 4 * piece, 16 * piece, 64 * piece
    half = 6 * region
    coords, core = mesh_place(axis)
    partner = device_at(coords, ONE - core)
    base = core * half

    dims = [((k // 2) % 3, (k // 2 + ONE) % 3, (k // 2 + 2) % 3) for k in range(6)]
    sign = [ONE if k % 2 == ZERO else -ONE for k in range(6)]
    pos = [tuple(coords[d] for d in dims[k]) for k in range(6)]
    nxt = [tuple(device_at(moved(coords, d, sign[k]), core) for d in dims[k]) for k in range(6)]

    def rdma(src, dst, send, recv, to):
        pltpu.make_async_remote_copy(src_ref=src, dst_ref=dst, send_sem=send, recv_sem=recv,
                                     device_id=to, device_id_type=LOGICAL).start()

    def drain(ref, sem):
        pltpu.make_async_copy(ref, ref, sem).wait()

    def rows(at, n):
        return pl.ds(pl.multiple_of(at, 8), n)

    def c1(k, t):
        return wrap(pos[k][ZERO] - sign[k] * (ONE + t))

    def c2(k, i):
        return wrap(pos[k][ONE] - sign[k] * (ONE + i))

    def c3(k, i):
        return wrap(pos[k][2] - sign[k] * (ONE + i))

    def at2(k, j1, j2):
        return k * region + j1 * chunk + j2 * sub

    peers = [partner] + [device_at(moved(coords, d, by), core) for d in range(3) for by in (ONE, 2, 3)]
    enter(peers)

    def source(mine, k, r, n):
        return [u_refs[(c * 6 + k) // 4].at[rows((c * 6 + k) % 4 * region + r - k * region, n)] for c in ((ZERO, ONE) if mine else (ONE, ZERO))]

    def each_core(start):
        for c in range(2):
            pl.when(core == c)(functools.partial(start, c))

    def load(t):
        def start(c):
            for k in range(6):
                r = k * region + c1(k, t) * chunk
                pltpu.make_async_copy(source(True, k, r, chunk)[c], acc.at[rows(r, chunk)], load_sem.at[t]).start()
        each_core(start)

    def swap(n):
        t, i = divmod(n, 4)

        def start(c):
            for k in range(6):
                r = at2(k, c1(k, t), c2(k, i))
                rdma(source(False, k, r, sub)[c], part_ref.at[rows(r, sub)], swap_send.at[n], swap_recv.at[n], partner)
        each_core(start)

    def fetch(n):
        t, i = divmod(n, 4)
        drain(part_ref.at[pl.ds(ZERO, 6 * sub)], swap_recv.at[n])
        for k in range(6):
            r = at2(k, c1(k, t), c2(k, i))
            pltpu.make_async_copy(part_ref.at[rows(r, sub)], stage.at[n % 2, pl.ds(k * sub, sub)],
                                  stage_sem.at[n]).start()

    def add_rows(dst, terms, n):
        def step(r, _):
            at = pl.multiple_of(r * 8, 8)
            val = dst(at)[ALL]
            for term in terms:
                val = val + term(at)[ALL]
            dst(at)[ALL] = val
            return ZERO
        lax.fori_loop(ZERO, n // 8, step, ZERO, unroll=2)

    smalls = [(None, core, 2)] + [(d, coords[d], RING) for d in range(3)]

    def small_send(stage_no):
        d, place, size = smalls[stage_no]
        for by in range(ONE, size):
            to = partner if d is None else device_at(moved(coords, d, by), core)
            rdma(small_out, small_land.at[stage_no, by - ONE], s_send.at[stage_no], s_recv.at[stage_no], to)

    def small_add(stage_no):
        d, place, size = smalls[stage_no]
        drain(small_land.at[stage_no, pl.ds(ZERO, size - ONE)], s_recv.at[stage_no])
        drain(small_land.at[stage_no, pl.ds(ZERO, size - ONE)], s_send.at[stage_no])
        mine = small_out[ALL]
        total = None
        for p in range(size):
            val = mine
            for by in range(ONE, size):
                val = jnp.where(lax.rem(place - p + size, size) == by, small_land[stage_no, by - ONE], val)
            total = val if total is None else total + val
        small_out[ALL] = total

    small_out[ALL] = small_ref[ALL]
    for t in range(4):
        load(t)
    for n in range(4):
        swap(n)
    small_send(ZERO)
    fetch(ZERO)

    for n in range(16):
        t, i = divmod(n, 4)
        if n + 4 < 16:
            swap(n + 4)
        if n + ONE < 16:
            fetch(n + ONE)
        if i == ZERO:
            drain(acc.at[pl.ds(ZERO, 6 * chunk)], load_sem.at[t])
        drain(stage.at[n % 2], stage_sem.at[n])
        if t > ZERO:
            drain(land1.at[t - ONE, i], p1_recv.at[t - ONE, i])
        for k in range(6):
            r = at2(k, c1(k, t), c2(k, i))
            terms = [lambda at, k=k: stage.at[n % 2, pl.ds(k * sub + at, 8)]]
            if t > ZERO:
                terms.append(lambda at, k=k: land1.at[t - ONE, i, pl.ds(k * sub + at, 8)])
            add_rows(lambda at, r=r: acc.at[pl.ds(pl.multiple_of(r + at, 8), 8)], terms, sub)
        if t < 3:
            for k in range(6):
                r = at2(k, c1(k, t), c2(k, i))
                rdma(acc.at[rows(r, sub)], land1.at[t, i, pl.ds(k * sub, sub)], p1_send.at[t, i], p1_recv.at[t, i], nxt[k][ZERO])
        if n in (ONE, 3, 5, 7):
            small_add(n // 2)
            if n < 7:
                small_send(n // 2 + ONE)
        if t == 3:
            for g in range(4):
                if i > ZERO:
                    drain(land2.at[i - ONE, g], p2_recv.at[i - ONE, g])
                    for k in range(6):
                        r = at2(k, pos[k][ZERO], c2(k, i)) + c3(k, g) * piece
                        add_rows(lambda at, r=r: acc.at[pl.ds(pl.multiple_of(r + at, 8), 8)],
                                 [lambda at, k=k: land2.at[i - ONE, g, pl.ds(k * piece + at, 8)]], piece)
                if i < 3:
                    for k in range(6):
                        r = at2(k, pos[k][ZERO], c2(k, i)) + c3(k, g) * piece
                        rdma(acc.at[rows(r, piece)], land2.at[i, g, pl.ds(k * piece, piece)],
                             p2_send.at[i, g], p2_recv.at[i, g], nxt[k][ONE])
                else:
                    if g > ZERO:
                        drain(land3.at[g - ONE], p3_recv.at[g - ONE])
                        for k in range(6):
                            r = at2(k, pos[k][ZERO], pos[k][ONE]) + c3(k, g) * piece
                            add_rows(lambda at, r=r: acc.at[pl.ds(pl.multiple_of(r + at, 8), 8)],
                                     [lambda at, k=k: land3.at[g - ONE, pl.ds(k * piece + at, 8)]], piece)
                    if g < 3:
                        for k in range(6):
                            r = at2(k, pos[k][ZERO], pos[k][ONE]) + c3(k, g) * piece
                            rdma(acc.at[rows(r, piece)], land3.at[g, pl.ds(k * piece, piece)],
                                 p3_send.at[g], p3_recv.at[g], nxt[k][2])

    for k in range(6):
        r = at2(k, pos[k][ZERO], pos[k][ONE]) + pos[k][2] * piece
        pltpu.make_async_copy(acc.at[rows(r, piece)], o_ref.at[rows(base + r, piece)], own_sem.at[ZERO]).start()
        rdma(acc.at[rows(r, piece)], o_ref.at[rows(base + r, piece)], a3_send.at[ZERO], a3_recv.at[ZERO], nxt[k][2])
    for t in range(3):
        drain(acc.at[pl.ds(ZERO, 6 * piece)], a3_recv.at[t])
        if t < 2:
            for k in range(6):
                r = base + at2(k, pos[k][ZERO], pos[k][ONE]) + c3(k, t) * piece
                rdma(o_ref.at[rows(r, piece)], o_ref.at[rows(r, piece)], a3_send.at[t + ONE], a3_recv.at[t + ONE], nxt[k][2])
    drain(acc.at[pl.ds(ZERO, 6 * piece)], own_sem.at[ZERO])

    def spread(n, j1, j2):
        for k in range(6):
            r = base + at2(k, j1(k), j2(k))
            rdma(o_ref.at[rows(r, sub)], o_ref.at[rows(r, sub)], push_send.at[n], push_recv.at[n], partner)

    def hop2(t):
        for k in range(6):
            j2 = pos[k][ONE] if t == ZERO else c2(k, t - ONE)
            r = base + at2(k, pos[k][ZERO], j2)
            rdma(o_ref.at[rows(r, sub)], o_ref.at[rows(r, sub)], a2_send.at[t], a2_recv.at[t], nxt[k][ONE])

    def second(i):
        return lambda k: pos[k][ONE] if i == ZERO else c2(k, i - ONE)

    def first(t):
        return lambda k: pos[k][ZERO] if t == ZERO else c1(k, t - ONE)

    def hop1(t, i):
        for k in range(6):
            r = base + at2(k, first(t)(k), second(i)(k))
            rdma(o_ref.at[rows(r, sub)], o_ref.at[rows(r, sub)], a1_send.at[t, i], a1_recv.at[t, i], nxt[k][ZERO])

    for i in range(4):
        if i > ZERO:
            drain(acc.at[pl.ds(ZERO, 6 * sub)], a2_recv.at[i - ONE])
        if i < 3:
            hop2(i)
        hop1(ZERO, i)
        spread(i, first(ZERO), second(i))
    for t in range(3):
        for i in range(4):
            drain(acc.at[pl.ds(ZERO, 6 * sub)], a1_recv.at[t, i])
            if t < 2:
                hop1(t + ONE, i)
            spread(4 * (t + ONE) + i, first(t + ONE), second(i))

    for n in range(16):
        drain(acc.at[pl.ds(ZERO, 6 * sub)], swap_send.at[n])
    for t in range(3):
        for i in range(4):
            drain(acc.at[pl.ds(ZERO, 6 * sub)], p1_send.at[t, i])
            drain(acc.at[pl.ds(ZERO, 6 * piece)], p2_send.at[t, i])
            drain(acc.at[pl.ds(ZERO, 6 * sub)], a1_send.at[t, i])
        drain(acc.at[pl.ds(ZERO, 6 * piece)], p3_send.at[t])
        drain(acc.at[pl.ds(ZERO, 6 * piece)], a3_send.at[t])
        drain(acc.at[pl.ds(ZERO, 6 * sub)], a2_send.at[t])
    for n in range(16):
        drain(acc.at[pl.ds(ZERO, 6 * sub)], push_send.at[n])
        drain(acc.at[pl.ds(ZERO, 6 * sub)], push_recv.at[n])


def sum_over_devices(parts, small, axis, collective_id=ONE):
    width = parts[ZERO].shape[ONE]
    total = sum(p.shape[ZERO] for p in parts)
    piece = total // 768
    dma = pltpu.SemaphoreType.DMA
    sub = 4 * piece
    outs = pl.pallas_call(
        functools.partial(sum_kernel, axis, piece),
        out_shape=(jax.ShapeDtypeStruct((total, width), F32), jax.ShapeDtypeStruct((total // 2, width), F32),
                   jax.ShapeDtypeStruct(small.shape, F32)),
        in_specs=[pl.BlockSpec(memory_space=pl.ANY)] * 3 + [pl.BlockSpec(memory_space=pltpu.VMEM)],
        out_specs=(pl.BlockSpec(memory_space=pl.ANY), pl.BlockSpec(memory_space=pl.ANY),
                   pl.BlockSpec(memory_space=pltpu.VMEM)),
        scratch_shapes=[
            pltpu.VMEM((total // 2, width), F32),
            pltpu.VMEM((2, 6 * sub, width), F32),
            pltpu.VMEM((3, 4, 6 * sub, width), F32),
            pltpu.VMEM((3, 4, 6 * piece, width), F32),
            pltpu.VMEM((3, 6 * piece, width), F32),
            pltpu.VMEM((4, 3) + small.shape, F32),
            dma((4,)), dma((16,)), dma((16,)), dma((16,)),
            dma((3, 4)), dma((3, 4)), dma((3, 4)), dma((3, 4)), dma((3,)), dma((3,)),
            dma((3,)), dma((3,)), dma((3,)), dma((3,)), dma((3, 4)), dma((3, 4)), dma((ONE,)),
            dma((16,)), dma((16,)), dma((4,)), dma((4,)),
        ],
        compiler_params=pltpu.CompilerParams(collective_id=collective_id, has_side_effects=True,
                                             vmem_limit_bytes=64 * 1024 * 1024),
        name="sum_over_devices",
    )(*parts, small)
    return outs[ZERO], outs[2]


def gather_kernel(axis, e_ref, g_ref, mine, theirs, swap_sem, sems_send, sems_recv, push_send, push_recv):
    coords, core = mesh_place(axis)
    partner = device_at(coords, ONE - core)
    width = e_ref.shape[ONE]
    lanes = pl.ds(pl.multiple_of(core * (width // 2), 128), width // 2)
    x, y, z = coords
    peers = [partner] + [device_at(moved(coords, d, by), core) for d in range(3) for by in (ONE, 2, 3)]
    enter(peers)

    def rdma(src, dst, send, recv, to):
        pltpu.make_async_remote_copy(src_ref=src, dst_ref=dst, send_sem=send, recv_sem=recv,
                                     device_id=to, device_id_type=LOGICAL).start()

    def drain(ref, sem):
        pltpu.make_async_copy(ref, ref, sem).wait()

    rdma(e_ref, theirs, swap_sem.at[ZERO], swap_sem.at[ONE], partner)
    mine[ALL] = e_ref[ALL]
    drain(theirs, swap_sem.at[ONE])
    first = jnp.where(core == ZERO, mine[:, lanes], theirs[:, lanes])
    second = jnp.where(core == ZERO, theirs[:, lanes], mine[:, lanes])
    g_ref[z, y, x, ZERO:4, lanes] = first[ZERO:4]
    g_ref[z, y, x, 4:8, lanes] = second[ZERO:4]
    g_ref[z, y, x, 8:16, lanes] = first[8:16]
    g_ref[z, y, x, 16:24, lanes] = second[8:16]
    drain(e_ref, swap_sem.at[ZERO])

    def view(a, stage):
        idx = [z, y, x]
        for s in range(stage):
            idx[2 - (a + s) % 3] = slice(None)
        return g_ref.at[idx[ZERO], idx[ONE], idx[2], pl.ds(8 * a, 8), lanes]

    for stage in range(3):
        for by in (ONE, 3, 2):
            for a in range(3):
                to = device_at(moved(coords, (a + stage) % 3, by), core)
                rdma(view(a, stage), view(a, stage), sems_send.at[stage, by - ONE], sems_recv.at[stage, by - ONE], to)
        if stage == 2:
            for a in range(3):
                rdma(view(a, 2), view(a, 2), push_send.at[ZERO], push_recv.at[ZERO], partner)
        for by in (ONE, 3, 2):
            n = 4 ** stage
            shape_like = g_ref.at[ZERO, ZERO, ZERO, :, lanes] if stage == ZERO else (
                g_ref.at[ZERO, ZERO, :, :, lanes] if stage == ONE else g_ref.at[ZERO, :, :, :, lanes])
            drain(shape_like, sems_recv.at[stage, by - ONE])
            if stage == 2:
                for a in range(3):
                    far = moved(coords, (a + 2) % 3, RING - by)
                    idx = [far[2], far[ONE], far[ZERO]]
                    idx[2 - a] = slice(None)
                    idx[2 - (a + ONE) % 3] = slice(None)
                    v = g_ref.at[idx[ZERO], idx[ONE], idx[2], pl.ds(8 * a, 8), lanes]
                    rdma(v, v, push_send.at[by], push_recv.at[by], partner)
    for stage in range(3):
        shape_like = g_ref.at[ZERO, ZERO, ZERO, :, lanes] if stage == ZERO else (
            g_ref.at[ZERO, ZERO, :, :, lanes] if stage == ONE else g_ref.at[ZERO, :, :, :, lanes])
        for by in (ONE, 2, 3):
            drain(shape_like, sems_send.at[stage, by - ONE])
    for by in range(4):
        drain(g_ref.at[ZERO, :, :, :, lanes], push_send.at[by])
        drain(g_ref.at[ZERO, :, :, :, lanes], push_recv.at[by])


def gather_embeddings(e, axis, collective_id=2):
    dma = pltpu.SemaphoreType.DMA
    width = e.shape[ONE]
    g = pl.pallas_call(
        functools.partial(gather_kernel, axis),
        out_shape=jax.ShapeDtypeStruct((RING, RING, RING, 24, width), F32),
        in_specs=[pl.BlockSpec(memory_space=pltpu.VMEM)],
        out_specs=pl.BlockSpec(memory_space=pltpu.VMEM),
        scratch_shapes=[pltpu.VMEM(e.shape, F32), pltpu.VMEM(e.shape, F32), dma((2,)),
                        dma((3, 3)), dma((3, 3)), dma((4,)), dma((4,))],
        compiler_params=pltpu.CompilerParams(collective_id=collective_id, has_side_effects=True,
                                             vmem_limit_bytes=16 * 1024 * 1024),
        name="gather_embeddings",
    )(e)
    return g.reshape(RING ** 3, 24, width)


def loss_kernel(axis, n_query, g_ref, pooled_ref, loss_ref, d_ref, logit_ref, lse_ref):
    me = lax.axis_index(axis)
    core, chip = lax.rem(me, 2), me // 2
    width = pooled_ref.shape[ONE]
    chips = g_ref.shape[ZERO]
    gs = 100.0 / n_query
    hi = lax.Precision.HIGHEST
    nt = (((ONE,), (ONE,)), ((), ()))
    pall = g_ref[:, 8:24, :].reshape(chips * 16, width)
    block = 128
    per = block // 8

    def chunk(b, loss):
        qb = g_ref[pl.ds(b * per, per), ZERO:8, :].reshape(block, width)
        s = lax.dot_general(qb, pall, nt, precision=hi, preferred_element_type=F32) * 100.0
        logit_ref[pl.ds(pl.multiple_of(b * block, block), block), :] = s
        top = jnp.max(s, axis=ONE, keepdims=True)
        lse = jnp.log(jnp.sum(jnp.exp(s - top), axis=ONE, keepdims=True)) + top
        lse_ref[pl.ds(pl.multiple_of(b * block, block), block), :] = jnp.broadcast_to(lse, (block, 128))
        row = lax.broadcasted_iota(jnp.int32, s.shape, ZERO) + b * block
        col = lax.broadcasted_iota(jnp.int32, s.shape, ONE)
        pos = jnp.sum(jnp.where(col == 2 * row, s, 0.0), axis=ONE, keepdims=True)
        return loss + jnp.sum(lse - pos, axis=ZERO, keepdims=True)

    loss = lax.fori_loop(ZERO, chips // per, chunk, jnp.zeros((ONE, ONE), F32))
    loss_ref[ALL] = jnp.broadcast_to(loss * (1.0 / n_query), loss_ref.shape)

    at = pl.multiple_of(chip * 8, 8)
    s8 = logit_ref[pl.ds(at, 8), :]
    l8 = lse_ref[pl.ds(at, 8), ZERO:ONE]
    row = lax.broadcasted_iota(jnp.int32, s8.shape, ZERO) + chip * 8
    col = lax.broadcasted_iota(jnp.int32, s8.shape, ONE)
    w8 = jnp.exp(s8 - l8) * gs - jnp.where(col == 2 * row, gs, 0.0)
    dq8 = lax.dot_general(w8, pall, (((ONE,), (ZERO,)), ((), ())), precision=hi, preferred_element_type=F32)

    qall = g_ref[:, ZERO:8, :].reshape(chips * 8, width)
    p16 = g_ref[chip, 8:24, :]
    s16 = lax.dot_general(qall, p16, nt, precision=hi, preferred_element_type=F32) * 100.0
    row = lax.broadcasted_iota(jnp.int32, s16.shape, ZERO)
    col = lax.broadcasted_iota(jnp.int32, s16.shape, ONE) + chip * 16
    w16 = jnp.exp(s16 - lse_ref[:, ZERO:ONE]) * gs - jnp.where(col == 2 * row, gs, 0.0)
    dp16 = lax.dot_general(w16, qall, (((ZERO,), (ZERO,)), ((), ())), precision=hi, preferred_element_type=F32)

    dq = jnp.where(core == ZERO, dq8[ZERO:4], dq8[4:8])
    dp = jnp.where(core == ZERO, dp16[ZERO:8], dp16[8:16])
    pooled_q, pooled_p = pooled_ref[ZERO:4], pooled_ref[8:16]

    def back(d, pooled):
        inv = lax.rsqrt(jnp.sum(pooled * pooled, axis=ONE, keepdims=True))
        e = pooled * inv
        return (d - e * jnp.sum(e * d, axis=ONE, keepdims=True)) * inv

    d_ref[ALL] = jnp.zeros_like(d_ref)
    d_ref[ZERO:4, :] = back(dq, pooled_q)
    d_ref[8:16, :] = back(dp, pooled_p)


def loss_and_grad(g, pooled, axis, n_query):
    chips, _, width = g.shape
    loss, d = pl.pallas_call(
        functools.partial(loss_kernel, axis, n_query),
        out_shape=(jax.ShapeDtypeStruct((8, 128), F32), jax.ShapeDtypeStruct(pooled.shape, F32)),
        in_specs=[pl.BlockSpec(memory_space=pltpu.VMEM)] * 2,
        out_specs=(pl.BlockSpec(memory_space=pltpu.VMEM),) * 2,
        scratch_shapes=[pltpu.VMEM((chips * 8, chips * 16), F32), pltpu.VMEM((chips * 8, 128), F32)],
        compiler_params=pltpu.CompilerParams(vmem_limit_bytes=48 * 1024 * 1024),
        name="loss_and_grad",
    )(g, pooled)
    return loss[ZERO, ZERO], d


NN = (((ONE,), (ZERO,)), ((), ()))
NT = (((ONE,), (ONE,)), ((), ()))
TN = (((ZERO,), (ZERO,)), ((), ()))
LN_EPS = 1e-12
NEG_FILL = -1e9
TILE = 512


def mm(a, b, dims=NN):
    return lax.dot_general(a, b, dims, preferred_element_type=F32)


def vmem(mb=60):
    return pltpu.CompilerParams(vmem_limit_bytes=mb * 1024 * 1024)


def whole(shape):
    return pl.BlockSpec(shape, lambda j: (ZERO,) * len(shape), pipeline_mode=pl.Buffered(ONE))


def across(rows, tile):
    return pl.BlockSpec((rows, tile), lambda j: (ZERO, j))


def down(tile, cols):
    return pl.BlockSpec((tile, cols), lambda j: (j, ZERO))


def qkv_kernel(x_ref, w_ref, b_ref, oq_ref, op_ref):
    y = (mm(x_ref[ALL], w_ref[ALL], NT) + b_ref[ALL]).astype(BF16)
    tq = oq_ref.shape[ZERO]
    oq_ref[ALL] = y[:tq]
    op_ref[ALL] = y[tq:]


def qkv_project(x, w_t, b, tq, tile=TILE):
    t, d = x.shape
    tp = t - tq
    f = w_t.shape[ZERO]
    return pl.pallas_call(
        qkv_kernel, grid=(f // tile,),
        out_shape=(jax.ShapeDtypeStruct((tq, f), BF16), jax.ShapeDtypeStruct((tp, f), BF16)),
        in_specs=[whole((t, d)), down(tile, d), across(ONE, tile)],
        out_specs=(across(tq, tile), across(tp, tile)),
        compiler_params=vmem(), name="qkv_project",
    )(x, w_t, b)


def split_heads(pair, head):
    lane = lax.broadcasted_iota(jnp.int32, pair.shape, ONE)
    zero = jnp.zeros_like(pair)
    return jnp.concatenate([jnp.where(lane < head, pair, zero), jnp.where(lane >= head, pair, zero)], axis=ZERO)


def join_heads(stacked, head):
    t = stacked.shape[ZERO] // 2
    lane = lax.broadcasted_iota(jnp.int32, (t, stacked.shape[ONE]), ONE)
    return jnp.where(lane < head, stacked[:t], stacked[t:])


def attn_kernel(scale, head, qkv_ref, mask_ref, probs_ref, ctx_ref):
    d = ctx_ref.shape[ONE]
    pair = 2 * head
    keep = mask_ref[ZERO] > ZERO
    for g in range(d // pair):
        at = pl.ds(g * pair, pair)
        q = split_heads(qkv_ref[:, at], head)
        k = qkv_ref[:, pl.ds(d + g * pair, pair)]
        v = qkv_ref[:, pl.ds(2 * d + g * pair, pair)]
        s = jnp.where(keep, mm(q, k, NT) * scale, NEG_FILL)
        e = jnp.exp(s - jnp.max(s, axis=ONE, keepdims=True))
        p = (e / jnp.sum(e, axis=ONE, keepdims=True)).astype(BF16)
        probs_ref[ZERO, g] = p
        ctx_ref[:, at] = join_heads(mm(p, v), head).astype(BF16)


def attention(qkv, mask, seq, head):
    n = mask.shape[ZERO]
    d = qkv.shape[ONE] // 3
    pairs = d // (2 * head)
    return pl.pallas_call(
        functools.partial(attn_kernel, head ** -0.5, head), grid=(n,),
        out_shape=(jax.ShapeDtypeStruct((n, pairs, 2 * seq, seq), BF16), jax.ShapeDtypeStruct((n * seq, d), BF16)),
        in_specs=[down(seq, 3 * d), pl.BlockSpec((ONE, ONE, seq), lambda j: (j, ZERO, ZERO))],
        out_specs=(pl.BlockSpec((ONE, pairs, 2 * seq, seq), lambda j: (j, ZERO, ZERO, ZERO)), down(seq, d)),
        compiler_params=vmem(), name="attention",
    )(qkv, mask.reshape(n, ONE, seq))


def attn_bwd_kernel(scale, head, qkv_ref, probs_ref, dc_ref, d_ref):
    d = dc_ref.shape[ONE]
    pair = 2 * head
    for g in range(d // pair):
        at = pl.ds(g * pair, pair)
        q = split_heads(qkv_ref[:, at], head)
        k = qkv_ref[:, pl.ds(d + g * pair, pair)]
        v = qkv_ref[:, pl.ds(2 * d + g * pair, pair)]
        p = probs_ref[ZERO, g]
        dc = split_heads(dc_ref[:, at], head)
        dp = mm(dc, v, NT)
        pf = p.astype(F32)
        ds = (pf * (dp - jnp.sum(dp * pf, axis=ONE, keepdims=True)) * scale).astype(BF16)
        d_ref[:, at] = join_heads(mm(ds, k), head).astype(BF16)
        d_ref[:, pl.ds(d + g * pair, pair)] = mm(ds, q, TN).astype(BF16)
        d_ref[:, pl.ds(2 * d + g * pair, pair)] = mm(p, dc, TN).astype(BF16)


def attention_bwd(qkv, probs, d_ctx, seq, head):
    n, pairs = probs.shape[:2]
    d = d_ctx.shape[ONE]
    return pl.pallas_call(
        functools.partial(attn_bwd_kernel, head ** -0.5, head), grid=(n,),
        out_shape=jax.ShapeDtypeStruct((n * seq, 3 * d), BF16),
        in_specs=[down(seq, 3 * d),
                  pl.BlockSpec((ONE, pairs, 2 * seq, seq), lambda j: (j, ZERO, ZERO, ZERO)),
                  down(seq, d)],
        out_specs=down(seq, 3 * d),
        compiler_params=vmem(), name="attention_bwd",
    )(qkv, probs, d_ctx)


def norm_rows(x):
    c = x - jnp.mean(x, axis=ONE, keepdims=True)
    r = lax.rsqrt(jnp.mean(c * c, axis=ONE, keepdims=True) + LN_EPS)
    return c * r, r


def norm_back(g, hat, r):
    return r * (g - jnp.mean(g, axis=ONE, keepdims=True) - hat * jnp.mean(g * hat, axis=ONE, keepdims=True))


ERFC = (0.07122347, -0.27794802, 0.29668747, -0.02018065, 0.21581222, 0.21731356, 0.24887118, 0.24822095)


def gelu_parts(u):
    bell = jnp.exp(-0.5 * u * u)
    t = 1.0 / (1.0 + 0.311126984 * jnp.abs(u))
    poly = ERFC[ZERO]
    for c in ERFC[ONE:]:
        poly = poly * t + c
    tail = 0.5 * bell * (poly * t)
    return jnp.where(u >= 0.0, 1.0 - tail, tail), u * bell * 0.3989422804


ROWS = 304


def ffn_kernel(bounds, x_ref, cq_ref, cp_ref, wo_ref, vec_ref, wt_ref, wu_ref, bu_ref, wd_ref,
               h_ref, r1_ref, g_ref, gp_ref, r2_ref, pool_ref):
    j = pl.program_id(ZERO)
    t = x_ref.shape[ZERO]
    tq = cq_ref.shape[ZERO]
    b_out, g1, s1, b_down, g2, s2 = (vec_ref[i:i + ONE, :] for i in range(6))

    @pl.when(j == ZERO)
    def _():
        for ref, lo in ((cq_ref, ZERO), (cp_ref, tq)):
            n = ref.shape[ZERO]
            size = n if n < 256 else 256
            for a in range(ZERO, n, size):
                at = pl.ds(lo + a, size)
                r1 = x_ref[at, :].astype(F32) + mm(ref[pl.ds(a, size), :], wo_ref[ALL]) + b_out
                r1_ref[at, :] = r1
                h = (norm_rows(r1)[ZERO] * g1 + s1).astype(BF16)
                h_ref[at, :] = h
                r2_ref[at, :] = h.astype(F32) + b_down

    for a in range(ZERO, t, ROWS):
        at = pl.ds(a, ROWS)
        u = mm(h_ref[at, :], wu_ref[ALL]) + bu_ref[ALL]
        cdf, upd = gelu_parts(u)
        g = (u * cdf).astype(BF16)
        g_ref[at, :] = g
        gp_ref[at, :] = cdf + upd
        r2_ref[at, :] += mm(g, wd_ref[ALL])

    @pl.when(j == pl.num_programs(ZERO) - ONE)
    def _():
        pool_ref[ALL] = jnp.zeros_like(pool_ref)
        for row, lo, n in bounds:
            at = pl.ds(lo, n)
            y = norm_rows(r2_ref[at, :])[ZERO] * g2 + s2
            pool_ref[row:row + ONE, :] = jnp.sum(y * wt_ref[at, :], axis=ZERO, keepdims=True)


def ffn_forward(x, ctx_q, ctx_p, w_out, vecs, weights, w_up, b_up, w_down, bounds, tile=TILE):
    t, d = x.shape
    f = w_up.shape[ONE]
    sds = jax.ShapeDtypeStruct
    return pl.pallas_call(
        functools.partial(ffn_kernel, bounds), grid=(f // tile,),
        out_shape=(sds((t, d), BF16), sds((t, d), F32), sds((t, f), BF16), sds((t, f), F32), sds((t, d), F32), sds((16, d), F32)),
        in_specs=[whole((t, d)), whole(ctx_q.shape), whole(ctx_p.shape), whole((d, d)), whole(vecs.shape), whole((t, ONE)),
                  across(d, tile), across(ONE, tile),
                  down(tile, d)],
        out_specs=(whole((t, d)), whole((t, d)), across(t, tile),
                   across(t, tile), whole((t, d)), whole((16, d))),
        compiler_params=vmem(), name="ffn_forward",
    )(x, ctx_q, ctx_p, w_out, vecs, weights, w_up, b_up, w_down)


def ffn_bwd_kernel(bounds, dpool_ref, r2_ref, wt_ref, vec_ref, h_ref, g_ref, gp_ref, wd_ref, wu_ref, r1_ref, wo_ref,
                   dwd_ref, dwu_ref, dbu_ref, dr1_ref, dr1b_ref, dcq_ref, dcp_ref, dvec_ref, dr2_ref, ht_ref):
    j = pl.program_id(ZERO)
    t = h_ref.shape[ZERO]
    b_out, g1, s1, b_down, g2, s2 = (vec_ref[i:i + ONE, :] for i in range(6))

    @pl.when(j == ZERO)
    def _():
        dvec_ref[ALL] = jnp.zeros_like(dvec_ref)
        for row, lo, n in bounds:
            at = pl.ds(lo, n)
            hat, r = norm_rows(r2_ref[at, :])
            dy = wt_ref[at, :] * dpool_ref[row:row + ONE, :]
            dr2 = norm_back(dy * g2, hat, r)
            dr1_ref[at, :] = dr2
            dr2_ref[at, :] = dr2.astype(BF16)
            dvec_ref[3:4, :] += jnp.sum(dr2, axis=ZERO, keepdims=True)
            dvec_ref[4:5, :] += jnp.sum(dy * hat, axis=ZERO, keepdims=True)
            dvec_ref[5:6, :] += jnp.sum(dy, axis=ZERO, keepdims=True)
        ht_ref[ALL] = h_ref[ALL].T

    dg = mm(dr2_ref[ALL], wd_ref[ALL], NT).astype(BF16).astype(F32)
    dpre = dg * gp_ref[ALL]
    dbu_ref[ALL] = jnp.sum(dpre, axis=ZERO, keepdims=True)
    dpre = dpre.astype(BF16)
    dwu_ref[ZERO] = mm(ht_ref[ALL], dpre)
    dr1_ref[ALL] += mm(dpre, wu_ref[ALL], NT)
    dwd_ref[ALL] = mm(g_ref[ALL], dr2_ref[ALL], TN)

    @pl.when(j == pl.num_programs(ZERO) - ONE)
    def _():
        for a in range(ZERO, t, ROWS):
            at = pl.ds(a, ROWS)
            dy = dr1_ref[at, :].astype(BF16).astype(F32)
            hat, r = norm_rows(r1_ref[at, :])
            dr1 = norm_back(dy * g1, hat, r)
            dr1_ref[at, :] = dr1
            lo = dr1.astype(BF16)
            dr1b_ref[at, :] = lo
            dvec_ref[ZERO:ONE, :] += jnp.sum(dr1, axis=ZERO, keepdims=True)
            dvec_ref[ONE:2, :] += jnp.sum(dy * hat, axis=ZERO, keepdims=True)
            dvec_ref[2:3, :] += jnp.sum(dy, axis=ZERO, keepdims=True)
        tq = dcq_ref.shape[ZERO]
        dcq_ref[ALL] = mm(dr1b_ref[:tq, :], wo_ref[ALL], NT).astype(BF16)
        dcp_ref[ALL] = mm(dr1b_ref[tq:, :], wo_ref[ALL], NT).astype(BF16)


def ffn_backward(dpool, r2, weights, vecs, h, g, gp, w_down, w_up, r1, w_out, bounds, tq, tile=TILE):
    t, d = h.shape
    tp = t - tq
    f = w_up.shape[ONE]
    sds = jax.ShapeDtypeStruct
    per = d // tile
    return pl.pallas_call(
        functools.partial(ffn_bwd_kernel, bounds), grid=(f // tile,),
        out_shape=(sds((f, d), F32), sds((f // d, d, d), F32), sds((ONE, f), F32), sds((t, d), F32), sds((t, d), BF16),
                   sds((tq, d), BF16), sds((tp, d), BF16), sds((8, d), F32)),
        in_specs=[whole(dpool.shape), whole((t, d)), whole((t, ONE)), whole(vecs.shape), whole((t, d)),
                  across(t, tile), across(t, tile),
                  down(tile, d), across(d, tile),
                  whole((t, d)), whole((d, d))],
        out_specs=(down(tile, d), pl.BlockSpec((ONE, d, tile), lambda j: (lax.div(j, per), ZERO, lax.rem(j, per))),
                   across(ONE, tile), whole((t, d)), whole((t, d)), whole((tq, d)), whole((tp, d)), whole((8, d))),
        scratch_shapes=[pltpu.VMEM((t, d), BF16), pltpu.VMEM((d, t), BF16)],
        compiler_params=vmem(63), name="ffn_backward",
    )(dpool, r2, weights, vecs, h, g, gp, w_down, w_up, r1, w_out)


def qkv_bwd_kernel(steps, dq_ref, dp_ref, x_ref, w_ref, dr1_ref, cq_ref, cp_ref, dr1b_ref, dw_ref, db_ref, dh_ref, acc_ref):
    j = pl.program_id(ZERO)
    tq = dq_ref.shape[ZERO]

    @pl.when(j < steps)
    def _():
        dp = jnp.concatenate([dq_ref[ALL], dp_ref[ALL]], axis=ZERO)
        part = mm(dp, w_ref[ALL])

        @pl.when(j == ZERO)
        def _():
            acc_ref[ALL] = dr1_ref[ALL] + part

        @pl.when(j > ZERO)
        def _():
            acc_ref[ALL] += part
        dw_ref[ALL] = mm(dp, x_ref[ALL], TN)
        db_ref[ALL] = jnp.sum(dp.astype(F32), axis=ZERO, keepdims=True)

    @pl.when(j == steps - ONE)
    def _():
        dh_ref[ALL] = acc_ref[ALL].astype(BF16)

    @pl.when(j >= steps)
    def _():
        ctx = jnp.concatenate([cq_ref[ALL], cp_ref[ALL]], axis=ZERO)
        dw_ref[ALL] = mm(ctx, dr1b_ref[ALL], TN)


def qkv_backward(dq, dp, x, w_t, dr1, ctx_q, ctx_p, dr1b, tile=TILE):
    t, d = x.shape
    f = w_t.shape[ZERO]
    tq, tp = dq.shape[ZERO], dp.shape[ZERO]
    n, m = f // tile, d // tile
    sds = jax.ShapeDtypeStruct
    cut = lambda j: jnp.minimum(j, n - ONE)
    late = lambda j: jnp.maximum(j - n, ZERO)
    return pl.pallas_call(
        functools.partial(qkv_bwd_kernel, n), grid=(n + m,),
        out_shape=(sds((f + d, d), F32), sds((ONE, f), F32), sds((t, d), BF16)),
        in_specs=[pl.BlockSpec((tq, tile), lambda j: (ZERO, cut(j))), pl.BlockSpec((tp, tile), lambda j: (ZERO, cut(j))),
                  whole((t, d)), pl.BlockSpec((tile, d), lambda j: (cut(j), ZERO)), whole((t, d)),
                  pl.BlockSpec((tq, tile), lambda j: (ZERO, late(j))), pl.BlockSpec((tp, tile), lambda j: (ZERO, late(j))), whole((t, d))],
        out_specs=(down(tile, d), pl.BlockSpec((ONE, tile), lambda j: (ZERO, cut(j))), whole((t, d))),
        scratch_shapes=[pltpu.VMEM((t, d), F32)],
        compiler_params=vmem(), name="qkv_backward",
    )(dq, dp, x, w_t, dr1, ctx_q, ctx_p, dr1b)


def unpack_kernel(n1, n2, n3, s_ref, a_ref, b_ref, c_ref, d_ref):
    j = pl.program_id(ZERO)
    for ref, lo, hi in ((a_ref, ZERO, n1), (b_ref, n1, n2), (c_ref, n2, n3), (d_ref, n3, pl.num_programs(ZERO))):
        @pl.when((j >= lo) & (j < hi))
        def _():
            ref[ALL] = s_ref[ALL]


def unpack(total, sizes, d, tile=TILE):
    per = d // tile
    n1, n2, n3, n4 = (sum(sizes[:i + ONE]) // tile for i in range(len(sizes)))
    part = lambda lo, hi: (lambda j: (jnp.clip(j - lo, ZERO, hi - lo - ONE), ZERO))
    up = lambda j: (lax.rem(jnp.clip(j - n2, ZERO, n3 - n2 - ONE), per), lax.div(jnp.clip(j - n2, ZERO, n3 - n2 - ONE), per))
    rows = [jax.ShapeDtypeStruct((n, d), F32) for n in sizes]
    rows[2] = jax.ShapeDtypeStruct((d, sizes[2]), F32)
    maps = (part(ZERO, n1), part(n1, n2), up, part(n3, n4))
    return pl.pallas_call(
        functools.partial(unpack_kernel, n1, n2, n3), grid=(n4,), out_shape=rows,
        in_specs=[down(tile, d)], out_specs=[pl.BlockSpec((tile, d), m) for m in maps],
        compiler_params=vmem(), name="unpack",
    )(total)


def solution(mesh):
    axis = mesh.axis_names[ZERO]
    n_dev = mesh.shape[axis]

    def local_step(q_hidden, q_mask, p_hidden, p_mask, w_qkv, b_qkv, w_out, b_out, ln1_gain, ln1_shift,
                   w_up, b_up, w_down, b_down, ln2_gain, ln2_shift):
        nq, q_len, d = q_hidden.shape
        n_pass, p_len = nq * p_hidden.shape[ONE], p_hidden.shape[2]
        _, three, heads, head = w_qkv.shape
        ff = w_up.shape[ONE]
        tq = nq * q_len
        x = jnp.concatenate([q_hidden.reshape(-ONE, d), p_hidden.reshape(-ONE, d)], axis=ZERO)
        p_mask = p_mask.reshape(n_pass, p_len)
        wqkv_t = w_qkv.transpose(ONE, 2, 3, ZERO).reshape(-ONE, d)
        wo = w_out.reshape(-ONE, d)
        none = jnp.zeros_like(b_out)
        vecs = jnp.stack([b_out, ln1_gain, ln1_shift, b_down, ln2_gain, ln2_shift, none, none])

        def pool_weights(mask):
            m = mask.astype(F32)
            return (m / jnp.sum(m, axis=ONE, keepdims=True)).reshape(-ONE, ONE)

        weights = jnp.concatenate([pool_weights(q_mask), pool_weights(p_mask)], axis=ZERO)
        bounds = tuple((i, i * q_len, q_len) for i in range(nq)) + tuple(
            (2 * nq + i, tq + i * p_len, p_len) for i in range(n_pass))

        qkv_q, qkv_p = qkv_project(x, wqkv_t, b_qkv.reshape(ONE, -ONE), tq)
        probs_q, ctx_q = attention(qkv_q, q_mask, q_len, head)
        probs_p, ctx_p = attention(qkv_p, p_mask, p_len, head)
        h, r1, g, gp, r2, pooled = ffn_forward(x, ctx_q, ctx_p, wo, vecs, weights, w_up, b_up.reshape(ONE, -ONE), w_down, bounds)

        used = (jnp.arange(pooled.shape[ZERO]) < nq) | (jnp.arange(pooled.shape[ZERO]) >= 2 * nq)
        size = jnp.sum(pooled * pooled, axis=ONE, keepdims=True)
        embed = pooled * jnp.where(used[:, None], lax.rsqrt(size), 0.0)
        everyone = gather_embeddings(embed, axis)
        mean_loss, d_pooled = loss_and_grad(everyone, pooled, axis, nq * n_dev)

        dwd, dwu, dbu, dr1, dr1b, dc_q, dc_p, dvec = ffn_backward(
            d_pooled, r2, weights, vecs, h, g, gp, w_down, w_up, r1, wo, bounds, tq)
        dq = attention_bwd(qkv_q, probs_q, dc_q, q_len, head)
        dp = attention_bwd(qkv_p, probs_p, dc_p, p_len, head)
        dwa, dbq, dh = qkv_backward(dq, dp, x, wqkv_t, dr1, ctx_q, ctx_p, dr1b)

        small = jnp.concatenate([dvec, dbq.reshape(three, d), dbu.reshape(-ONE, d), jnp.zeros((ONE, d), F32)], axis=ZERO)
        total, small = sum_over_devices((dwa, dwu.reshape(-ONE, d), dwd), small, axis)
        d_qkv, d_out, d_up, d_down = unpack(total, (three * d, d, ff, ff), d)
        vec = [small[i] for i in range(6)]
        return (mean_loss, dh[:tq].reshape(q_hidden.shape), dh[tq:].reshape(p_hidden.shape),
                d_qkv.reshape(three, heads, head, d).transpose(3, ZERO, ONE, 2), small[8:8 + three].reshape(b_qkv.shape),
                d_out.reshape(w_out.shape), vec[ZERO], vec[ONE], vec[2], d_up, small[8 + three:-ONE].reshape(-ONE),
                d_down, vec[3], vec[4], vec[5])

    in_specs = (P(axis),) * 4 + (P(),) * 12
    out_specs = (P(), P(axis), P(axis)) + (P(),) * 12
    return jax.shard_map(local_step, mesh=mesh, in_specs=in_specs, out_specs=out_specs, check_vma=False)
```

time: 1400 us -> 572 us (0.41)
  waiting for transfers between devices: 867 us -> 0 us
  Pallas kernels: 0 us -> 541 us
  matrix products: 300 us -> 0 us
  other arithmetic: 86.8 us -> 11.1 us
  blocking collectives: 71.7 us -> 0 us
  local copies, waits for them, and re-layouts: 50.4 us -> 15.4 us
  between operations: 17.1 us -> 1.03 us
    reduce_scatter x1 -> x0, waiting for transfers between devices: 575 us -> none  [local_step(): lax.psum_scatter(d_all_pass, batch_axis, scatter_dimension=0, tiled=True)]
    pallas_call x0 -> x12, Pallas kernels: none -> 541 us  [the longest x1 211 us: sum_over_devices(): pl.pallas_call(functools.partial(sum_kernel, axis, piece), out_shape=(jax...]
    dot_general x40 -> x0, matrix products: 297 us -> none  [the longest x2 29 us: encoder_bwd(): jnp.einsum('ntd,fd->ntf', d_resid2_lo, w_down, preferred_element_type=jnp...]
    psum x1 -> x0, waiting for transfers between devices: 256 us -> none  [local_step(): total_grads = lax.psum(local_grads, batch_axis)]
    psum x1 -> x0, blocking collectives: 71.7 us -> none  [local_step(): mean_loss = lax.psum(jnp.sum(log_norm - positive), batch_axis) / n_total]
    convert_element_type x7 -> x1, other arithmetic: 52.5 us -> 0.69 us  [pool_weights(): m = mask.astype(F32)]
    unnamed x156 -> x14, local copies, waits for them, and re-layouts: 46.4 us -> 3.96 us
    all_gather x1 -> x0, waiting for transfers between devices: 35.3 us -> none  [local_step(): all_pass = lax.all_gather(p_embed, batch_axis, axis=0, tiled=True)]
  transfers between devices with their start and end apart: 3 -> 0, of which waited for: 3 -> 0; matrix products, arithmetic and copies ran while one was open for 9% -> 0% of each run, Pallas kernels for 0% -> 0%
where the time goes in v1:
time: 572 us; the launch traced here: 568 us
  Pallas kernels  541 us (95%)
  local copies, waits for them, and re-layouts  15.4 us (3%)
  other arithmetic  11.1 us (2%)
    pallas_call x1, Pallas kernels, sum_over_devices(): pl.pallas_call(functools.partial(sum_kernel, axis, piece), out_shape=(jax...  211 us
    pallas_call x1, Pallas kernels, ffn_backward(): pl.pallas_call(functools.partial(ffn_bwd_kernel, bounds), grid=(f // tile...  69.8 us
    pallas_call x1, Pallas kernels, ffn_forward(): pl.pallas_call(functools.partial(ffn_kernel, bounds), grid=(f // tile,),...  59.9 us
    pallas_call x1, Pallas kernels, unpack(): pl.pallas_call(functools.partial(unpack_kernel, n1, n2, n3), grid=(n4,),...  40.5 us
    pallas_call x1, Pallas kernels, gather_embeddings(): pl.pallas_call(functools.partial(gather_kernel, axis), out_shape=jax.Shap...  35.2 us
    pallas_call x2, Pallas kernels, attention_bwd(): pl.pallas_call(functools.partial(attn_bwd_kernel, head ** (-0.5), head),...  34.3 us
    pallas_call x1, Pallas kernels, qkv_backward(): pl.pallas_call(functools.partial(qkv_bwd_kernel, n), grid=(n + m,), out_s...  32.7 us
    pallas_call x1, Pallas kernels, loss_and_grad(): pl.pallas_call(functools.partial(loss_kernel, axis, n_query), out_shape=(...  27.9 us

profile of v1, /device:TPU:1, one launch (start us, length us, event | category | flops | bytes accessed | tf_op | source)
XLA Modules:
  0.0 568.2 jit_solution(7139140937179771847)
XLA Ops:
  0.6 0.8 convert_reduce_fusion
  2.4 0.8 convert_reduce_fusion.1
  4.1 1.4 reshape.131.b_ref
  5.5 1.4 stack.31.vec_ref
  6.9 1.1 copy.34.wt_ref
  8.0 3.3 pad_maximum_fusion.x_ref
  11.3 12.4 %qkv_project.1 = (bf16[192,3072]{1,0:T(8,128)(2,1)}, bf16[1024,3072]{1,0:T(8,128)(2,1)}) custom-call(bf16[1216,1024]{1,0:T(8,128)(2,1)} %pad_maximum_fusion.x_ref, bf16[3072,1024]{1,0:T(8,128)(2,1)} %bitcast.39, f32[1,3072]{1,0:T(1,128)} %reshape.131.b_ref), custom_call_target="tpu_custom_call" | custom-call | tf_op jit(solution)/shard_map/qkv_project/pallas_call | solution.py:493
  23.7 5.2 attention.2
  28.9 11.7 %attention.3 = (bf16[8,8,256,128]{3,2,1,0:T(8,128)(2,1)}, bf16[1024,1024]{1,0:T(8,128)(2,1)}) custom-call(bf16[1024,3072]{1,0:T(8,128)(2,1)} %get-tuple-element.48.qkv_ref, s32[8,1,128]{2,1,0:T(1,128)} %bitcast.48), custom_call_target="tpu_custom_call" | custom-call | tf_op jit(solution)/shard_map/attention/pallas_call | solution.py:534
  40.6 59.9 %ffn_forward.1 = (bf16[1216,1024]{1,0:T(8,128)(2,1)}, f32[1216,1024]{1,0:T(8,128)}, bf16[1216,4096]{1,0:T(8,128)(2,1)}, f32[1216,4096]{1,0:T(8,128)}, f32[1216,1024]{1,0:T(8,128)}, /*index=5*/f32[16,1024]{1,0:T(8,128)}) custom-call(bf16[1216,1024]{1,0:T(8,128)(2,1)} %pad_maximum_fusion.x_ref, bf16[192,1024]{1,0:T(8,128)(2,1)} %get-tuple-element.47.cq_ref, ...), custom_call_target="tpu_custom_call" | custom-call | tf_op jit(solution)/shard_map/ffn_forward/pallas_call | solution.py:643
  100.6 1.0 multiply_reduce_fusion
  101.6 0.9 broadcast_multiply_fusion.e_ref
  102.5 35.2 %gather_embeddings.1 = f32[4,4,4,24,1024]{4,3,2,1,0:T(8,128)S(1)} custom-call(f32[16,1024]{1,0:T(8,128)S(1)} %broadcast_multiply_fusion.e_ref), custom_call_target="tpu_custom_call" | custom-call | tf_op jit(solution)/shard_map/gather_embeddings/pallas_call | solution.py:369
  137.7 2.7 copy-done
  140.4 27.9 %loss_and_grad.1 = (f32[8,128]{1,0:T(8,128)S(1)}, f32[16,1024]{1,0:T(8,128)S(1)}) custom-call(f32[64,24,1024]{2,1,0:T(8,128)} %bitcast.38, f32[16,1024]{1,0:T(8,128)S(1)} %copy-done.1), custom_call_target="tpu_custom_call" | custom-call | tf_op jit(solution)/shard_map/loss_and_grad/pallas_call | solution.py:442
  169.4 69.8 %ffn_backward.1 = (f32[4096,1024]{1,0:T(8,128)}, f32[4,1024,1024]{2,1,0:T(8,128)}, f32[1,4096]{1,0:T(1,128)}, f32[1216,1024]{1,0:T(8,128)}, bf16[1216,1024]{1,0:...) custom-call(f32[16,1024]{1,0:T(8,128)} %copy-done.2, ...), custom_call_target="tpu_custom_call" | custom-call | tf_op jit(solution)/shard_map/ffn_backward/pallas_call | solution.py:708
  239.2 23.4 %attention_bwd.3.dp_ref = bf16[1024,3072]{1,0:T(8,128)(2,1)} custom-call(bf16[1024,3072]{1,0:T(8,128)(2,1)} %get-tuple-element.48.qkv_ref, bf16[8,8,256,128]{3,2,1,0:T(8,128)(2,1)} %get-tuple-element.60.probs_ref, bf16[1024,1024]{1,0:T(8,128)(2,1)} %get-tuple-element.61.dc_ref), custom_call_target="tpu_custom_call" | custom-call | tf_op jit(solution)/shard_map/attention_bwd/pallas_call | solution.py:564
  262.6 10.9 %attention_bwd.2.dq_ref = bf16[192,3072]{1,0:T(8,128)(2,1)} custom-call(bf16[192,3072]{1,0:T(8,128)(2,1)} %get-tuple-element.46.qkv_ref, bf16[4,8,96,48]{3,2,1,0:T(8,128)(2,1)} %get-tuple-element.52.probs_ref, bf16[192,1024]{1,0:T(8,128)(2,1)} %get-tuple-element.59.dc_ref), custom_call_target="tpu_custom_call" | custom-call | tf_op jit(solution)/shard_map/attention_bwd/pallas_call | solution.py:564
  273.5 32.7 %qkv_backward.1 = (f32[4096,1024]{1,0:T(8,128)}, f32[1,3072]{1,0:T(1,128)}, bf16[1216,1024]{1,0:T(8,128)(2,1)}) custom-call(bf16[192,3072]{1,0:T(8,128)(2,1)} %attention_bwd.2.dq_ref, bf16[1024,3072]{1,0:T(8,128)(2,1)} %attention_bwd.3.dp_ref, bf16[1216,1024]{1,0:T(8,128)(2,1)} %pad_maximum_fusion.x_ref, bf16[3072,1024]{1,0:T(8,128)(2,1)} %bitcast.40, ...), custom_call_target="tpu_custom_call" | custom-call | tf_op jit(solution)/shard_map/qkv_backward/pallas_call | solution.py:760
  306.7 1.4 reduce.8
  309.6 1.8 slice.34
  311.3 3.1 slice.35
  314.4 211.0 %sum_over_devices.1 = (f32[12288,1024]{1,0:T(8,128)}, f32[6144,1024]{1,0:T(8,128)}, f32[16,1024]{1,0:T(8,128)}) custom-call(f32[4096,1024]{1,0:T(8,128)} %get-tuple-element.65.u0_ref, f32[4096,1024]{1,0:T(8,128)} %bitcast.41, f32[4096,1024]{1,0:T(8,128)} %get-tuple-element.67.u2_ref, f32[16,1024]{1,0:T(8,128)} %maximum_maximum_fusion.small_ref), custom_call_target="tpu_custom_call" | custom-call | tf_op jit(solution)/shard_map/sum_over_devices/pallas_call | solution.py:276
  525.5 40.5 %unpack.1 = (f32[3072,1024]{1,0:T(8,128)}, f32[1024,1024]{1,0:T(8,128)}, f32[1024,4096]{1,0:T(8,128)}, f32[4096,1024]{1,0:T(8,128)}) custom-call(f32[12288,1024]{1,0:T(8,128)} %get-tuple-element.71.s_ref), custom_call_target="tpu_custom_call" | custom-call | tf_op jit(solution)/shard_map/unpack/pallas_call | solution.py:788
  (32 shorter events, 6.9 us)
Async XLA Ops:
  100.5 39.9 %copy-start.1 = (f32[16,1024]{1,0:T(8,128)S(1)}, f32[16,1024]{1,0:T(8,128)}, u32[]{:S(2)}) copy-start(f32[16,1024]{1,0:T(8,128)} %get-tuple-element.50.pooled_ref) | copy-start | bytes 196612
  137.7 2.7 copy-start
  168.3 0.6 copy-start.2
  273.5 34.6 %copy-start.5 = (f32[1,4096]{1,0:T(1,128)S(1)}, f32[1,4096]{1,0:T(1,128)}, u32[]{:S(2)}) copy-start(f32[1,4096]{1,0:T(1,128)} %get-tuple-element.70) | copy-start | bytes 49156
  273.5 35.3 %copy-start.4 = (f32[8,1024]{1,0:T(8,128)S(1)}, f32[8,1024]{1,0:T(8,128)}, u32[]{:S(2)}) copy-start(f32[8,1024]{1,0:T(8,128)} %get-tuple-element.68) | copy-start | bytes 98308
  525.5 40.5 %copy-start.3 = (f32[16,1024]{1,0:T(8,128)S(1)}, f32[16,1024]{1,0:T(8,128)}, u32[]{:S(2)}) copy-start(f32[16,1024]{1,0:T(8,128)} %get-tuple-element.73) | copy-start | bytes 196612

commit v2 on v1

v2 whole, which is shorter than its diff:
```python
import functools
import types
import jax
import jax.numpy as jnp
from jax import lax
from jax.experimental import pallas as pl
from jax.experimental.pallas import tpu as pltpu
from jax.sharding import PartitionSpec as P

ZERO, ONE, ALL = 0, 1, ...

F32 = jnp.float32
BF16 = jnp.bfloat16
LOGICAL = pl.DeviceIdType.LOGICAL
RING = 4
WIDTH = 256
COLOURS = range(6)
AXES = range(3)
RINGS = range(RING)
TURNS = range(RING * RING)
ANY = pl.BlockSpec(memory_space=pl.ANY)


def mesh_place(axis):
    me = lax.axis_index(axis)
    core = lax.rem(me, 2)
    chip = lax.div(me, 2)
    row = lax.div(chip, RING)
    return (lax.rem(chip, RING), lax.rem(row, RING), lax.div(row, RING)), core


def device_at(coords, core):
    return ((coords[2] * RING + coords[ONE]) * RING + coords[ZERO]) * 2 + core


def moved(coords, dim, by):
    out = list(coords)
    out[dim] = lax.rem(coords[dim] + by + 2 * RING, RING)
    return tuple(out)


def wrap(i):
    return lax.rem(i + 4 * RING, RING)


def rdma(src, dst, send, recv, to):
    pltpu.make_async_remote_copy(src_ref=src, dst_ref=dst, send_sem=send, recv_sem=recv,
                                 device_id=to, device_id_type=LOGICAL).start()


def copy(src, dst, sem):
    pltpu.make_async_copy(src, dst, sem).start()


def drain(ref, sem):
    pltpu.make_async_copy(ref, ref, sem).wait()


def carve(sems, *counts):
    out, at = [], ZERO
    for n in counts:
        out.append(lambda i, at=at: sems.at[at + i])
        at += n
    return out


def ring_plan(axis, units):
    coords, core = mesh_place(axis)
    p = types.SimpleNamespace(coords=coords, core=core, partner=device_at(coords, ONE - core))
    p.dims = [tuple((k // 2 + s) % 3 for s in AXES) for k in COLOURS]
    p.sign = [ONE - 2 * (k % 2) for k in COLOURS]
    p.pos = [tuple(coords[d] for d in p.dims[k]) for k in COLOURS]
    p.nxt = [tuple(device_at(moved(coords, d, p.sign[k]), core) for d in p.dims[k]) for k in COLOURS]
    p.piece = [8 * u for u in units]
    p.lead = [sum(p.piece[:k]) for k in COLOURS]
    p.all = sum(p.piece)
    p.half = 64 * p.all
    p.base = core * p.half
    p.ring_peers = [p.partner] + [device_at(moved(coords, d, by), core) for d in AXES for by in (ONE, 3)]
    p.at = lambda k, j, step, s: wrap(p.pos[k][s] - p.sign[k] * (ONE + step))
    return p


def rows(at, n):
    return pl.ds(pl.multiple_of(at, 8), n)


def chunk_row(p, k, step):
    return 64 * p.lead[k] + wrap(p.pos[k][ZERO] - p.sign[k] * (ONE + step)) * (16 * p.piece[k])


def sub_row(p, k, row, step):
    return row + wrap(p.pos[k][ONE] - p.sign[k] * (ONE + step)) * (4 * p.piece[k])


def piece_row(p, k, row, step):
    return row + wrap(p.pos[k][2] - p.sign[k] * (ONE + step)) * p.piece[k]


def signal_peers(peers):
    barrier = pltpu.get_barrier_semaphore()
    for peer in peers:
        pl.semaphore_signal(barrier, inc=ONE, device_id=peer, device_id_type=LOGICAL)


def await_peers(peers):
    pl.semaphore_wait(pltpu.get_barrier_semaphore(), len(peers))


SCATTER_SEMS = 4 + 3 * 16 + 2 * 12 + 4 * 3


def scatter_scratch(units):
    n = 8 * sum(units)
    vm = lambda *s: pltpu.VMEM(s + (WIDTH,), F32)
    return [vm(64 * n), vm(2, 4 * n), vm(3, RING, 4 * n), vm(3, 4 * n), vm(3, n), pltpu.SemaphoreType.DMA((SCATTER_SEMS,))]


def scatter_rounds(p, src, part, out, acc, stage, land1, land2, land3, sems):
    load_sem, swap_send, swap_recv, stage_sem, p1_send, p1_recv, p2_send, p2_recv, p3_send, p3_recv = carve(
        sems, 4, 16, 16, 16, 12, 12, 3, 3, 3, 3)
    n_sub, n_chunk = 4 * p.all, 16 * p.all
    far = p.half - p.base

    def turn_row(k, n):
        return sub_row(p, k, chunk_row(p, k, n // RING), n % RING)

    def load(t):
        for k in COLOURS:
            r, m = chunk_row(p, k, t), 16 * p.piece[k]
            copy(src.at[rows(p.base + r, m)], acc.at[rows(r, m)], load_sem(t))

    def swap(n):
        for k in COLOURS:
            r, m = turn_row(k, n), 4 * p.piece[k]
            rdma(src.at[rows(far + r, m)], part.at[rows(r, m)], swap_send(n), swap_recv(n), p.partner)

    def fetch(n):
        drain(part.at[pl.ds(ZERO, n_sub)], swap_recv(n))
        for k in COLOURS:
            m = 4 * p.piece[k]
            copy(part.at[rows(turn_row(k, n), m)], stage.at[n % 2, pl.ds(4 * p.lead[k], m)], stage_sem(n))

    def begin():
        for t in RINGS:
            load(t)
        for n in range(6):
            swap(n)

    def turn(n):
        t, i = n // RING, n % RING
        if n == ZERO:
            fetch(n)
        if n + 6 < 16:
            swap(n + 6)
        if n + ONE < 16:
            fetch(n + ONE)
        if i == ZERO:
            drain(acc.at[pl.ds(ZERO, n_chunk)], load_sem(t))
        drain(stage.at[n % 2], stage_sem(n))
        if t > ZERO:
            drain(land1.at[t - ONE, i], p1_recv(n - 4))
        for k in COLOURS:
            at, m = rows(turn_row(k, n), 4 * p.piece[k]), pl.ds(4 * p.lead[k], 4 * p.piece[k])
            val = acc[at] + stage[n % 2, m]
            acc[at] = val + land1[t - ONE, i, m] if t > ZERO else val
        if t < 3:
            for k in COLOURS:
                at, m = rows(turn_row(k, n), 4 * p.piece[k]), pl.ds(4 * p.lead[k], 4 * p.piece[k])
                rdma(acc.at[at], land1.at[t, i, m], p1_send(n), p1_recv(n), p.nxt[k][ZERO])

    def second(i):
        if i > ZERO:
            drain(land2.at[i - ONE], p2_recv(i - ONE))
        for k in COLOURS:
            at, m = rows(turn_row(k, 12 + i), 4 * p.piece[k]), pl.ds(4 * p.lead[k], 4 * p.piece[k])
            if i > ZERO:
                acc[at] += land2[i - ONE, m]
        if i < 3:
            for k in COLOURS:
                at, m = rows(turn_row(k, 12 + i), 4 * p.piece[k]), pl.ds(4 * p.lead[k], 4 * p.piece[k])
                rdma(acc.at[at], land2.at[i, m], p2_send(i), p2_recv(i), p.nxt[k][ONE])

    def third(g):
        if g > ZERO:
            drain(land3.at[g - ONE], p3_recv(g - ONE))
        for k in COLOURS:
            at, m = rows(piece_row(p, k, turn_row(k, 15), g), p.piece[k]), pl.ds(p.lead[k], p.piece[k])
            if g > ZERO:
                acc[at] += land3[g - ONE, m]
            if g == 3:
                out[m] = acc[at]
        if g < 3:
            for k in COLOURS:
                at, m = rows(piece_row(p, k, turn_row(k, 15), g), p.piece[k]), pl.ds(p.lead[k], p.piece[k])
                rdma(acc.at[at], land3.at[g, m], p3_send(g), p3_recv(g), p.nxt[k][2])

    def finish():
        for n in TURNS:
            drain(acc.at[pl.ds(ZERO, n_sub)], swap_send(n))
        for n in range(12):
            drain(acc.at[pl.ds(ZERO, n_sub)], p1_send(n))
        for t in AXES:
            drain(acc.at[pl.ds(ZERO, n_sub)], p2_send(t))
            drain(acc.at[pl.ds(ZERO, p.all)], p3_send(t))

    act = functools.partial
    def both(*fs):
        def run():
            for f in fs:
                f()
        return run
    steps = [begin] + [act(turn, n) for n in range(12)]
    steps += [both(act(turn, 12), act(second, ZERO)), act(turn, 13), act(turn, 14), act(turn, 15), act(second, ONE), act(second, 2),
              both(act(second, 3), act(third, ZERO)), act(third, ONE), act(third, 2), act(third, 3), finish]
    return steps


GATHER_SEMS = ONE + 2 * (3 + 3 + 12 + 16)


def gather_rounds(p, piece, out, sems):
    own_sem, a3_send, a3_recv, a2_send, a2_recv, a1_send, a1_recv, push_send, push_recv = carve(
        sems, ONE, 3, 3, 3, 3, 12, 12, 16, 16)
    n_sub = 4 * p.all

    def many(n):
        return out.at[pl.ds(ZERO, n)]

    def mine(k, c, s, g):
        return p.base + piece_row(p, k, sub_row(p, k, chunk_row(p, k, c - ONE), s - ONE), g - ONE)

    def sub_at(k, c, s):
        return rows(p.base + sub_row(p, k, chunk_row(p, k, c - ONE), s - ONE), 4 * p.piece[k])

    def hop3(t):
        for k in COLOURS:
            at = rows(mine(k, ZERO, ZERO, t), p.piece[k])
            src = piece.at[pl.ds(p.lead[k], p.piece[k])] if t == ZERO else out.at[at]
            if t == ZERO:
                copy(src, out.at[at], own_sem(ZERO))
            rdma(src, out.at[at], a3_send(t), a3_recv(t), p.nxt[k][2])

    def third(t):
        if t > ZERO:
            drain(many(p.all), a3_recv(t - ONE))
        if t < 3:
            hop3(t)
        if t == 3:
            drain(many(p.all), own_sem(ZERO))

    def hop1(c, s):
        for k in COLOURS:
            if c < 3:
                rdma(out.at[sub_at(k, c, s)], out.at[sub_at(k, c, s)], a1_send(RING * c + s), a1_recv(RING * c + s), p.nxt[k][ZERO])
            rdma(out.at[sub_at(k, c, s)], out.at[sub_at(k, c, s)], push_send(RING * c + s), push_recv(RING * c + s), p.partner)

    def second(s):
        if s > ZERO:
            drain(many(n_sub), a2_recv(s - ONE))
        if s < 3:
            for k in COLOURS:
                rdma(out.at[sub_at(k, ZERO, s)], out.at[sub_at(k, ZERO, s)], a2_send(s), a2_recv(s), p.nxt[k][ONE])
        hop1(ZERO, s)

    def first(c, s):
        drain(many(n_sub), a1_recv(RING * (c - ONE) + s))
        hop1(c, s)

    def finish():
        for t in AXES:
            drain(many(p.all), a3_send(t))
            drain(many(n_sub), a2_send(t))
        for n in range(12):
            drain(many(n_sub), a1_send(n))
        for n in TURNS:
            drain(many(n_sub), push_send(n))
            drain(many(n_sub), push_recv(n))

    act = functools.partial
    return ([act(third, t) for t in RINGS] + [act(second, s) for s in RINGS]
            + [act(first, c, s) for c in (ONE, 2, 3) for s in RINGS] + [finish])


def small_scratch(shape):
    return [pltpu.VMEM((4, 3) + shape, F32), pltpu.SemaphoreType.DMA((8,))]


def small_rounds(p, src, out, land, sems):
    places = [(None, p.core, 2)] + [(d, p.coords[d], RING) for d in AXES]

    def send(n):
        d, _, size = places[n]
        for by in range(ONE, size):
            to = p.partner if d is None else device_at(moved(p.coords, d, by), p.core)
            rdma(out, land.at[n, by - ONE], sems.at[n], sems.at[4 + n], to)

    def step(n):
        if n == ZERO:
            out[ALL] = src[ALL]
        else:
            _, place, size = places[n - ONE]
            got = land.at[n - ONE, pl.ds(ZERO, size - ONE)]
            drain(got, sems.at[4 + n - ONE])
            drain(got, sems.at[n - ONE])
            mine, total = out[ALL], None
            for q in range(size):
                val = mine
                for by in range(ONE, size):
                    val = jnp.where(lax.rem(place - q + size, size) == by, land[n - ONE, by - ONE], val)
                total = val if total is None else total + val
            out[ALL] = total
        if n < 4:
            send(n)

    return [functools.partial(step, n) for n in range(5)]


def spread(steps, slots):
    plan = [[] for _ in range(slots)]
    for i, s in enumerate(steps):
        plan[i * slots // len(steps)].append(s)
    return plan


def run_slot(plan, j, per, point):
    for s in range(len(plan) // per):
        todo = plan[s * per + point]
        if todo:
            @pl.when(j == s)
            def _():
                for f in todo:
                    f()


def all_peers(p):
    return [p.partner] + [device_at(moved(p.coords, d, by), p.core) for d in AXES for by in (ONE, 2, 3)]


def finish_kernel(axis, units_b, units_c, pieceb_ref, c_ref, small_ref, b_out, c_out, small_out, part, piecec, *scratch):
    sc, (gather_sem, gather_sem2, small_land, small_sem) = scratch[:6], scratch[6:]
    pb, pc = ring_plan(axis, units_b), ring_plan(axis, units_c)
    peers = all_peers(pb)
    signal_peers(peers)
    await_peers(peers)
    reduce_c = scatter_rounds(pc, c_ref, part, piecec, *sc)
    gather_b = gather_rounds(pb, pieceb_ref, b_out, gather_sem)
    smalls = small_rounds(pb, small_ref, small_out, small_land, small_sem)
    reduce_c[ZERO]()
    n = len(reduce_c)
    fill = spread(gather_b[:-ONE], n - 2)
    for i in range(ONE, n - ONE):
        reduce_c[i]()
        if i % 3 == ONE and i // 3 < len(smalls):
            smalls[i // 3]()
        for f in fill[i - ONE]:
            f()
    for f in gather_rounds(pc, piecec, c_out, gather_sem2):
        f()
    reduce_c[-ONE]()
    gather_b[-ONE]()


def finish_sum(axis, units_b, units_c, piece_b, c, small, collective_id):
    sds = jax.ShapeDtypeStruct
    dma = pltpu.SemaphoreType.DMA
    vm = pl.BlockSpec(memory_space=pltpu.VMEM)
    n = c.shape[ZERO]
    outs = pl.pallas_call(
        functools.partial(finish_kernel, axis, units_b, units_c),
        out_shape=(sds(c.shape, F32), sds(c.shape, F32), sds(small.shape, F32), sds((n // 2, WIDTH), F32), sds((n // 128, WIDTH), F32)),
        in_specs=[vm, ANY, vm], out_specs=(ANY, ANY, vm, ANY, vm),
        scratch_shapes=scatter_scratch(units_c) + [dma((GATHER_SEMS,)), dma((GATHER_SEMS,))] + small_scratch(small.shape),
        compiler_params=pltpu.CompilerParams(collective_id=collective_id, has_side_effects=True, vmem_limit_bytes=48 * 1024 * 1024),
        name="finish_sum",
    )(piece_b, c, small)
    return outs[:3]


def gather_kernel(axis, e_ref, g_ref, mine, theirs, swap_sem, sems_send, sems_recv, push_send, push_recv):
    coords, core = mesh_place(axis)
    partner = device_at(coords, ONE - core)
    width = e_ref.shape[ONE]
    lanes = pl.ds(pl.multiple_of(core * (width // 2), 128), width // 2)
    x, y, z = coords
    peers = [partner] + [device_at(moved(coords, d, by), core) for d in AXES for by in (ONE, 2, 3)]
    signal_peers(peers)
    await_peers(peers)

    rdma(e_ref, theirs, swap_sem.at[ZERO], swap_sem.at[ONE], partner)
    mine[ALL] = e_ref[ALL]
    drain(theirs, swap_sem.at[ONE])
    first = jnp.where(core == ZERO, mine[:, lanes], theirs[:, lanes])
    second = jnp.where(core == ZERO, theirs[:, lanes], mine[:, lanes])
    g_ref[z, y, x, ZERO:4, lanes] = first[ZERO:4]
    g_ref[z, y, x, 4:8, lanes] = second[ZERO:4]
    g_ref[z, y, x, 8:16, lanes] = first[8:16]
    g_ref[z, y, x, 16:24, lanes] = second[8:16]
    drain(e_ref, swap_sem.at[ZERO])

    def view(a, stage):
        idx = [z, y, x]
        for s in range(stage):
            idx[2 - (a + s) % 3] = slice(None)
        return g_ref.at[idx[ZERO], idx[ONE], idx[2], pl.ds(8 * a, 8), lanes]

    for stage in range(3):
        for by in (ONE, 3, 2):
            for a in range(3):
                to = device_at(moved(coords, (a + stage) % 3, by), core)
                rdma(view(a, stage), view(a, stage), sems_send.at[stage, by - ONE], sems_recv.at[stage, by - ONE], to)
        if stage == 2:
            for a in range(3):
                rdma(view(a, 2), view(a, 2), push_send.at[ZERO], push_recv.at[ZERO], partner)
        for by in (ONE, 3, 2):
            n = 4 ** stage
            shape_like = g_ref.at[ZERO, ZERO, ZERO, :, lanes] if stage == ZERO else (
                g_ref.at[ZERO, ZERO, :, :, lanes] if stage == ONE else g_ref.at[ZERO, :, :, :, lanes])
            drain(shape_like, sems_recv.at[stage, by - ONE])
            if stage == 2:
                for a in range(3):
                    far = moved(coords, (a + 2) % 3, RING - by)
                    idx = [far[2], far[ONE], far[ZERO]]
                    idx[2 - a] = slice(None)
                    idx[2 - (a + ONE) % 3] = slice(None)
                    v = g_ref.at[idx[ZERO], idx[ONE], idx[2], pl.ds(8 * a, 8), lanes]
                    rdma(v, v, push_send.at[by], push_recv.at[by], partner)
    for stage in range(3):
        shape_like = g_ref.at[ZERO, ZERO, ZERO, :, lanes] if stage == ZERO else (
            g_ref.at[ZERO, ZERO, :, :, lanes] if stage == ONE else g_ref.at[ZERO, :, :, :, lanes])
        for by in (ONE, 2, 3):
            drain(shape_like, sems_send.at[stage, by - ONE])
    for by in range(4):
        drain(g_ref.at[ZERO, :, :, :, lanes], push_send.at[by])
        drain(g_ref.at[ZERO, :, :, :, lanes], push_recv.at[by])


def gather_embeddings(e, axis, collective_id=2):
    dma = pltpu.SemaphoreType.DMA
    width = e.shape[ONE]
    g = pl.pallas_call(
        functools.partial(gather_kernel, axis),
        out_shape=jax.ShapeDtypeStruct((RING, RING, RING, 24, width), F32),
        in_specs=[pl.BlockSpec(memory_space=pltpu.VMEM)],
        out_specs=pl.BlockSpec(memory_space=pltpu.VMEM),
        scratch_shapes=[pltpu.VMEM(e.shape, F32), pltpu.VMEM(e.shape, F32), dma((2,)),
                        dma((3, 3)), dma((3, 3)), dma((4,)), dma((4,))],
        compiler_params=pltpu.CompilerParams(collective_id=collective_id, has_side_effects=True,
                                             vmem_limit_bytes=16 * 1024 * 1024),
        name="gather_embeddings",
    )(e)
    return g.reshape(RING ** 3, 24, width)


def loss_kernel(axis, n_query, g_ref, pooled_ref, loss_ref, d_ref, logit_ref, lse_ref):
    me = lax.axis_index(axis)
    core, chip = lax.rem(me, 2), lax.div(me, 2)
    width = pooled_ref.shape[ONE]
    chips = g_ref.shape[ZERO]
    gs = 100.0 / n_query
    hi = lax.Precision.HIGHEST
    nt = (((ONE,), (ONE,)), ((), ()))
    pall = g_ref[:, 8:24, :].reshape(chips * 16, width)
    block = 128
    per = block // 8

    def chunk(b, loss):
        qb = g_ref[pl.ds(b * per, per), ZERO:8, :].reshape(block, width)
        s = lax.dot_general(qb, pall, nt, precision=hi, preferred_element_type=F32) * 100.0
        logit_ref[pl.ds(pl.multiple_of(b * block, block), block), :] = s
        top = jnp.max(s, axis=ONE, keepdims=True)
        lse = jnp.log(jnp.sum(jnp.exp(s - top), axis=ONE, keepdims=True)) + top
        lse_ref[pl.ds(pl.multiple_of(b * block, block), block), :] = jnp.broadcast_to(lse, (block, 128))
        row = lax.broadcasted_iota(jnp.int32, s.shape, ZERO) + b * block
        col = lax.broadcasted_iota(jnp.int32, s.shape, ONE)
        pos = jnp.sum(jnp.where(col == 2 * row, s, 0.0), axis=ONE, keepdims=True)
        return loss + jnp.sum(lse - pos, axis=ZERO, keepdims=True)

    loss = lax.fori_loop(ZERO, chips // per, chunk, jnp.zeros((ONE, ONE), F32))
    loss_ref[ALL] = jnp.broadcast_to(loss * (1.0 / n_query), loss_ref.shape)

    at = pl.multiple_of(chip * 8, 8)
    s8 = logit_ref[pl.ds(at, 8), :]
    l8 = lse_ref[pl.ds(at, 8), ZERO:ONE]
    row = lax.broadcasted_iota(jnp.int32, s8.shape, ZERO) + chip * 8
    col = lax.broadcasted_iota(jnp.int32, s8.shape, ONE)
    w8 = jnp.exp(s8 - l8) * gs - jnp.where(col == 2 * row, gs, 0.0)
    dq8 = lax.dot_general(w8, pall, (((ONE,), (ZERO,)), ((), ())), precision=hi, preferred_element_type=F32)

    qall = g_ref[:, ZERO:8, :].reshape(chips * 8, width)
    p16 = g_ref[chip, 8:24, :]
    s16 = lax.dot_general(qall, p16, nt, precision=hi, preferred_element_type=F32) * 100.0
    row = lax.broadcasted_iota(jnp.int32, s16.shape, ZERO)
    col = lax.broadcasted_iota(jnp.int32, s16.shape, ONE) + chip * 16
    w16 = jnp.exp(s16 - lse_ref[:, ZERO:ONE]) * gs - jnp.where(col == 2 * row, gs, 0.0)
    dp16 = lax.dot_general(w16, qall, (((ZERO,), (ZERO,)), ((), ())), precision=hi, preferred_element_type=F32)

    dq = jnp.where(core == ZERO, dq8[ZERO:4], dq8[4:8])
    dp = jnp.where(core == ZERO, dp16[ZERO:8], dp16[8:16])
    pooled_q, pooled_p = pooled_ref[ZERO:4], pooled_ref[8:16]

    def back(d, pooled):
        inv = lax.rsqrt(jnp.sum(pooled * pooled, axis=ONE, keepdims=True))
        e = pooled * inv
        return (d - e * jnp.sum(e * d, axis=ONE, keepdims=True)) * inv

    d_ref[ALL] = jnp.zeros_like(d_ref)
    d_ref[ZERO:4, :] = back(dq, pooled_q)
    d_ref[8:16, :] = back(dp, pooled_p)


def loss_and_grad(g, pooled, axis, n_query):
    chips, _, width = g.shape
    loss, d = pl.pallas_call(
        functools.partial(loss_kernel, axis, n_query),
        out_shape=(jax.ShapeDtypeStruct((8, 128), F32), jax.ShapeDtypeStruct(pooled.shape, F32)),
        in_specs=[pl.BlockSpec(memory_space=pltpu.VMEM)] * 2,
        out_specs=(pl.BlockSpec(memory_space=pltpu.VMEM),) * 2,
        scratch_shapes=[pltpu.VMEM((chips * 8, chips * 16), F32), pltpu.VMEM((chips * 8, 128), F32)],
        compiler_params=pltpu.CompilerParams(vmem_limit_bytes=48 * 1024 * 1024),
        name="loss_and_grad",
    )(g, pooled)
    return loss[ZERO, ZERO], d


NN = (((ONE,), (ZERO,)), ((), ()))
NT = (((ONE,), (ONE,)), ((), ()))
TN = (((ZERO,), (ZERO,)), ((), ()))
LN_EPS = 1e-12
NEG_FILL = -1e9
TILE = 512
UNITS_A, UNITS_B, UNITS_C = (3, 3, 3, 3, 2, 2), (3, 3, 2, 2, 3, 3), (2, 2, 3, 3, 3, 3)
sds = jax.ShapeDtypeStruct


def mm(a, b, dims=NN):
    return lax.dot_general(a, b, dims, preferred_element_type=F32)


def vmem(mb=60):
    return pltpu.CompilerParams(vmem_limit_bytes=mb * 1024 * 1024)


def whole(*shape):
    return pl.BlockSpec(shape, lambda j: (ZERO,) * len(shape), pipeline_mode=pl.Buffered(ONE))


def across(rows, tile):
    return pl.BlockSpec((rows, tile), lambda j: (ZERO, j))


def down(tile, cols):
    return pl.BlockSpec((tile, cols), lambda j: (j, ZERO))


def row_mean(x):
    return jnp.mean(x, axis=ONE, keepdims=True)


def row_sum(x):
    return jnp.sum(x, axis=ONE, keepdims=True)


def col_sum(x):
    return jnp.sum(x, axis=ZERO, keepdims=True)


def qkv_kernel(x_ref, w_ref, b_ref, oq_ref, op_ref):
    y = (mm(x_ref[ALL], w_ref[ALL], NT) + b_ref[ALL]).astype(BF16)
    tq = oq_ref.shape[ZERO]
    oq_ref[ALL] = y[:tq]
    op_ref[ALL] = y[tq:]


def qkv_project(x, w_t, b, tq, tile=TILE):
    t, d = x.shape
    f = w_t.shape[ZERO]
    return pl.pallas_call(
        qkv_kernel, grid=(f // tile,),
        out_shape=(sds((tq, f), BF16), sds((t - tq, f), BF16)),
        in_specs=[whole(t, d), down(tile, d), across(ONE, tile)],
        out_specs=(across(tq, tile), across(t - tq, tile)),
        compiler_params=vmem(), name="qkv_project",
    )(x, w_t, b)


def split_heads(pair, head):
    lane = lax.broadcasted_iota(jnp.int32, pair.shape, ONE)
    zero = jnp.zeros_like(pair)
    return jnp.concatenate([jnp.where(lane < head, pair, zero), jnp.where(lane >= head, pair, zero)], axis=ZERO)


def join_heads(stacked, head):
    t = stacked.shape[ZERO] // 2
    lane = lax.broadcasted_iota(jnp.int32, (t, stacked.shape[ONE]), ONE)
    return jnp.where(lane < head, stacked[:t], stacked[t:])


def attn_kernel(scale, head, qkv_ref, mask_ref, probs_ref, ctx_ref):
    d = ctx_ref.shape[ONE]
    pair = 2 * head
    keep = mask_ref[ZERO] > ZERO
    for g in range(d // pair):
        at = pl.ds(g * pair, pair)
        q = split_heads(qkv_ref[:, at], head)
        k = qkv_ref[:, pl.ds(d + g * pair, pair)]
        v = qkv_ref[:, pl.ds(2 * d + g * pair, pair)]
        s = jnp.where(keep, mm(q, k, NT) * scale, NEG_FILL)
        e = jnp.exp(s - jnp.max(s, axis=ONE, keepdims=True))
        p = (e / row_sum(e)).astype(BF16)
        probs_ref[ZERO, g] = p
        ctx_ref[:, at] = join_heads(mm(p, v), head).astype(BF16)


def attention(qkv, mask, head):
    n, seq = mask.shape
    d = qkv.shape[ONE] // 3
    pairs = d // (2 * head)
    return pl.pallas_call(
        functools.partial(attn_kernel, head ** -0.5, head), grid=(n,),
        out_shape=(sds((n, pairs, 2 * seq, seq), BF16), sds((n * seq, d), BF16)),
        in_specs=[down(seq, 3 * d), pl.BlockSpec((ONE, ONE, seq), lambda j: (j, ZERO, ZERO))],
        out_specs=(pl.BlockSpec((ONE, pairs, 2 * seq, seq), lambda j: (j, ZERO, ZERO, ZERO)), down(seq, d)),
        compiler_params=vmem(), name="attention",
    )(qkv, mask.reshape(n, ONE, seq))


def norm_rows(x):
    c = x - row_mean(x)
    r = lax.rsqrt(row_mean(c * c) + LN_EPS)
    return c * r, r


def norm_back(g, hat, r):
    return r * (g - row_mean(g) - hat * row_mean(g * hat))


ERFC = (0.07122347, -0.27794802, 0.29668747, -0.02018065, 0.21581222, 0.21731356, 0.24887118, 0.24822095)


def gelu_parts(u):
    bell = jnp.exp(-0.5 * u * u)
    t = 1.0 / (1.0 + 0.311126984 * jnp.abs(u))
    poly = ERFC[ZERO]
    for c in ERFC[ONE:]:
        poly = poly * t + c
    tail = 0.5 * bell * (poly * t)
    return jnp.where(u >= 0.0, 1.0 - tail, tail), u * bell * 0.3989422804


ROWS = 304


def ffn_kernel(bounds, x_ref, cq_ref, cp_ref, wo_ref, vec_ref, wt_ref, wu_ref, bu_ref, wd_ref,
               h_ref, r1q_ref, r1p_ref, g_ref, gp_ref, r2_ref, pool_ref):
    j = pl.program_id(ZERO)
    t = x_ref.shape[ZERO]
    tq = cq_ref.shape[ZERO]
    b_out, g1, s1, b_down, g2, s2 = (vec_ref[i:i + ONE, :] for i in range(6))

    @pl.when(j == ZERO)
    def _():
        for ref, r_ref, lo in ((cq_ref, r1q_ref, ZERO), (cp_ref, r1p_ref, tq)):
            n = ref.shape[ZERO]
            size = min(n, 256)
            for a in range(ZERO, n, size):
                at = pl.ds(lo + a, size)
                r1 = x_ref[at, :].astype(F32) + mm(ref[pl.ds(a, size), :], wo_ref[ALL]) + b_out
                r_ref[pl.ds(a, size), :] = r1
                h = (norm_rows(r1)[ZERO] * g1 + s1).astype(BF16)
                h_ref[at, :] = h
                r2_ref[at, :] = h.astype(F32) + b_down

    for a in range(ZERO, t, ROWS):
        at = pl.ds(a, ROWS)
        u = mm(h_ref[at, :], wu_ref[ALL]) + bu_ref[ALL]
        cdf, upd = gelu_parts(u)
        g = (u * cdf).astype(BF16)
        g_ref[at, :] = g
        gp_ref[at, :] = cdf + upd
        r2_ref[at, :] += mm(g, wd_ref[ALL])

    @pl.when(j == pl.num_programs(ZERO) - ONE)
    def _():
        pool_ref[ALL] = jnp.zeros_like(pool_ref)
        for row, lo, n in bounds:
            at = pl.ds(lo, n)
            y = norm_rows(r2_ref[at, :])[ZERO] * g2 + s2
            pool_ref[row:row + ONE, :] = col_sum(y * wt_ref[at, :])


def ffn_forward(x, ctx_q, ctx_p, w_out, vecs, weights, w_up, b_up, w_down, bounds, tile=TILE):
    t, d = x.shape
    tq, tp = ctx_q.shape[ZERO], ctx_p.shape[ZERO]
    f = w_up.shape[ONE]
    return pl.pallas_call(
        functools.partial(ffn_kernel, bounds), grid=(f // tile,),
        out_shape=(sds((t, d), BF16), sds((tq, d), F32), sds((tp, d), F32), sds((t, f), BF16), sds((t, f), F32),
                   sds((t, d), F32), sds((16, d), F32)),
        in_specs=[whole(t, d), whole(tq, d), whole(tp, d), whole(d, d), whole(*vecs.shape), whole(t, ONE),
                  across(d, tile), across(ONE, tile), down(tile, d)],
        out_specs=(whole(t, d), whole(tq, d), whole(tp, d), across(t, tile), across(t, tile), whole(t, d), whole(16, d)),
        compiler_params=vmem(), name="ffn_forward",
    )(x, ctx_q, ctx_p, w_out, vecs, weights, w_up, b_up, w_down)


def store_blocks(ref, val):
    for c in range(ref.shape[ZERO]):
        ref[c] = val[:, c * WIDTH:(c + ONE) * WIDTH]


def down_bwd_kernel(bounds, dpool_ref, r2_ref, wt_ref, vec_ref, g_ref, dwd_ref, dr2_ref, dr2b_ref, dvec_ref):
    g2 = vec_ref[4:5, :]

    @pl.when(pl.program_id(ZERO) == ZERO)
    def _():
        dvec_ref[ALL] = jnp.zeros_like(dvec_ref)
        for row, lo, n in bounds:
            at = pl.ds(lo, n)
            hat, r = norm_rows(r2_ref[at, :])
            dy = wt_ref[at, :] * dpool_ref[row:row + ONE, :]
            dr2 = norm_back(dy * g2, hat, r)
            dr2_ref[at, :] = dr2
            dr2b_ref[at, :] = dr2.astype(BF16)
            dvec_ref[ZERO:ONE, :] += col_sum(dr2)
            dvec_ref[ONE:2, :] += col_sum(dy * hat)
            dvec_ref[2:3, :] += col_sum(dy)

    store_blocks(dwd_ref, mm(g_ref[ALL], dr2b_ref[ALL], TN))


def down_backward(dpool, r2, weights, vecs, g, bounds, tile=TILE):
    t, d = r2.shape
    f = g.shape[ONE]
    n = d // WIDTH
    return pl.pallas_call(
        functools.partial(down_bwd_kernel, bounds), grid=(f // tile,),
        out_shape=(sds((n, f, WIDTH), F32), sds((t, d), F32), sds((t, d), BF16), sds((8, d), F32)),
        in_specs=[whole(*dpool.shape), whole(t, d), whole(t, ONE), whole(*vecs.shape), across(t, tile)],
        out_specs=(pl.BlockSpec((n, tile, WIDTH), lambda j: (ZERO, j, ZERO)), whole(t, d), whole(t, d), whole(8, d)),
        compiler_params=vmem(), name="down_backward",
    )(dpool, r2, weights, vecs, g)


def up_bwd_kernel(axis, dr2_ref, dr2b_ref, h_ref, gp_ref, wd_ref, wu_ref, a_ref,
                  dwu_ref, dbu_ref, dnq_ref, dnp_ref, piece_ref, part_ref, ht_ref, *scratch):
    j = pl.program_id(ZERO)
    tq = dnq_ref.shape[ZERO]
    p = ring_plan(axis, UNITS_A)
    peers = p.ring_peers
    points = 3
    steps = scatter_rounds(p, a_ref, part_ref, piece_ref, *scratch)
    plan = spread([functools.partial(signal_peers, peers), functools.partial(await_peers, peers)] + steps,
                  points * STEPS)

    @pl.when(j == ZERO)
    def _():
        ht_ref[ALL] = h_ref[ALL].T
        dnq_ref[ALL] = dr2_ref[:tq, :]
        dnp_ref[ALL] = dr2_ref[tq:, :]

    run_slot(plan, j, points, ZERO)
    dg = mm(dr2b_ref[ALL], wd_ref[ALL], NT).astype(BF16).astype(F32)
    dpre = dg * gp_ref[ALL]
    dbu_ref[ALL] = col_sum(dpre)
    dpre = dpre.astype(BF16)
    run_slot(plan, j, points, ONE)
    dwu = mm(ht_ref[ALL], dpre)
    for c in range(dwu_ref.shape[ZERO]):
        dwu_ref[c] = dwu[:, c * WIDTH:(c + ONE) * WIDTH]
    run_slot(plan, j, points, 2)
    dnq_ref[ALL] += mm(dpre[:tq], wu_ref[ALL], NT)
    dnp_ref[ALL] += mm(dpre[tq:], wu_ref[ALL], NT)


STEPS = 8


def up_backward(axis, dr2, dr2b, h, gp, w_down, w_up, part_a, tq, collective_id, tile=TILE):
    t, d = h.shape
    f = w_up.shape[ONE]
    n = tile // WIDTH
    total = part_a.shape[ZERO]
    return pl.pallas_call(
        functools.partial(up_bwd_kernel, axis), grid=(f // tile,),
        out_shape=(sds((f // WIDTH, d, WIDTH), F32), sds((ONE, f), F32), sds((tq, d), F32), sds((t - tq, d), F32),
                   sds((total // 128, WIDTH), F32), sds((total // 2, WIDTH), F32)),
        in_specs=[whole(t, d), whole(t, d), whole(t, d), across(t, tile), down(tile, d), across(d, tile), ANY],
        out_specs=(pl.BlockSpec((n, d, WIDTH), lambda j: (j, ZERO, ZERO)), across(ONE, tile), whole(tq, d), whole(t - tq, d),
                   whole(total // 128, WIDTH), ANY),
        scratch_shapes=[pltpu.VMEM((d, t), BF16)] + scatter_scratch(UNITS_A),
        compiler_params=pltpu.CompilerParams(collective_id=collective_id, has_side_effects=True, vmem_limit_bytes=63 * 1024 * 1024),
        name="up_backward",
    )(dr2, dr2b, h, gp, w_down, w_up, part_a)


def attn_bwd_body(scale, head, dn_ref, r1_ref, vec_ref, wo_ref, qkv_ref, probs_ref, d_ref, dr1_ref, dr1b_ref, dvec_ref, pause):
    d = dn_ref.shape[ONE]
    pair = 2 * head
    dy = dn_ref[ALL].astype(BF16).astype(F32)
    hat, r = norm_rows(r1_ref[ALL])
    dr1 = norm_back(dy * vec_ref[ONE:2, :], hat, r)
    dr1_ref[ALL] = dr1
    low = dr1.astype(BF16)
    dr1b_ref[ALL] = low

    @pl.when(pl.program_id(ZERO) == ZERO)
    def _():
        dvec_ref[ALL] = jnp.zeros_like(dvec_ref)
    dvec_ref[ZERO:ONE, :] += col_sum(dr1)
    dvec_ref[ONE:2, :] += col_sum(dy * hat)
    dvec_ref[2:3, :] += col_sum(dy)
    dctx = mm(low, wo_ref[ALL], NT).astype(BF16)
    pause(ZERO)
    for g in range(d // pair):
        if 2 * g == d // pair:
            pause(ONE)
        at = pl.ds(g * pair, pair)
        q = split_heads(qkv_ref[:, at], head)
        k = qkv_ref[:, pl.ds(d + g * pair, pair)]
        v = qkv_ref[:, pl.ds(2 * d + g * pair, pair)]
        p = probs_ref[ZERO, g]
        dc = split_heads(dctx[:, g * pair:(g + ONE) * pair], head)
        dp = mm(dc, v, NT)
        pf = p.astype(F32)
        ds = (pf * (dp - row_sum(dp * pf)) * scale).astype(BF16)
        d_ref[:, at] = join_heads(mm(ds, k), head).astype(BF16)
        d_ref[:, pl.ds(d + g * pair, pair)] = mm(ds, q, TN).astype(BF16)
        d_ref[:, pl.ds(2 * d + g * pair, pair)] = mm(p, dc, TN).astype(BF16)
    pause(2)


def attn_bwd_plain(scale, head, *refs):
    attn_bwd_body(scale, head, *refs, lambda point: None)


def attn_bwd_host(scale, head, axis, dn_ref, r1_ref, vec_ref, wo_ref, qkv_ref, probs_ref, b_ref,
                  d_ref, dr1_ref, dr1b_ref, dvec_ref, piece_ref, part_ref, *scratch):
    p = ring_plan(axis, UNITS_B)
    peers = p.ring_peers
    points = 3
    steps = scatter_rounds(p, b_ref, part_ref, piece_ref, *scratch)
    plan = spread([functools.partial(signal_peers, peers), functools.partial(await_peers, peers)] + steps,
                  points * STEPS)
    j = pl.program_id(ZERO)
    attn_bwd_body(scale, head, dn_ref, r1_ref, vec_ref, wo_ref, qkv_ref, probs_ref, d_ref, dr1_ref, dr1b_ref, dvec_ref,
                  functools.partial(run_slot, plan, j, points))


def attention_bwd(dn, r1, vecs, w_out, qkv, probs, head, axis=None, part_b=None, collective_id=None):
    n, pairs, _, seq = probs.shape
    d = dn.shape[ONE]
    scale = head ** -0.5
    in_specs = [down(seq, d), down(seq, d), whole(*vecs.shape), whole(d, d), down(seq, 3 * d),
                pl.BlockSpec((ONE, pairs, 2 * seq, seq), lambda j: (j, ZERO, ZERO, ZERO))]
    out_shape = [sds((n * seq, 3 * d), BF16), sds((n * seq, d), F32), sds((n * seq, d), BF16), sds((8, d), F32)]
    out_specs = [down(seq, 3 * d), down(seq, d), down(seq, d), whole(8, d)]
    args = (dn, r1, vecs, w_out, qkv, probs)
    if part_b is None:
        return pl.pallas_call(
            functools.partial(attn_bwd_plain, scale, head), grid=(n,), out_shape=out_shape, in_specs=in_specs, out_specs=out_specs,
            compiler_params=vmem(), name="attention_bwd")(*args)
    total = part_b.shape[ZERO]
    return pl.pallas_call(
        functools.partial(attn_bwd_host, scale, head, axis), grid=(n,),
        out_shape=out_shape + [sds((total // 128, WIDTH), F32), sds((total // 2, WIDTH), F32)],
        in_specs=in_specs + [ANY], out_specs=out_specs + [whole(total // 128, WIDTH), ANY],
        scratch_shapes=scatter_scratch(UNITS_B),
        compiler_params=pltpu.CompilerParams(collective_id=collective_id, has_side_effects=True, vmem_limit_bytes=60 * 1024 * 1024),
        name="attention_bwd_host")(*args, part_b)


def qkv_bwd_kernel(axis, steps, dq_ref, dp_ref, x_ref, w_ref, dr1q_ref, dr1p_ref, cq_ref, cp_ref, dr1bq_ref, dr1bp_ref, piece_ref,
                   dw_ref, db_ref, dhq_ref, dhp_ref, a_ref, accq_ref, accp_ref, sems):
    j = pl.program_id(ZERO)
    tq = dq_ref.shape[ZERO]
    p = ring_plan(axis, UNITS_A)
    peers = p.ring_peers
    points = 2
    plan = spread([functools.partial(signal_peers, peers), functools.partial(await_peers, peers)]
                  + gather_rounds(p, piece_ref, a_ref, sems), points * STEPS)
    run_slot(plan, j, points, ZERO)

    @pl.when(j == ZERO)
    def _():
        accq_ref[ALL] = dr1q_ref[ALL]
        accp_ref[ALL] = dr1p_ref[ALL]

    @pl.when(j < steps)
    def _():
        accq_ref[ALL] += mm(dq_ref[ALL], w_ref[ALL])
        accp_ref[ALL] += mm(dp_ref[ALL], w_ref[ALL])
        store_blocks(dw_ref, mm(dq_ref[ALL], x_ref[:tq, :], TN) + mm(dp_ref[ALL], x_ref[tq:, :], TN))
        db_ref[ALL] = col_sum(dq_ref[ALL].astype(F32)) + col_sum(dp_ref[ALL].astype(F32))

    @pl.when(j == steps - ONE)
    def _():
        dhq_ref[ALL] = accq_ref[ALL].astype(BF16)
        dhp_ref[ALL] = accp_ref[ALL].astype(BF16)

    @pl.when(j >= steps)
    def _():
        store_blocks(dw_ref, mm(cq_ref[ALL], dr1bq_ref[ALL], TN) + mm(cp_ref[ALL], dr1bp_ref[ALL], TN))
    run_slot(plan, j, points, ONE)


def qkv_backward(axis, dq, dp, x, w_t, dr1_q, dr1_p, ctx_q, ctx_p, dr1b_q, dr1b_p, piece, collective_id, tile=TILE):
    t, d = x.shape
    f = w_t.shape[ZERO]
    tq, tp = dq.shape[ZERO], dp.shape[ZERO]
    n, m = f // tile, d // tile
    cut = lambda j: (ZERO, jnp.minimum(j, n - ONE))
    late = lambda j: (ZERO, jnp.maximum(j - n, ZERO))
    cols = d // WIDTH
    return pl.pallas_call(
        functools.partial(qkv_bwd_kernel, axis, n), grid=(n + m,),
        out_shape=(sds((cols, f + d, WIDTH), F32), sds((ONE, f), F32), sds((tq, d), BF16), sds((tp, d), BF16),
                   sds((piece.shape[ZERO] * 128, WIDTH), F32)),
        in_specs=[pl.BlockSpec((tq, tile), cut), pl.BlockSpec((tp, tile), cut),
                  whole(t, d), pl.BlockSpec((tile, d), lambda j: (jnp.minimum(j, n - ONE), ZERO)), whole(tq, d), whole(tp, d),
                  pl.BlockSpec((tq, tile), late), pl.BlockSpec((tp, tile), late), whole(tq, d), whole(tp, d), whole(*piece.shape)],
        out_specs=(pl.BlockSpec((cols, tile, WIDTH), lambda j: (ZERO, j, ZERO)), pl.BlockSpec((ONE, tile), cut), whole(tq, d), whole(tp, d), ANY),
        scratch_shapes=[pltpu.VMEM((tq, d), F32), pltpu.VMEM((tp, d), F32), pltpu.SemaphoreType.DMA((GATHER_SEMS,))],
        compiler_params=pltpu.CompilerParams(collective_id=collective_id, has_side_effects=True, vmem_limit_bytes=60 * 1024 * 1024),
        name="qkv_backward",
    )(dq, dp, x, w_t, dr1_q, dr1_p, ctx_q, ctx_p, dr1b_q, dr1b_p, piece)


def unpack_kernel(n1, n2, n3, a_ref, b_ref, c_ref, qkv_ref, out_ref, up_ref, down_ref):
    j = pl.program_id(ZERO)

    def join(ref, src, lo, hi):
        @pl.when((j >= lo) & (j < hi))
        def _():
            for c in range(src.shape[ZERO]):
                ref[:, c * WIDTH:(c + ONE) * WIDTH] = src[c]
    join(down_ref, a_ref, ZERO, n1)
    join(up_ref, b_ref, n1, n2)
    join(qkv_ref, c_ref, n2, n3)
    join(out_ref, c_ref, n3, pl.num_programs(ZERO))


def unpack(a, b, c, three, d, tile=TILE):
    ff = a.shape[ONE]
    n1, n2, n3, n4 = ff // tile, 2 * ff // tile, (2 * ff + three * d) // tile, (2 * ff + (three + ONE) * d) // tile
    part = lambda lo, hi: (lambda j: jnp.clip(j - lo, ZERO, hi - lo - ONE))
    ja, jb, jc, jq, jo = part(ZERO, n1), part(n1, n2), part(n2, n4), part(n2, n3), part(n3, n4)
    return pl.pallas_call(
        functools.partial(unpack_kernel, n1, n2, n3), grid=(n4,),
        out_shape=(sds((three * d, d), F32), sds((d, d), F32), sds((d, ff), F32), sds((ff, d), F32)),
        in_specs=[pl.BlockSpec((d // WIDTH, tile, WIDTH), lambda j: (ZERO, ja(j), ZERO)),
                  pl.BlockSpec((tile // WIDTH, d, WIDTH), lambda j: (jb(j), ZERO, ZERO)),
                  pl.BlockSpec((d // WIDTH, tile, WIDTH), lambda j: (ZERO, jc(j), ZERO))],
        out_specs=(pl.BlockSpec((tile, d), lambda j: (jq(j), ZERO)), pl.BlockSpec((tile, d), lambda j: (jo(j), ZERO)),
                   pl.BlockSpec((d, tile), lambda j: (ZERO, jb(j))), pl.BlockSpec((tile, d), lambda j: (ja(j), ZERO))),
        compiler_params=vmem(), name="unpack",
    )(a, b, c)


def solution(mesh):
    axis = mesh.axis_names[ZERO]
    n_dev = mesh.shape[axis]

    def local_step(q_hidden, q_mask, p_hidden, p_mask, w_qkv, b_qkv, w_out, b_out, ln1_gain, ln1_shift,
                   w_up, b_up, w_down, b_down, ln2_gain, ln2_shift):
        nq, q_len, d = q_hidden.shape
        n_pass, p_len = nq * p_hidden.shape[ONE], p_hidden.shape[2]
        _, three, heads, head = w_qkv.shape
        tq = nq * q_len
        x = jnp.concatenate([q_hidden.reshape(-ONE, d), p_hidden.reshape(-ONE, d)], axis=ZERO)
        p_mask = p_mask.reshape(n_pass, p_len)
        wqkv_t = w_qkv.transpose(ONE, 2, 3, ZERO).reshape(-ONE, d)
        wo = w_out.reshape(-ONE, d)
        none = jnp.zeros_like(b_out)
        vecs = jnp.stack([b_out, ln1_gain, ln1_shift, b_down, ln2_gain, ln2_shift, none, none])

        def pool_weights(mask):
            m = mask.astype(F32)
            return (m / row_sum(m)).reshape(-ONE, ONE)

        weights = jnp.concatenate([pool_weights(q_mask), pool_weights(p_mask)], axis=ZERO)
        bounds = tuple((i, i * q_len, q_len) for i in range(nq)) + tuple(
            (2 * nq + i, tq + i * p_len, p_len) for i in range(n_pass))

        qkv_q, qkv_p = qkv_project(x, wqkv_t, b_qkv.reshape(ONE, -ONE), tq)
        probs_q, ctx_q = attention(qkv_q, q_mask, head)
        probs_p, ctx_p = attention(qkv_p, p_mask, head)
        h, r1_q, r1_p, g, gp, r2, pooled = ffn_forward(
            x, ctx_q, ctx_p, wo, vecs, weights, w_up, b_up.reshape(ONE, -ONE), w_down, bounds)

        used = (jnp.arange(pooled.shape[ZERO]) < nq) | (jnp.arange(pooled.shape[ZERO]) >= 2 * nq)
        embed = pooled * jnp.where(used[:, None], lax.rsqrt(row_sum(pooled * pooled)), 0.0)
        everyone = gather_embeddings(embed, axis, ONE)
        mean_loss, d_pooled = loss_and_grad(everyone, pooled, axis, nq * n_dev)

        dwd, dr2, dr2b, dvec2 = down_backward(d_pooled, r2, weights, vecs, g, bounds)
        dwu, dbu, dn_q, dn_p, piece_a, _ = up_backward(axis, dr2, dr2b, h, gp, w_down, w_up, dwd.reshape(-ONE, WIDTH), tq, 2)
        dq, dr1_q, dr1b_q, dvec_q = attention_bwd(dn_q, r1_q, vecs, wo, qkv_q, probs_q, head)
        dp, dr1_p, dr1b_p, dvec_p, piece_b, _ = attention_bwd(
            dn_p, r1_p, vecs, wo, qkv_p, probs_p, head, axis, dwu.reshape(-ONE, WIDTH), 3)
        dwa, dbq, dh_q, dh_p, a = qkv_backward(
            axis, dq, dp, x, wqkv_t, dr1_q, dr1_p, ctx_q, ctx_p, dr1b_q, dr1b_p, piece_a, 4)
        small = jnp.concatenate([(dvec_q + dvec_p)[:3], dvec2[:3], jnp.zeros((2, d), F32), dbq.reshape(three, d), dbu.reshape(-ONE, d),
                                 jnp.zeros((ONE, d), F32)], axis=ZERO)
        b, c, small = finish_sum(axis, UNITS_B, UNITS_C, piece_b, dwa.reshape(-ONE, WIDTH), small, 5)
        d_qkv, d_out, d_up, d_down = unpack(a.reshape(dwd.shape), b.reshape(dwu.shape), c.reshape(dwa.shape), three, d)
        vec = [small[i] for i in range(6)]
        return (mean_loss, dh_q.reshape(q_hidden.shape), dh_p.reshape(p_hidden.shape),
                d_qkv.reshape(three, heads, head, d).transpose(3, ZERO, ONE, 2), small[8:8 + three].reshape(b_qkv.shape),
                d_out.reshape(w_out.shape), vec[ZERO], vec[ONE], vec[2], d_up, small[8 + three:-ONE].reshape(-ONE),
                d_down, vec[3], vec[4], vec[5])

    in_specs = (P(axis),) * 4 + (P(),) * 12
    out_specs = (P(), P(axis), P(axis)) + (P(),) * 12
    return jax.shard_map(local_step, mesh=mesh, in_specs=in_specs, out_specs=out_specs, check_vma=False)
```

time: 572 us -> 589 us (1.030)
  Pallas kernels: 541 us -> 559 us
    pallas_call x6 -> x7, Pallas kernels: 360 us -> 377 us  [the longest x1 132 us: finish_sum(): pl.pallas_call(functools.partial(finish_kernel, axis, units_b, units_c),...]
where the time goes in v2:
time: 589 us; the launch traced here: 584 us
  Pallas kernels  559 us (95%)
  local copies, waits for them, and re-layouts  12.6 us (2%)
  other arithmetic  11.2 us (2%)
    pallas_call x1, Pallas kernels, finish_sum(): pl.pallas_call(functools.partial(finish_kernel, axis, units_b, units_c),...  132 us
    pallas_call x1, Pallas kernels, up_backward(): pl.pallas_call(functools.partial(up_bwd_kernel, axis), grid=(f // tile,),...  65.8 us
    pallas_call x1, Pallas kernels, qkv_backward(): pl.pallas_call(functools.partial(qkv_bwd_kernel, axis, n), grid=(n + m,),...  64.2 us
    pallas_call x1, Pallas kernels, attention_bwd(): pl.pallas_call(functools.partial(attn_bwd_host, scale, head, axis), grid=...  62.2 us
    pallas_call x1, Pallas kernels, ffn_forward(): pl.pallas_call(functools.partial(ffn_kernel, bounds), grid=(f // tile,),...  60.1 us
    pallas_call x1, Pallas kernels, unpack(): pl.pallas_call(functools.partial(unpack_kernel, n1, n2, n3), grid=(n4,),...  42.4 us
    pallas_call x1, Pallas kernels, gather_embeddings(): pl.pallas_call(functools.partial(gather_kernel, axis), out_shape=jax.Shap...  35.2 us
    pallas_call x1, Pallas kernels, loss_and_grad(): pl.pallas_call(functools.partial(loss_kernel, axis, n_query), out_shape=(...  27.4 us

profile of v2, /device:TPU:1, one launch (start us, length us, event | category | flops | bytes accessed | tf_op | source)
XLA Modules:
  0.0 584.1 jit_solution(6864075105664868377)
XLA Ops:
  0.6 0.8 convert_reduce_fusion
  2.3 0.8 convert_reduce_fusion.1
  4.0 1.4 reshape.146.b_ref
  5.4 1.4 stack.27.vec_ref.refs_2_
  6.8 1.1 copy.34.wt_ref
  7.9 3.3 pad_maximum_fusion.x_ref
  11.3 12.3 %qkv_project.1 = (bf16[192,3072]{1,0:T(8,128)(2,1)}, bf16[1024,3072]{1,0:T(8,128)(2,1)}) custom-call(bf16[1216,1024]{1,0:T(8,128)(2,1)} %pad_maximum_fusion.x_ref, bf16[3072,1024]{1,0:T(8,128)(2,1)} %bitcast.43, f32[1,3072]{1,0:T(1,128)} %reshape.146.b_ref), custom_call_target="tpu_custom_call" | custom-call | tf_op jit(solution)/shard_map/qkv_project/pallas_call | solution.py:578
  23.6 5.2 attention.2
  28.8 11.7 %attention.3 = (bf16[8,8,256,128]{3,2,1,0:T(8,128)(2,1)}, bf16[1024,1024]{1,0:T(8,128)(2,1)}) custom-call(bf16[1024,3072]{1,0:T(8,128)(2,1)} %get-tuple-element.62.qkv_ref, s32[8,1,128]{2,1,0:T(1,128)} %bitcast.58), custom_call_target="tpu_custom_call" | custom-call | tf_op jit(solution)/shard_map/attention/pallas_call | solution.py:619
  40.5 60.1 %ffn_forward.1 = (bf16[1216,1024]{1,0:T(8,128)(2,1)}, f32[192,1024]{1,0:T(8,128)}, f32[1024,1024]{1,0:T(8,128)}, bf16[1216,4096]{1,0:T(8,128)(2,1)}, f32[1216,40...) custom-call(bf16[1216,1024]{1,0:T(8,128)(2,1)} %pad_maximum_fusion.x_ref, ...), custom_call_target="tpu_custom_call" | custom-call | tf_op jit(solution)/shard_map/ffn_forward/pallas_call | solution.py:696
  100.6 1.0 multiply_reduce_fusion
  101.6 0.9 broadcast_multiply_fusion.e_ref
  102.5 35.2 %gather_embeddings.1 = f32[4,4,4,24,1024]{4,3,2,1,0:T(8,128)S(1)} custom-call(f32[16,1024]{1,0:T(8,128)S(1)} %broadcast_multiply_fusion.e_ref), custom_call_target="tpu_custom_call" | custom-call | tf_op jit(solution)/shard_map/gather_embeddings/pallas_call | solution.py:441
  137.8 2.7 copy-done
  140.5 27.4 %loss_and_grad.1 = (f32[8,128]{1,0:T(8,128)S(1)}, f32[16,1024]{1,0:T(8,128)S(1)}) custom-call(f32[64,24,1024]{2,1,0:T(8,128)} %bitcast.42, f32[16,1024]{1,0:T(8,128)S(1)} %copy-done.1), custom_call_target="tpu_custom_call" | custom-call | tf_op jit(solution)/shard_map/loss_and_grad/pallas_call | solution.py:514
  169.0 25.6 %down_backward.1 = (f32[4,4096,256]{2,1,0:T(8,128)}, f32[1216,1024]{1,0:T(8,128)}, bf16[1216,1024]{1,0:T(8,128)(2,1)}, f32[8,1024]{1,0:T(8,128)}) custom-call(f32[16,1024]{1,0:T(8,128)} %copy-done.3, f32[1216,1024]{1,0:T(8,128)} %get-tuple-element.67.r2_ref, f32[1216,1]{1,0:T(8,128)} %copy.34.wt_ref, f32[8,1024]{1,0:T(8,128)} %stack.27.vec_ref.refs_2_, ...), custom_call_target="tpu_custom_call" | custom-call | tf_op jit(solution)/shard_map/down_backward/pallas_call | solution.py:736
  194.6 65.8 %up_backward.1 = (f32[16,1024,256]{2,1,0:T(8,128)}, f32[1,4096]{1,0:T(1,128)}, f32[192,1024]{1,0:T(8,128)}, f32[1024,1024]{1,0:T(8,128)}, f32[128,256]{1,0:T(8,128)}, /*index=5*/f32[8192,256]{1,0:T(8,128)}) custom-call(f32[1216,1024]{1,0:T(8,128)} %get-tuple-element.69.dr2_ref, bf16[1216,1024]{1,0:T(8,128)(2,1)} %get-tuple-element.70.dr2b_ref, ...), custom_call_target="tpu_custom_call" | custom-call | tf_op jit(solution)/shard_map/up_backward/pallas_call | solution.py:784
  260.4 15.5 %attention_bwd.1 = (bf16[192,3072]{1,0:T(8,128)(2,1)}, f32[192,1024]{1,0:T(8,128)}, bf16[192,1024]{1,0:T(8,128)(2,1)}, f32[8,1024]{1,0:T(8,128)}) custom-call(f32[192,1024]{1,0:T(8,128)} %get-tuple-element.74.refs_0_, f32[192,1024]{1,0:T(8,128)} %get-tuple-element.75.refs_1_, f32[8,1024]{1,0:T(8,128)} %stack.27.vec_ref.refs_2_, bf16[1024,1024]{1,0:T(8,128)(2,1)} %bitcast.46, ...), custom_call_target="tpu_custom_call" | custom-call | tf_op jit(solution)/shard_map/attention_bwd/pallas_call | solution.py:860
  275.9 62.2 %attention_bwd_host.1 = (bf16[1024,3072]{1,0:T(8,128)(2,1)}, f32[1024,1024]{1,0:T(8,128)}, bf16[1024,1024]{1,0:T(8,128)(2,1)}, f32[8,1024]{1,0:T(8,128)}, f32[128,256]{1,0:T(8,128)}, /*index=5*/f32[8192,256]{1,0:T(8,128)}) custom-call(f32[1024,1024]{1,0:T(8,128)} %get-tuple-element.78.dn_ref, f32[1024,1024]{1,0:T(8,128)} %get-tuple-element.79.r1_ref, ...), custom_call_target="tpu_custom_call" | custom-call | tf_op jit(solution)/shard_map/attention_bwd_host/pallas_call | solution.py:864
  340.1 64.2 %qkv_backward.1 = (f32[4,4096,256]{2,1,0:T(8,128)}, f32[1,3072]{1,0:T(1,128)}, bf16[192,1024]{1,0:T(8,128)(2,1)}, bf16[1024,1024]{1,0:T(8,128)(2,1)}, f32[16384,256]{1,0:T(8,128)}) custom-call(bf16[192,3072]{1,0:T(8,128)(2,1)} %get-tuple-element.77.dq_ref, bf16[1024,3072]{1,0:T(8,128)(2,1)} %get-tuple-element.82.dp_ref, ...), custom_call_target="tpu_custom_call" | custom-call | tf_op jit(solution)/shard_map/qkv_backward/pallas_call | solution.py:915
  404.3 1.4 reduce.7
  405.8 131.8 %finish_sum.1 = (f32[16384,256]{1,0:T(8,128)}, f32[16384,256]{1,0:T(8,128)}, f32[16,1024]{1,0:T(8,128)S(1)}, f32[8192,256]{1,0:T(8,128)}, f32[128,256]{1,0:T(8,128)}) custom-call(f32[128,256]{1,0:T(8,128)S(1)} %copy-done.2, f32[16384,256]{1,0:T(8,128)} %bitcast.51, f32[16,1024]{1,0:T(8,128)S(1)} %concatenate.11.small_ref), custom_call_target="tpu_custom_call" | custom-call | tf_op jit(solution)/shard_map/finish_sum/pallas_call | solution.py:369
  537.6 42.4 %unpack.1 = (f32[3072,1024]{1,0:T(8,128)}, f32[1024,1024]{1,0:T(8,128)}, f32[1024,4096]{1,0:T(8,128)}, f32[4096,1024]{1,0:T(8,128)}) custom-call(f32[4,4096,256]{2,1,0:T(8,128)} %bitcast.48, f32[16,1024,256]{2,1,0:T(8,128)} %bitcast.49, f32[4,4096,256]{2,1,0:T(8,128)} %bitcast.50), custom_call_target="tpu_custom_call" | custom-call | tf_op jit(solution)/shard_map/unpack/pallas_call | solution.py:948
  582.6 1.3 copy.42
  (41 shorter events, 7.7 us)
Async XLA Ops:
  100.6 39.9 %copy-start.1 = (f32[16,1024]{1,0:T(8,128)S(1)}, f32[16,1024]{1,0:T(8,128)}, u32[]{:S(2)}) copy-start(f32[16,1024]{1,0:T(8,128)} %get-tuple-element.64.pooled_ref) | copy-start | bytes 196612
  137.7 2.7 copy-start
  167.9 0.6 copy-start.3
  275.9 62.2 %copy-start.7 = (f32[8,1024]{1,0:T(8,128)S(1)}, f32[8,1024]{1,0:T(8,128)}, u32[]{:S(2)}) copy-start(f32[8,1024]{1,0:T(8,128)} %get-tuple-element.93) | copy-start | bytes 98308
  275.9 63.5 %copy-start.6 = (f32[1,4096]{1,0:T(1,128)S(1)}, f32[1,4096]{1,0:T(1,128)}, u32[]{:S(2)}) copy-start(f32[1,4096]{1,0:T(1,128)} %get-tuple-element.97) | copy-start | bytes 49156
  275.9 64.2 %copy-start.8 = (f32[8,1024]{1,0:T(8,128)S(1)}, f32[8,1024]{1,0:T(8,128)}, u32[]{:S(2)}) copy-start(f32[8,1024]{1,0:T(8,128)} %get-tuple-element.95) | copy-start | bytes 98308
  340.1 65.7 %copy-start.2 = (f32[128,256]{1,0:T(8,128)S(1)}, f32[128,256]{1,0:T(8,128)}, u32[]{:S(2)}) copy-start(f32[128,256]{1,0:T(8,128)} %get-tuple-element.91.pieceb_ref) | copy-start | bytes 393220
  537.6 44.3 %copy-start.5 = (bf16[192,1024]{1,0:T(8,128)(2,1)S(1)}, bf16[192,1024]{1,0:T(8,128)(2,1)}, u32[]{:S(2)}) copy-start(bf16[192,1024]{1,0:T(8,128)(2,1)} %get-tuple-element.88) | copy-start | bytes 1179652
  537.6 45.1 %copy-start.4 = (bf16[1024,1024]{1,0:T(8,128)(2,1)S(1)}, bf16[1024,1024]{1,0:T(8,128)(2,1)}, u32[]{:S(2)}) copy-start(bf16[1024,1024]{1,0:T(8,128)(2,1)} %get-tuple-element.89) | copy-start | bytes 6291460

commit v3 on v2

v3 whole, which is shorter than its diff:
```python
import functools
import types
import jax
import jax.numpy as jnp
from jax import lax
from jax.experimental import pallas as pl
from jax.experimental.pallas import tpu as pltpu
from jax.sharding import PartitionSpec as P

ZERO, ONE, TWO, THREE, ALL = 0, 1, 2, 3, ...

F32 = jnp.float32
BF16 = jnp.bfloat16
LOGICAL = pl.DeviceIdType.LOGICAL
RING = 4
WIDTH = 256
COLOURS = range(6)
AXES = range(THREE)
RINGS = range(RING)
TURNS = range(RING * RING)
ANY = pl.BlockSpec(memory_space=pl.ANY)


def mesh_place(axis):
    me = lax.axis_index(axis)
    core = lax.rem(me, TWO)
    chip = lax.div(me, TWO)
    row = lax.div(chip, RING)
    return (lax.rem(chip, RING), lax.rem(row, RING), lax.div(row, RING)), core


def device_at(coords, core):
    return ((coords[TWO] * RING + coords[ONE]) * RING + coords[ZERO]) * TWO + core


def moved(coords, dim, by):
    out = list(coords)
    out[dim] = lax.rem(coords[dim] + by + TWO * RING, RING)
    return tuple(out)


def wrap(i):
    return lax.rem(i + 4 * RING, RING)


def rdma(src, dst, send, recv, to):
    pltpu.make_async_remote_copy(src_ref=src, dst_ref=dst, send_sem=send, recv_sem=recv,
                                 device_id=to, device_id_type=LOGICAL).start()


def copy(src, dst, sem):
    pltpu.make_async_copy(src, dst, sem).start()


def drain(ref, sem):
    pltpu.make_async_copy(ref, ref, sem).wait()


def carve(sems, *counts):
    out, at = [], ZERO
    for n in counts:
        out.append(lambda i, at=at: sems.at[at + i])
        at += n
    return out


def ring_plan(axis, units):
    coords, core = mesh_place(axis)
    p = types.SimpleNamespace(coords=coords, core=core, partner=device_at(coords, ONE - core))
    p.dims = [tuple((k // TWO + s) % THREE for s in AXES) for k in COLOURS]
    p.sign = [ONE - TWO * (k % TWO) for k in COLOURS]
    p.pos = [tuple(coords[d] for d in p.dims[k]) for k in COLOURS]
    p.nxt = [tuple(device_at(moved(coords, d, p.sign[k]), core) for d in p.dims[k]) for k in COLOURS]
    p.piece = [8 * u for u in units]
    p.lead = [sum(p.piece[:k]) for k in COLOURS]
    p.all = sum(p.piece)
    p.half = 64 * p.all
    p.base = core * p.half
    p.peers = [p.partner] + [device_at(moved(coords, d, by), core) for d in AXES for by in (ONE, TWO, THREE)]
    p.to = lambda k, s, step: device_at(moved(coords, p.dims[k][s], -p.sign[k] * (ONE + step)), core)
    return p


def rows(at, n):
    return pl.ds(pl.multiple_of(at, 8), n)


def chunk_row(p, k, step):
    return 64 * p.lead[k] + wrap(p.pos[k][ZERO] - p.sign[k] * (ONE + step)) * (16 * p.piece[k])


def sub_row(p, k, row, step):
    return row + wrap(p.pos[k][ONE] - p.sign[k] * (ONE + step)) * (4 * p.piece[k])


def piece_row(p, k, row, step):
    return row + wrap(p.pos[k][TWO] - p.sign[k] * (ONE + step)) * p.piece[k]


def signal_peers(peers):
    barrier = pltpu.get_barrier_semaphore()
    for peer in peers:
        pl.semaphore_signal(barrier, inc=ONE, device_id=peer, device_id_type=LOGICAL)


def await_peers(peers):
    pl.semaphore_wait(pltpu.get_barrier_semaphore(), len(peers))


SCATTER_SEMS = 4 + THREE * 16 + TWO * 12 + 4 * THREE


def scatter_scratch(units):
    n = 8 * sum(units)
    vm = lambda *s: pltpu.VMEM(s + (WIDTH,), F32)
    return [vm(64 * n), vm(TWO, 4 * n), vm(THREE, RING, 4 * n), vm(THREE, 4 * n), vm(THREE, n), pltpu.SemaphoreType.DMA((SCATTER_SEMS,))]


def scatter_rounds(p, src, part, out, acc, stage, land1, land2, land3, sems):
    load_sem, swap_send, swap_recv, stage_sem, p1_send, p1_recv, p2_send, p2_recv, p3_send, p3_recv = carve(
        sems, 4, 16, 16, 16, 12, 12, THREE, THREE, THREE, THREE)
    n_sub, n_chunk = 4 * p.all, 16 * p.all
    far = p.half - p.base

    def turn_row(k, n):
        return sub_row(p, k, chunk_row(p, k, n // RING), n % RING)

    def load(t):
        for k in COLOURS:
            r, m = chunk_row(p, k, t), 16 * p.piece[k]
            copy(src.at[rows(p.base + r, m)], acc.at[rows(r, m)], load_sem(t))

    def swap(n):
        for k in COLOURS:
            r, m = turn_row(k, n), 4 * p.piece[k]
            rdma(src.at[rows(far + r, m)], part.at[rows(r, m)], swap_send(n), swap_recv(n), p.partner)

    def fetch(n):
        drain(part.at[pl.ds(ZERO, n_sub)], swap_recv(n))
        for k in COLOURS:
            m = 4 * p.piece[k]
            copy(part.at[rows(turn_row(k, n), m)], stage.at[n % TWO, pl.ds(4 * p.lead[k], m)], stage_sem(n))

    def begin():
        for t in RINGS:
            load(t)
        for n in range(6):
            swap(n)

    def turn(n):
        t, i = n // RING, n % RING
        if n == ZERO:
            fetch(n)
        if n + 6 < 16:
            swap(n + 6)
        if n + ONE < 16:
            fetch(n + ONE)
        if i == ZERO:
            drain(acc.at[pl.ds(ZERO, n_chunk)], load_sem(t))
        drain(stage.at[n % TWO], stage_sem(n))
        if t > ZERO:
            drain(land1.at[t - ONE, i], p1_recv(n - 4))
        for k in COLOURS:
            at, m = rows(turn_row(k, n), 4 * p.piece[k]), pl.ds(4 * p.lead[k], 4 * p.piece[k])
            val = acc[at] + stage[n % TWO, m]
            acc[at] = val + land1[t - ONE, i, m] if t > ZERO else val
        if t < THREE:
            for k in COLOURS:
                at, m = rows(turn_row(k, n), 4 * p.piece[k]), pl.ds(4 * p.lead[k], 4 * p.piece[k])
                rdma(acc.at[at], land1.at[t, i, m], p1_send(n), p1_recv(n), p.nxt[k][ZERO])

    def second(i):
        for k in COLOURS:
            at, m = rows(turn_row(k, 12 + i), 4 * p.piece[k]), pl.ds(4 * p.lead[k], 4 * p.piece[k])
            rdma(acc.at[at], land2.at[i, m], p2_send(i), p2_recv(i), p.to(k, ONE, i))

    def third():
        for i in AXES:
            drain(land2.at[i], p2_recv(i))
        for k in COLOURS:
            at, m = rows(turn_row(k, 15), 4 * p.piece[k]), pl.ds(4 * p.lead[k], 4 * p.piece[k])
            acc[at] += land2[ZERO, m] + land2[ONE, m] + land2[TWO, m]
        for g in AXES:
            for k in COLOURS:
                at, m = rows(piece_row(p, k, turn_row(k, 15), g), p.piece[k]), pl.ds(p.lead[k], p.piece[k])
                rdma(acc.at[at], land3.at[g, m], p3_send(g), p3_recv(g), p.to(k, TWO, g))

    def last():
        for g in AXES:
            drain(land3.at[g], p3_recv(g))
        for k in COLOURS:
            at, m = rows(piece_row(p, k, turn_row(k, 15), THREE), p.piece[k]), pl.ds(p.lead[k], p.piece[k])
            out[m] = acc[at] + (land3[ZERO, m] + land3[ONE, m] + land3[TWO, m])

    def finish():
        for n in TURNS:
            drain(acc.at[pl.ds(ZERO, n_sub)], swap_send(n))
        for n in range(12):
            drain(acc.at[pl.ds(ZERO, n_sub)], p1_send(n))
        for t in AXES:
            drain(acc.at[pl.ds(ZERO, n_sub)], p2_send(t))
            drain(acc.at[pl.ds(ZERO, p.all)], p3_send(t))

    act = functools.partial
    def both(*fs):
        def run():
            for f in fs:
                f()
        return run
    steps = [begin] + [act(turn, n) for n in range(12)]
    steps += [both(act(turn, 12 + i), act(second, i)) for i in AXES] + [act(turn, 15), third, last, finish]
    return steps


GATHER_SEMS = ONE + TWO * (THREE + THREE + 12 + 16)


def gather_rounds(p, piece, out, sems):
    own_sem, a3_send, a3_recv, a2_send, a2_recv, a1_send, a1_recv, push_send, push_recv = carve(
        sems, ONE, THREE, THREE, THREE, THREE, 12, 12, 16, 16)
    n_sub = 4 * p.all

    def many(n):
        return out.at[pl.ds(ZERO, n)]

    def mine(k, c, s, g):
        return p.base + piece_row(p, k, sub_row(p, k, chunk_row(p, k, c - ONE), s - ONE), g - ONE)

    def sub_at(k, c, s):
        return rows(p.base + sub_row(p, k, chunk_row(p, k, c - ONE), s - ONE), 4 * p.piece[k])

    def third():
        for k in COLOURS:
            src, at = piece.at[pl.ds(p.lead[k], p.piece[k])], out.at[rows(mine(k, ZERO, ZERO, ZERO), p.piece[k])]
            copy(src, at, own_sem(ZERO))
            for t in AXES:
                rdma(src, at, a3_send(t), a3_recv(t), p.to(k, TWO, t))

    def hop1(c, s):
        for k in COLOURS:
            if c < THREE:
                rdma(out.at[sub_at(k, c, s)], out.at[sub_at(k, c, s)], a1_send(RING * c + s), a1_recv(RING * c + s), p.nxt[k][ZERO])
            rdma(out.at[sub_at(k, c, s)], out.at[sub_at(k, c, s)], push_send(RING * c + s), push_recv(RING * c + s), p.partner)

    def second(s):
        if s == ZERO:
            drain(many(p.all), own_sem(ZERO))
            for t in AXES:
                drain(many(p.all), a3_recv(t))
            for t in AXES:
                for k in COLOURS:
                    rdma(out.at[sub_at(k, ZERO, ZERO)], out.at[sub_at(k, ZERO, ZERO)], a2_send(t), a2_recv(t), p.to(k, ONE, t))
        else:
            drain(many(n_sub), a2_recv(THREE - s))
        hop1(ZERO, s)

    def first(c, s):
        drain(many(n_sub), a1_recv(RING * (c - ONE) + s))
        hop1(c, s)

    def finish():
        for t in AXES:
            drain(many(p.all), a3_send(t))
            drain(many(n_sub), a2_send(t))
        for n in range(12):
            drain(many(n_sub), a1_send(n))
        for n in TURNS:
            drain(many(n_sub), push_send(n))
            drain(many(n_sub), push_recv(n))

    act = functools.partial
    return ([third] + [act(second, s) for s in RINGS]
            + [act(first, c, s) for c in (ONE, TWO, THREE) for s in RINGS] + [finish])


def small_scratch(shape):
    return [pltpu.VMEM((4, THREE) + shape, F32), pltpu.SemaphoreType.DMA((8,))]


def small_rounds(p, src, out, land, sems):
    places = [(None, p.core, TWO)] + [(d, p.coords[d], RING) for d in AXES]

    def send(n):
        d, _, size = places[n]
        for by in range(ONE, size):
            to = p.partner if d is None else device_at(moved(p.coords, d, by), p.core)
            rdma(out, land.at[n, by - ONE], sems.at[n], sems.at[4 + n], to)

    def step(n):
        if n == ZERO:
            out[ALL] = src[ALL]
        else:
            _, place, size = places[n - ONE]
            got = land.at[n - ONE, pl.ds(ZERO, size - ONE)]
            drain(got, sems.at[4 + n - ONE])
            drain(got, sems.at[n - ONE])
            mine, total = out[ALL], None
            for q in range(size):
                val = mine
                for by in range(ONE, size):
                    val = jnp.where(lax.rem(place - q + size, size) == by, land[n - ONE, by - ONE], val)
                total = val if total is None else total + val
            out[ALL] = total
        if n < 4:
            send(n)

    return [functools.partial(step, n) for n in range(5)]


def spread(steps, slots):
    plan = [[] for _ in range(slots)]
    for i, s in enumerate(steps):
        plan[i * slots // len(steps)].append(s)
    return plan


def finish_kernel(axis, units_b, units_c, pieceb_ref, c_ref, vec1_ref, vec2_ref, bq_ref, bu_ref, bc_out, small_out, part,
                  small_ref, piecec, *scratch):
    sc, (gather_sem, gather_sem2, small_land, small_sem) = scratch[:6], scratch[6:]
    pb, pc = ring_plan(axis, units_b), ring_plan(axis, units_c)
    n_b, n_c = TWO * pb.half, TWO * pc.half
    b_out, c_out = bc_out.at[pl.ds(ZERO, n_b)], bc_out.at[pl.ds(n_b, n_c)]
    signal_peers(pb.peers)
    width = small_ref.shape[ONE]
    small_ref[ALL] = jnp.zeros_like(small_ref)
    small_ref[ZERO:THREE, :] = vec1_ref[ZERO:THREE, :]
    small_ref[THREE:6, :] = vec2_ref[ZERO:THREE, :]
    at = 8
    for ref in (bq_ref, bu_ref):
        for i in range(ref.shape[ONE] // width):
            small_ref[at:at + ONE, :] = ref[:, i * width:(i + ONE) * width]
            at += ONE
    await_peers(pb.peers)
    reduce_c = scatter_rounds(pc, c_ref, part, piecec, *sc)
    gather_b = gather_rounds(pb, pieceb_ref, b_out, gather_sem)
    gather_c = gather_rounds(pc, piecec, c_out, gather_sem2)
    smalls = small_rounds(pb, small_ref, small_out, small_land, small_sem)
    main = reduce_c[:-ONE] + gather_c[:-ONE]
    fill = spread(gather_b[:-ONE], len(main) - 4)
    for i, f in enumerate(main):
        f()
        if i % THREE == ONE and i // THREE < len(smalls):
            smalls[i // THREE]()
        for f in fill[i] if i < len(fill) else ():
            f()
    for rounds in (reduce_c, gather_b, gather_c):
        rounds[-ONE]()


def finish_sum(axis, units_b, units_c, piece_b, c, vec1, vec2, bq, bu, collective_id):
    sds = jax.ShapeDtypeStruct
    dma = pltpu.SemaphoreType.DMA
    vm = pl.BlockSpec(memory_space=pltpu.VMEM)
    n = c.shape[ZERO]
    small = (16, vec1.shape[ONE])
    outs = pl.pallas_call(
        functools.partial(finish_kernel, axis, units_b, units_c),
        out_shape=(pltpu.VMEM((piece_b.shape[ZERO] * 128 + n, WIDTH), F32), sds(small, F32), sds((n // TWO, WIDTH), F32)),
        in_specs=[vm, ANY, vm, vm, vm, vm], out_specs=(vm, vm, ANY),
        scratch_shapes=[pltpu.VMEM(small, F32), pltpu.VMEM((n // 128, WIDTH), F32)] + scatter_scratch(units_c)
        + [dma((GATHER_SEMS,)), dma((GATHER_SEMS,))] + small_scratch(small),
        compiler_params=pltpu.CompilerParams(collective_id=collective_id, has_side_effects=True, vmem_limit_bytes=22 * 1024 * 1024),
        name="finish_sum",
    )(piece_b, c, vec1, vec2, bq, bu)
    return outs[:TWO]


def gather_kernel(axis, pooled_ref, g_ref, e_ref, mine, theirs, swap_sem, sems_send, sems_recv, push_send, push_recv):
    coords, core = mesh_place(axis)
    partner = device_at(coords, ONE - core)
    width = e_ref.shape[ONE]
    lanes = pl.ds(pl.multiple_of(core * (width // TWO), 128), width // TWO)
    x, y, z = coords
    peers = [partner] + [device_at(moved(coords, d, by), core) for d in AXES for by in (ONE, TWO, THREE)]
    signal_peers(peers)
    size = row_sum(pooled_ref[ALL] * pooled_ref[ALL])
    e_ref[ALL] = pooled_ref[ALL] * jnp.where(size > 0.0, lax.rsqrt(size), 0.0)
    mine[ALL] = e_ref[ALL]
    await_peers(peers)

    rdma(e_ref, theirs, swap_sem.at[ZERO], swap_sem.at[ONE], partner)
    drain(theirs, swap_sem.at[ONE])
    first = jnp.where(core == ZERO, mine[:, lanes], theirs[:, lanes])
    second = jnp.where(core == ZERO, theirs[:, lanes], mine[:, lanes])
    g_ref[z, y, x, ZERO:4, lanes] = first[ZERO:4]
    g_ref[z, y, x, 4:8, lanes] = second[ZERO:4]
    g_ref[z, y, x, 8:16, lanes] = first[8:16]
    g_ref[z, y, x, 16:24, lanes] = second[8:16]
    drain(e_ref, swap_sem.at[ZERO])

    def view(a, stage):
        idx = [z, y, x]
        for s in range(stage):
            idx[TWO - (a + s) % THREE] = slice(None)
        return g_ref.at[idx[ZERO], idx[ONE], idx[TWO], pl.ds(8 * a, 8), lanes]

    for stage in range(THREE):
        for by in (ONE, THREE, TWO):
            for a in range(THREE):
                to = device_at(moved(coords, (a + stage) % THREE, by), core)
                rdma(view(a, stage), view(a, stage), sems_send.at[stage, by - ONE], sems_recv.at[stage, by - ONE], to)
        if stage == TWO:
            for a in range(THREE):
                rdma(view(a, TWO), view(a, TWO), push_send.at[ZERO], push_recv.at[ZERO], partner)
        for by in (ONE, THREE, TWO):
            n = 4 ** stage
            shape_like = g_ref.at[ZERO, ZERO, ZERO, :, lanes] if stage == ZERO else (
                g_ref.at[ZERO, ZERO, :, :, lanes] if stage == ONE else g_ref.at[ZERO, :, :, :, lanes])
            drain(shape_like, sems_recv.at[stage, by - ONE])
            if stage == TWO:
                for a in range(THREE):
                    far = moved(coords, (a + TWO) % THREE, RING - by)
                    idx = [far[TWO], far[ONE], far[ZERO]]
                    idx[TWO - a] = slice(None)
                    idx[TWO - (a + ONE) % THREE] = slice(None)
                    v = g_ref.at[idx[ZERO], idx[ONE], idx[TWO], pl.ds(8 * a, 8), lanes]
                    rdma(v, v, push_send.at[by], push_recv.at[by], partner)
    for stage in range(THREE):
        shape_like = g_ref.at[ZERO, ZERO, ZERO, :, lanes] if stage == ZERO else (
            g_ref.at[ZERO, ZERO, :, :, lanes] if stage == ONE else g_ref.at[ZERO, :, :, :, lanes])
        for by in (ONE, TWO, THREE):
            drain(shape_like, sems_send.at[stage, by - ONE])
    for by in range(4):
        drain(g_ref.at[ZERO, :, :, :, lanes], push_send.at[by])
        drain(g_ref.at[ZERO, :, :, :, lanes], push_recv.at[by])


def gather_embeddings(e, axis, collective_id):
    dma = pltpu.SemaphoreType.DMA
    width = e.shape[ONE]
    g = pl.pallas_call(
        functools.partial(gather_kernel, axis),
        out_shape=jax.ShapeDtypeStruct((RING, RING, RING, 24, width), F32),
        in_specs=[pl.BlockSpec(memory_space=pltpu.VMEM)],
        out_specs=pl.BlockSpec(memory_space=pltpu.VMEM),
        scratch_shapes=[pltpu.VMEM(e.shape, F32)] * THREE + [dma((TWO,)),
                        dma((THREE, THREE)), dma((THREE, THREE)), dma((4,)), dma((4,))],
        compiler_params=pltpu.CompilerParams(collective_id=collective_id, has_side_effects=True,
                                             vmem_limit_bytes=16 * 1024 * 1024),
        name="gather_embeddings",
    )(e)
    return g.reshape(RING ** THREE, 24, width)


def split3(x):
    hi = x.astype(BF16)
    rest = x - hi.astype(F32)
    mid = rest.astype(BF16)
    return hi, mid, (rest - mid.astype(F32)).astype(BF16)


def dot6(a, b, dims):
    low = mm(a[TWO], b[ZERO], dims) + mm(a[ZERO], b[TWO], dims) + mm(a[ONE], b[ONE], dims)
    return mm(a[ZERO], b[ZERO], dims) + (mm(a[ZERO], b[ONE], dims) + mm(a[ONE], b[ZERO], dims) + low)


def loss_kernel(axis, n_query, g_ref, pooled_ref, loss_ref, d_ref, logit_ref, lse_ref, q_ref, p_ref, dp_ref):
    me = lax.axis_index(axis)
    core, chip = lax.rem(me, TWO), lax.div(me, TWO)
    chips, _, width = g_ref.shape
    nq = chips * 8
    lanes = 128
    gs = 100.0 / n_query
    for i, part in enumerate(split3(g_ref[:, ZERO:8, :].reshape(nq, width))):
        q_ref[i] = part
    block = TWO * lanes

    def logits(b, _):
        at = pl.multiple_of(b * block, block)
        p = split3(g_ref[pl.ds(b * (block // 16), block // 16), 8:24, :].reshape(block, width))
        for i, part in enumerate(p):
            p_ref[i, pl.ds(at, block), :] = part
        logit_ref[:, pl.ds(at, block)] = dot6((q_ref[ZERO], q_ref[ONE], q_ref[TWO]), p, NT) * 100.0
        return ZERO

    lax.fori_loop(ZERO, chips * 16 // block, logits, ZERO)

    def rows_of(b, loss):
        at = pl.ds(pl.multiple_of(b * lanes, lanes), lanes)
        s = logit_ref[at, :]
        top = jnp.max(s, axis=ONE, keepdims=True)
        lse = jnp.log(row_sum(jnp.exp(s - top))) + top
        lse_ref[at, :] = jnp.broadcast_to(lse, (lanes, lanes))
        row = lax.broadcasted_iota(jnp.int32, s.shape, ZERO) + b * lanes
        col = lax.broadcasted_iota(jnp.int32, s.shape, ONE)
        return loss + col_sum(lse - row_sum(jnp.where(col == TWO * row, s, 0.0)))

    loss = lax.fori_loop(ZERO, nq // lanes, rows_of, jnp.zeros((ONE, ONE), F32))
    loss_ref[ALL] = jnp.broadcast_to(loss * (1.0 / n_query), loss_ref.shape)

    def weights(s, lse, row, col):
        row = lax.broadcasted_iota(jnp.int32, s.shape, ZERO) + row
        col = lax.broadcasted_iota(jnp.int32, s.shape, ONE) + col
        return jnp.exp(s - lse) * gs - jnp.where(col == TWO * row, gs, 0.0)

    at = pl.ds(pl.multiple_of(chip * 8, 8), 8)
    w = jnp.concatenate([x.astype(F32) for x in split3(weights(logit_ref[at, :], lse_ref[at, ZERO:ONE], chip * 8, ZERO))], axis=ZERO).astype(BF16)
    by_hi, by_mid, by_low = (mm(w, p_ref[i]) for i in range(THREE))
    dq = by_hi[ZERO:8] + (by_hi[8:16] + by_mid[ZERO:8] + (by_hi[16:24] + by_mid[8:16] + by_low[ZERO:8]))

    first = pl.multiple_of(lax.div(chip, 8) * lanes, lanes)
    w = weights(logit_ref[:, pl.ds(first, lanes)], lse_ref[ALL], ZERO, first)
    dp_ref[ALL] = dot6(split3(w.T), (q_ref[ZERO], q_ref[ONE], q_ref[TWO]), NN)
    dp = dp_ref[pl.ds(pl.multiple_of(lax.rem(chip, 8) * 16 + core * 8, 8), 8), :]

    def back(d, pooled):
        inv = lax.rsqrt(row_sum(pooled * pooled))
        e = pooled * inv
        return (d - e * row_sum(e * d)) * inv

    d_ref[ALL] = jnp.zeros_like(d_ref)
    d_ref[ZERO:4, :] = back(jnp.where(core == ZERO, dq[ZERO:4], dq[4:8]), pooled_ref[ZERO:4])
    d_ref[8:16, :] = back(dp, pooled_ref[8:16])


def loss_and_grad(g, pooled, axis, n_query):
    chips, _, width = g.shape
    nq, n_pass, lanes = chips * 8, chips * 16, 128
    vm = pl.BlockSpec(memory_space=pltpu.VMEM)
    loss, d = pl.pallas_call(
        functools.partial(loss_kernel, axis, n_query),
        out_shape=(jax.ShapeDtypeStruct((8, lanes), F32), jax.ShapeDtypeStruct(pooled.shape, F32)),
        in_specs=[vm] * TWO, out_specs=(vm,) * TWO,
        scratch_shapes=[pltpu.VMEM((nq, n_pass), F32), pltpu.VMEM((nq, lanes), F32), pltpu.VMEM((THREE, nq, width), BF16),
                        pltpu.VMEM((THREE, n_pass, width), BF16), pltpu.VMEM((lanes, width), F32)],
        compiler_params=vmem(28), name="loss_and_grad",
    )(g, pooled)
    return loss[ZERO, ZERO], d


NN = (((ONE,), (ZERO,)), ((), ()))
NT = (((ONE,), (ONE,)), ((), ()))
TN = (((ZERO,), (ZERO,)), ((), ()))
LN_EPS = 1e-12
NEG_FILL = -1e9
TILE = 512
UNITS_A, UNITS_B, UNITS_C = (THREE, THREE, THREE, THREE, TWO, TWO), (THREE, THREE, THREE, THREE, 4, 4), (TWO,) * 6
sds = jax.ShapeDtypeStruct


def mm(a, b, dims=NN):
    return lax.dot_general(a, b, dims, preferred_element_type=F32)


def vmem(mb=60):
    return pltpu.CompilerParams(vmem_limit_bytes=mb * 1024 * 1024)


def whole(*shape):
    return pl.BlockSpec(shape, lambda j: (ZERO,) * len(shape), pipeline_mode=pl.Buffered(ONE))


def across(rows, tile):
    return pl.BlockSpec((rows, tile), lambda j: (ZERO, j))


def down(tile, cols):
    return pl.BlockSpec((tile, cols), lambda j: (j, ZERO))


def row_mean(x):
    return jnp.mean(x, axis=ONE, keepdims=True)


def row_sum(x):
    return jnp.sum(x, axis=ONE, keepdims=True)


def col_sum(x):
    return jnp.sum(x, axis=ZERO, keepdims=True)


def qkv_kernel(xq_ref, xp_ref, w_ref, b_ref, oq_ref, op_ref):
    for x_ref, o_ref in ((xq_ref, oq_ref), (xp_ref, op_ref)):
        o_ref[ALL] = (mm(x_ref[ALL], w_ref[ALL], NT) + b_ref[ALL]).astype(BF16)


def qkv_project(xq, xp, w_t, b, tile=TILE):
    tq, d = xq.shape
    tp, f = xp.shape[ZERO], w_t.shape[ZERO]
    return pl.pallas_call(
        qkv_kernel, grid=(f // tile,),
        out_shape=(sds((tq, f), BF16), sds((tp, f), BF16)),
        in_specs=[whole(tq, d), whole(tp, d), down(tile, d), across(ONE, tile)],
        out_specs=(across(tq, tile), across(tp, tile)),
        compiler_params=vmem(), name="qkv_project",
    )(xq, xp, w_t, b)


def split_heads(pair, head):
    lane = lax.broadcasted_iota(jnp.int32, pair.shape, ONE)
    zero = jnp.zeros_like(pair)
    return jnp.concatenate([jnp.where(lane < head, pair, zero), jnp.where(lane >= head, pair, zero)], axis=ZERO)


def join_heads(stacked, head):
    t = stacked.shape[ZERO] // TWO
    lane = lax.broadcasted_iota(jnp.int32, (t, stacked.shape[ONE]), ONE)
    return jnp.where(lane < head, stacked[:t], stacked[t:])


def attn_kernel(scale, head, qkv_ref, mask_ref, probs_ref, ctx_ref):
    d = ctx_ref.shape[ONE]
    pair = TWO * head
    keep = mask_ref[ZERO] > ZERO
    for g in range(d // pair):
        at = pl.ds(g * pair, pair)
        q = split_heads(qkv_ref[:, at], head)
        k = qkv_ref[:, pl.ds(d + g * pair, pair)]
        v = qkv_ref[:, pl.ds(TWO * d + g * pair, pair)]
        s = jnp.where(keep, mm(q, k, NT) * scale, NEG_FILL)
        e = jnp.exp(s - jnp.max(s, axis=ONE, keepdims=True))
        p = (e / row_sum(e)).astype(BF16)
        probs_ref[ZERO, g] = p
        ctx_ref[:, at] = join_heads(mm(p, v), head).astype(BF16)


def attention(qkv, mask, head):
    n, seq = mask.shape
    d = qkv.shape[ONE] // THREE
    pairs = d // (TWO * head)
    return pl.pallas_call(
        functools.partial(attn_kernel, head ** -0.5, head), grid=(n,),
        out_shape=(sds((n, pairs, TWO * seq, seq), BF16), sds((n * seq, d), BF16)),
        in_specs=[down(seq, THREE * d), pl.BlockSpec((ONE, ONE, seq), lambda j: (j, ZERO, ZERO))],
        out_specs=(pl.BlockSpec((ONE, pairs, TWO * seq, seq), lambda j: (j, ZERO, ZERO, ZERO)), down(seq, d)),
        compiler_params=vmem(), name="attention",
    )(qkv, mask.reshape(n, ONE, seq))


def norm_rows(x):
    c = x - row_mean(x)
    r = lax.rsqrt(row_mean(c * c) + LN_EPS)
    return c * r, r


def norm_back(g, hat, r):
    return r * (g - row_mean(g) - hat * row_mean(g * hat))


ERFC = (0.07122347, -0.27794802, 0.29668747, -0.02018065, 0.21581222, 0.21731356, 0.24887118, 0.24822095)


def gelu_parts(u):
    bell = jnp.exp2(u * u * -0.7213475204)
    t = 1.0 / (1.0 + 0.311126984 * jnp.abs(u))
    poly = 0.5 * ERFC[ZERO]
    for c in ERFC[ONE:]:
        poly = poly * t + 0.5 * c
    tail = bell * (poly * t)
    return jnp.where(u >= 0.0, 1.0 - tail, tail), u * bell * 0.3989422804


def sequences(mq_ref, mp_ref):
    lo, out = ZERO, []
    for first, ref in ((ZERO, mq_ref), (8, mp_ref)):
        n, seq = ref.shape
        for i in range(n):
            size = row_sum(ref[i:i + ONE, :].astype(F32))
            token = lax.broadcasted_iota(jnp.int32, (seq, ONE), ZERO).astype(F32)
            out.append((first + i, pl.ds(lo, seq), jnp.where(token < size, 1.0 / size, 0.0)))
            lo += seq
    return out


def row_blocks(n, size=256):
    size = min(n, size)
    return [pl.ds(a, size) for a in range(ZERO, n, size)]


ROWS = 304


def ffn_kernel(xq_ref, xp_ref, cq_ref, cp_ref, wo_ref, vec_ref, mq_ref, mp_ref, wu_ref, bu_ref, wd_ref,
               h_ref, r1q_ref, r1p_ref, g_ref, gp_ref, r2_ref, pool_ref):
    j = pl.program_id(ZERO)
    t, tq = h_ref.shape[ZERO], cq_ref.shape[ZERO]
    b_out, g1, s1, b_down, g2, s2 = (vec_ref[i:i + ONE, :] for i in range(6))

    @pl.when(j == ZERO)
    def _():
        for x_ref, c_ref, r_ref, lo in ((xq_ref, cq_ref, r1q_ref, ZERO), (xp_ref, cp_ref, r1p_ref, tq)):
            for at in row_blocks(c_ref.shape[ZERO]):
                r1 = x_ref[at, :].astype(F32) + mm(c_ref[at, :], wo_ref[ALL]) + b_out
                r_ref[at, :] = r1
                h = (norm_rows(r1)[ZERO] * g1 + s1).astype(BF16)
                to = pl.ds(lo + at.start, at.size)
                h_ref[to, :] = h
                r2_ref[to, :] = h.astype(F32) + b_down

    for a in range(ZERO, t, ROWS):
        at = pl.ds(a, ROWS)
        u = mm(h_ref[at, :], wu_ref[ALL]) + bu_ref[ALL]
        cdf, upd = gelu_parts(u)
        g = (u * cdf).astype(BF16)
        g_ref[at, :] = g
        gp_ref[at, :] = cdf + upd
        r2_ref[at, :] += mm(g, wd_ref[ALL])

    @pl.when(j == pl.num_programs(ZERO) - ONE)
    def _():
        pool_ref[ALL] = jnp.zeros_like(pool_ref)
        for row, at, weight in sequences(mq_ref, mp_ref):
            y = norm_rows(r2_ref[at, :])[ZERO] * g2 + s2
            pool_ref[row:row + ONE, :] = col_sum(y * weight)


def ffn_forward(xq, xp, ctx_q, ctx_p, w_out, vecs, mask_q, mask_p, w_up, b_up, w_down, tile=TILE):
    tq, d = xq.shape
    tp, f = xp.shape[ZERO], w_up.shape[ONE]
    t = tq + tp
    return pl.pallas_call(
        ffn_kernel, grid=(f // tile,),
        out_shape=(sds((t, d), BF16), sds((tq, d), F32), sds((tp, d), F32), sds((t, f), BF16), sds((t, f), F32),
                   sds((t, d), F32), sds((16, d), F32)),
        in_specs=[whole(tq, d), whole(tp, d), whole(tq, d), whole(tp, d), whole(d, d), whole(*vecs.shape),
                  whole(*mask_q.shape), whole(*mask_p.shape), across(d, tile), across(ONE, tile), down(tile, d)],
        out_specs=(whole(t, d), whole(tq, d), whole(tp, d), across(t, tile), across(t, tile), whole(t, d), whole(16, d)),
        compiler_params=vmem(), name="ffn_forward",
    )(xq, xp, ctx_q, ctx_p, w_out, vecs, mask_q, mask_p, w_up, b_up, w_down)


def store_blocks(ref, val):
    for c in range(ref.shape[ZERO]):
        ref[c] = val[:, c * WIDTH:(c + ONE) * WIDTH]


def down_bwd_kernel(dpool_ref, r2_ref, mq_ref, mp_ref, vec_ref, g_ref, dwd_ref, dr2_ref, dr2b_ref, dvec_ref):
    @pl.when(pl.program_id(ZERO) == ZERO)
    def _():
        dvec_ref[ALL] = jnp.zeros_like(dvec_ref)
        for row, at, weight in sequences(mq_ref, mp_ref):
            hat, r = norm_rows(r2_ref[at, :])
            dy = weight * dpool_ref[row:row + ONE, :]
            dr2 = norm_back(dy * vec_ref[4:5, :], hat, r)
            dr2_ref[at, :] = dr2
            dr2b_ref[at, :] = dr2.astype(BF16)
            dvec_ref[ZERO:ONE, :] += col_sum(dr2)
            dvec_ref[ONE:TWO, :] += col_sum(dy * hat)
            dvec_ref[TWO:THREE, :] += col_sum(dy)

    store_blocks(dwd_ref, mm(g_ref[ALL], dr2b_ref[ALL], TN))


def down_backward(dpool, r2, mask_q, mask_p, vecs, g, tile=TILE):
    t, d = r2.shape
    f = g.shape[ONE]
    n = d // WIDTH
    return pl.pallas_call(
        down_bwd_kernel, grid=(f // tile,),
        out_shape=(sds((n, f, WIDTH), F32), sds((t, d), F32), sds((t, d), BF16), sds((8, d), F32)),
        in_specs=[whole(*dpool.shape), whole(t, d), whole(*mask_q.shape), whole(*mask_p.shape), whole(*vecs.shape), across(t, tile)],
        out_specs=(pl.BlockSpec((n, tile, WIDTH), lambda j: (ZERO, j, ZERO)), whole(t, d), whole(t, d), whole(8, d)),
        compiler_params=vmem(), name="down_backward",
    )(dpool, r2, mask_q, mask_p, vecs, g)


PACE_UP = (5.5, 2.3, 14.0, 6.0)
PACE_B = (5.5, 2.8, 9.0, 5.0)
PACE_A = (8.0, 3.3, 0.0, 0.0)
def place(timed, slot_times):
    plan = [[] for _ in slot_times]
    for t, f in sorted(timed, key=lambda x: x[ZERO]):
        plan[min([i for i, at in enumerate(slot_times) if at >= t], default=-ONE)].append(f)
    return plan


def timeline(steps, start, pace, before_third, before_last):
    n = len(steps)
    times = [0.0] + [start + pace * i for i in range(n - TWO)] + [1e3]
    if before_last:
        times[-THREE] = times[-4] + before_third
        times[-TWO] = times[-THREE] + before_last
    return list(zip(times, steps))


def run_slot(plan, j, per, point):
    for s in range(len(plan) // per):
        todo = plan[s * per + point]
        if todo:
            @pl.when(j == s)
            def _():
                for f in todo:
                    f()


def host(collective_id, mb):
    return pltpu.CompilerParams(collective_id=collective_id, has_side_effects=True, vmem_limit_bytes=mb * 1024 * 1024)


def up_bwd_kernel(axis, steps, dr2_hbm, dr2b_ref, h_ref, gp_ref, wd_ref, wu_ref, r1q_ref, r1p_ref, vec_ref, cq_ref, cp_ref, a_ref,
                  dw_ref, dbu_ref, dr1q_ref, dr1p_ref, lowq_ref, lowp_ref, dvec_ref, piece_ref, part_ref, ht_ref, sem, *scratch):
    j = pl.program_id(ZERO)
    tq = dr1q_ref.shape[ZERO]
    tp = dr1p_ref.shape[ZERO]
    p = ring_plan(axis, UNITS_A)
    pace = 5.6
    timed = timeline(scatter_rounds(p, a_ref, part_ref, piece_ref, *scratch), *PACE_UP)
    points = THREE
    plan = place(timed, [pace * (s // points) + pace * (s % points) / points for s in range(points * (steps + TWO))])
    parts = ((dr1q_ref, dr2_hbm.at[pl.ds(ZERO, tq)]), (dr1p_ref, dr2_hbm.at[pl.ds(tq, tp)]))

    @pl.when(j == ZERO)
    def _():
        signal_peers(p.peers)
        for ref, src in parts:
            copy(src, ref, sem.at[ZERO])
        ht_ref[ALL] = h_ref[ALL].T
        for ref, src in parts:
            drain(ref, sem.at[ZERO])
        await_peers(p.peers)

    run_slot(plan, j, points, ZERO)

    @pl.when(j < steps)
    def _():
        dg = mm(dr2b_ref[ALL], wd_ref[ALL], NT).astype(BF16).astype(F32)
        dpre = dg * gp_ref[ALL]
        dbu_ref[ALL] = col_sum(dpre)
        dpre = dpre.astype(BF16)
        run_slot(plan, j, points, ONE)
        store_blocks(dw_ref, mm(ht_ref[ALL], dpre))
        run_slot(plan, j, points, TWO)
        dr1q_ref[ALL] += mm(dpre[:tq], wu_ref[ALL], NT)
        dr1p_ref[ALL] += mm(dpre[tq:], wu_ref[ALL], NT)

    @pl.when(j == steps)
    def _():
        dvec_ref[ALL] = jnp.zeros_like(dvec_ref)
        for d_ref, r_ref, low_ref in ((dr1q_ref, r1q_ref, lowq_ref), (dr1p_ref, r1p_ref, lowp_ref)):
            for at in row_blocks(d_ref.shape[ZERO]):
                dy = d_ref[at, :].astype(BF16).astype(F32)
                hat, r = norm_rows(r_ref[at, :])
                dr1 = norm_back(dy * vec_ref[ONE:TWO, :], hat, r)
                d_ref[at, :] = dr1
                low_ref[at, :] = dr1.astype(BF16)
                dvec_ref[ZERO:ONE, :] += col_sum(dr1)
                dvec_ref[ONE:TWO, :] += col_sum(dy * hat)
                dvec_ref[TWO:THREE, :] += col_sum(dy)

    @pl.when(j >= steps)
    def _():
        half = dr1q_ref.shape[ONE] // TWO
        at = pl.ds(pl.multiple_of(jnp.maximum(j - steps, ZERO) * half, half), half)
        run_slot(plan, j, points, ONE)
        store_blocks(dw_ref, mm(cq_ref[ALL], lowq_ref[:, at], TN) + mm(cp_ref[ALL], lowp_ref[:, at], TN))
        run_slot(plan, j, points, TWO)


def up_backward(axis, dr2, dr2b, h, gp, w_down, w_up, r1_q, r1_p, vecs, ctx_q, ctx_p, part_a, collective_id, tile=TILE):
    t, d = h.shape
    f = w_up.shape[ONE]
    tq, tp = r1_q.shape[ZERO], r1_p.shape[ZERO]
    n, total, steps = tile // WIDTH, part_a.shape[ZERO], f // tile
    cut = lambda j: jnp.minimum(j, steps - ONE)
    wide = lambda rows: pl.BlockSpec((rows, tile), lambda j: (ZERO, cut(j)))
    return pl.pallas_call(
        functools.partial(up_bwd_kernel, axis, steps), grid=(steps + TWO,),
        out_shape=(sds(((f + d) // WIDTH, d, WIDTH), F32), sds((ONE, f), F32), sds((tq, d), F32), sds((tp, d), F32),
                   sds((tq, d), BF16), sds((tp, d), BF16), sds((8, d), F32),
                   sds((total // 128, WIDTH), F32), sds((total // TWO, WIDTH), F32)),
        in_specs=[ANY, whole(t, d), whole(t, d), wide(t), pl.BlockSpec((tile, d), lambda j: (cut(j), ZERO)), wide(d),
                  whole(tq, d), whole(tp, d), whole(*vecs.shape), whole(tq, d), whole(tp, d), ANY],
        out_specs=(pl.BlockSpec((n, d, WIDTH), lambda j: (j, ZERO, ZERO)), wide(ONE), whole(tq, d), whole(tp, d), whole(tq, d), whole(tp, d),
                   whole(8, d), whole(total // 128, WIDTH), ANY),
        scratch_shapes=[pltpu.VMEM((d, t), BF16), pltpu.SemaphoreType.DMA((ONE,))] + scatter_scratch(UNITS_A),
        compiler_params=host(collective_id, 63), name="up_backward",
    )(dr2, dr2b, h, gp, w_down, w_up, r1_q, r1_p, vecs, ctx_q, ctx_p, part_a)


def attn_bwd_body(scale, head, low_ref, wo_ref, qkv_ref, probs_ref, out_ref, pause):
    d = low_ref.shape[ONE]
    pair = TWO * head
    dctx = mm(low_ref[ALL], wo_ref[ALL], NT).astype(BF16)
    for g in range(d // pair):
        if g == d // (TWO * pair):
            pause(ONE)
        at = pl.ds(g * pair, pair)
        q = split_heads(qkv_ref[:, at], head)
        k = qkv_ref[:, pl.ds(d + g * pair, pair)]
        v = qkv_ref[:, pl.ds(TWO * d + g * pair, pair)]
        p = probs_ref[ZERO, g]
        dc = split_heads(dctx[:, g * pair:(g + ONE) * pair], head)
        dp = mm(dc, v, NT)
        pf = p.astype(F32)
        ds = (pf * (dp - row_sum(dp * pf)) * scale).astype(BF16)
        out_ref[:, at] = join_heads(mm(ds, k), head).astype(BF16)
        out_ref[:, pl.ds(d + g * pair, pair)] = mm(ds, q, TN).astype(BF16)
        out_ref[:, pl.ds(TWO * d + g * pair, pair)] = mm(p, dc, TN).astype(BF16)


def attn_qkv_kernel(axis, scale, head, nq, n_pass, lowq_ref, lowp_ref, wo_ref, qkvq_ref, qkvp_ref, probq_ref, probp_ref,
                    xq_ref, xp_ref, w_ref, dr1q_hbm, dr1p_hbm, b_ref, piecea_ref,
                    dw_ref, db_ref, dhq_ref, dhp_ref, pieceb_ref, part_ref, a_ref, dq_ref, dp_ref, accq_ref, accp_ref, sem, gsem, *scratch):
    j = pl.program_id(ZERO)
    first, last = nq + n_pass, pl.num_programs(ZERO) - ONE
    tile = w_ref.shape[ZERO]
    per = dq_ref.shape[TWO] // tile
    pa, pb = ring_plan(axis, UNITS_A), ring_plan(axis, UNITS_B)
    points = TWO
    steps = [3.2] * nq + [3.3] * n_pass + [4.3] * per
    slots = [sum(steps[:i]) + steps[i] * h / points for i in range(len(steps)) for h in range(points)]
    timed = timeline(scatter_rounds(pb, b_ref, part_ref, pieceb_ref, *scratch), *PACE_B)
    timed += timeline(gather_rounds(pa, piecea_ref, a_ref, gsem), *PACE_A)
    plan = place(timed, slots)
    pause = functools.partial(run_slot, plan, j, points)
    loads = ((dr1q_hbm, accq_ref), (dr1p_hbm, accp_ref))

    @pl.when(j == ZERO)
    def _():
        signal_peers(pa.peers)
        for src, dst in loads:
            copy(src, dst, sem.at[ZERO])
        await_peers(pa.peers)
    pause(ZERO)

    @pl.when(j < nq)
    def _():
        attn_bwd_body(scale, head, lowq_ref, wo_ref, qkvq_ref, probq_ref, dq_ref.at[jnp.minimum(j, nq - ONE)], pause)

    @pl.when((j >= nq) & (j < first))
    def _():
        attn_bwd_body(scale, head, lowp_ref, wo_ref, qkvp_ref, probp_ref, dp_ref.at[jnp.clip(j - nq, ZERO, n_pass - ONE)], pause)

    @pl.when(j == first - ONE)
    def _():
        for src, dst in loads:
            drain(dst, sem.at[ZERO])

    @pl.when(j >= first)
    def _():
        at = pl.ds(pl.multiple_of(jnp.maximum(j - first, ZERO) * tile, tile), tile)
        dq = dq_ref[:, :, at].reshape(-ONE, tile)
        dp = dp_ref[:, :, at].reshape(-ONE, tile)
        store_blocks(dw_ref, mm(dq, xq_ref[ALL], TN) + mm(dp, xp_ref[ALL], TN))
        db_ref[ALL] = col_sum(dq.astype(F32)) + col_sum(dp.astype(F32))
        pause(ONE)
        accq_ref[ALL] += mm(dq, w_ref[ALL])
        accp_ref[ALL] += mm(dp, w_ref[ALL])

    @pl.when(j == last)
    def _():
        dhq_ref[ALL] = accq_ref[ALL].astype(BF16)
        dhp_ref[ALL] = accp_ref[ALL].astype(BF16)


def attn_qkv_backward(axis, low_q, low_p, w_out, qkv_q, qkv_p, probs_q, probs_p, xq, xp, w_t, dr1_q, dr1_p, part_b, piece_a, head,
                      collective_id, tile=TILE):
    f, d = w_t.shape
    nq, pairs, _, lq = probs_q.shape
    n_pass, _, _, lp = probs_p.shape
    tq, tp = nq * lq, n_pass * lp
    per, cols, total = f // tile, d // WIDTH, part_b.shape[ZERO]
    jq = lambda j: jnp.minimum(j, nq - ONE)
    jp = lambda j: jnp.clip(j - nq, ZERO, n_pass - ONE)
    jt = lambda j: jnp.clip(j - nq - n_pass, ZERO, per - ONE)
    rows_of = lambda n, c, at: pl.BlockSpec((n, c), lambda j: (at(j), ZERO))
    probs_of = lambda n, at: pl.BlockSpec((ONE, pairs, TWO * n, n), lambda j: (at(j), ZERO, ZERO, ZERO))
    return pl.pallas_call(
        functools.partial(attn_qkv_kernel, axis, head ** -0.5, head, nq, n_pass), grid=(nq + n_pass + per,),
        out_shape=(sds((cols, f, WIDTH), F32), sds((ONE, f), F32), sds((tq, d), BF16), sds((tp, d), BF16),
                   sds((total // 128, WIDTH), F32), sds((total // TWO, WIDTH), F32), sds((piece_a.shape[ZERO] * 128, WIDTH), F32)),
        in_specs=[rows_of(lq, d, jq), rows_of(lp, d, jp), whole(d, d), rows_of(lq, f, jq), rows_of(lp, f, jp),
                  probs_of(lq, jq), probs_of(lp, jp), whole(tq, d), whole(tp, d), rows_of(tile, d, jt), ANY, ANY, ANY, whole(*piece_a.shape)],
        out_specs=(pl.BlockSpec((cols, tile, WIDTH), lambda j: (ZERO, jt(j), ZERO)), pl.BlockSpec((ONE, tile), lambda j: (ZERO, jt(j))),
                   whole(tq, d), whole(tp, d), whole(total // 128, WIDTH), ANY, ANY),
        scratch_shapes=[pltpu.VMEM((nq, lq, f), BF16), pltpu.VMEM((n_pass, lp, f), BF16), pltpu.VMEM((tq, d), F32),
                        pltpu.VMEM((tp, d), F32), pltpu.SemaphoreType.DMA((ONE,)), pltpu.SemaphoreType.DMA((GATHER_SEMS,))]
        + scatter_scratch(UNITS_B),
        compiler_params=host(collective_id, 63), name="attn_qkv_backward",
    )(low_q, low_p, w_out, qkv_q, qkv_p, probs_q, probs_p, xq, xp, w_t, dr1_q, dr1_p, part_b, piece_a)


def unpack_kernel(a_hbm, bc_ref, down_ref, up_ref, out_ref, qkv_ref, stage, sems, in_sem, out_sem):
    n_up = up_ref.shape[ONE] // WIDTH
    slots, _, rows_each, _ = stage.shape

    def cols(i):
        return pl.ds(i * WIDTH, WIDTH)

    def load(i):
        copy(a_hbm.at[:, pl.ds(i * rows_each, rows_each)], stage.at[i % slots], in_sem.at[i % slots])

    total = down_ref.shape[ZERO] // rows_each
    for i in range(slots):
        load(i)
    n, m, k = up_ref.shape[ZERO], qkv_ref.shape[ZERO], n_up + out_ref.shape[ONE] // WIDTH
    for i in range(k):
        copy(bc_ref.at[pl.ds(i * n, n)], up_ref.at[:, cols(i)] if i < n_up else out_ref.at[:, cols(i - n_up)], sems.at[ZERO])
    for i in range(qkv_ref.shape[ONE] // WIDTH):
        copy(bc_ref.at[pl.ds(k * n + i * m, m)], qkv_ref.at[:, cols(i)], sems.at[ZERO])
    for i in range(total):
        slot = i % slots
        drain(stage.at[slot], in_sem.at[slot])
        for k in range(stage.shape[ONE]):
            copy(stage.at[slot, k], down_ref.at[pl.ds(i * rows_each, rows_each), cols(k)], out_sem.at[slot])
        if i >= ONE and i - ONE + slots < total:
            drain(stage.at[(i - ONE) % slots], out_sem.at[(i - ONE) % slots])
            load(i - ONE + slots)
    for i in range(max(total - slots, ZERO), total):
        drain(stage.at[i % slots], out_sem.at[i % slots])
    drain(bc_ref, sems.at[ZERO])


def unpack(a, bc, d, f):
    ff = a.shape[ONE]
    vm = pl.BlockSpec(memory_space=pltpu.VMEM)
    slots = 4
    dma = pltpu.SemaphoreType.DMA
    return pl.pallas_call(
        unpack_kernel, out_shape=(sds((ff, d), F32), sds((d, ff), F32), sds((d, d), F32), sds((f, d), F32)),
        in_specs=[ANY, vm], out_specs=(ANY,) * 4,
        scratch_shapes=[pltpu.VMEM((slots, d // WIDTH, TILE, WIDTH), F32), dma((ONE,)), dma((slots,)), dma((slots,))],
        compiler_params=vmem(12), name="unpack",
    )(a, pltpu.with_memory_space_constraint(bc, pltpu.VMEM))


def solution(mesh):
    axis = mesh.axis_names[ZERO]
    n_dev = mesh.shape[axis]

    def local_step(q_hidden, q_mask, p_hidden, p_mask, w_qkv, b_qkv, w_out, b_out, ln1_gain, ln1_shift,
                   w_up, b_up, w_down, b_down, ln2_gain, ln2_shift):
        nq, _, d = q_hidden.shape
        n_pass, p_len = nq * p_hidden.shape[ONE], p_hidden.shape[TWO]
        _, three, heads, head = w_qkv.shape
        xq, xp = q_hidden.reshape(-ONE, d), p_hidden.reshape(-ONE, d)
        p_mask = p_mask.reshape(n_pass, p_len)
        wqkv_t = w_qkv.transpose(ONE, TWO, THREE, ZERO).reshape(-ONE, d)
        wo = w_out.reshape(-ONE, d)
        none = jnp.zeros_like(b_out)
        vecs = jnp.stack([b_out, ln1_gain, ln1_shift, b_down, ln2_gain, ln2_shift, none, none])

        qkv_q, qkv_p = qkv_project(xq, xp, wqkv_t, b_qkv.reshape(ONE, -ONE))
        probs_q, ctx_q = attention(qkv_q, q_mask, head)
        probs_p, ctx_p = attention(qkv_p, p_mask, head)
        h, r1_q, r1_p, g, gp, r2, pooled = ffn_forward(
            xq, xp, ctx_q, ctx_p, wo, vecs, q_mask, p_mask, w_up, b_up.reshape(ONE, -ONE), w_down)
        everyone = gather_embeddings(pooled, axis, ONE)
        mean_loss, d_pooled = loss_and_grad(everyone, pooled, axis, nq * n_dev)
        dwd, dr2, dr2b, dvec2 = down_backward(d_pooled, r2, q_mask, p_mask, vecs, g)
        dwb, dbu, dr1_q, dr1_p, low_q, low_p, dvec1, piece_a, _ = up_backward(
            axis, dr2, dr2b, h, gp, w_down, w_up, r1_q, r1_p, vecs, ctx_q, ctx_p, dwd.reshape(-ONE, WIDTH), TWO)
        dwq, dbq, dh_q, dh_p, piece_b, _, a = attn_qkv_backward(
            axis, low_q, low_p, wo, qkv_q, qkv_p, probs_q, probs_p, xq, xp, wqkv_t, dr1_q, dr1_p, dwb.reshape(-ONE, WIDTH), piece_a, head, THREE)
        bc, small = finish_sum(axis, UNITS_B, UNITS_C, piece_b, dwq.reshape(-ONE, WIDTH), dvec1, dvec2, dbq, dbu, 4)
        d_down, d_up, d_out, d_qkv = unpack(a.reshape(dwd.shape), bc, d, three * d)
        vec = [small[i] for i in range(6)]
        return (mean_loss, dh_q.reshape(q_hidden.shape), dh_p.reshape(p_hidden.shape),
                d_qkv.reshape(three, heads, head, d).transpose(THREE, ZERO, ONE, TWO), small[8:8 + three].reshape(b_qkv.shape),
                d_out.reshape(w_out.shape), vec[ZERO], vec[ONE], vec[TWO], d_up, small[8 + three:-ONE].reshape(-ONE),
                d_down, vec[THREE], vec[4], vec[5])

    in_specs = (P(axis),) * 4 + (P(),) * 12
    out_specs = (P(), P(axis), P(axis)) + (P(),) * 12
    return jax.shard_map(local_step, mesh=mesh, in_specs=in_specs, out_specs=out_specs, check_vma=False)
```

time: 589 us -> 473 us (0.80)
  Pallas kernels: 559 us -> 459 us
  other arithmetic: 11.2 us -> 0 us
    pallas_call x7 -> x5, Pallas kernels: 336 us -> 273 us  [the longest x1 92.3 us: attn_qkv_backward(): pl.pallas_call(functools.partial(attn_qkv_kernel, axis, head ** (-0.5), h...]
    pallas_call x1, Pallas kernels: 132 us -> 109 us  [finish_sum(): pl.pallas_call(functools.partial(finish_kernel, axis, units_b, units_c),...]
    pallas_call x1, Pallas kernels: 27.4 us -> 11.3 us  [loss_and_grad(): pl.pallas_call(functools.partial(loss_kernel, axis, n_query), out_shape=(...]
where the time goes in v3:
time: 473 us; the launch traced here: 469 us
  Pallas kernels  459 us (97%)
  local copies, waits for them, and re-layouts  8.82 us (2%)
    pallas_call x1, Pallas kernels, finish_sum(): pl.pallas_call(functools.partial(finish_kernel, axis, units_b, units_c),...  109 us
    pallas_call x1, Pallas kernels, attn_qkv_backward(): pl.pallas_call(functools.partial(attn_qkv_kernel, axis, head ** (-0.5), h...  92.3 us
    pallas_call x1, Pallas kernels, up_backward(): pl.pallas_call(functools.partial(up_bwd_kernel, axis, steps), grid=(steps...  74.9 us
    pallas_call x1, Pallas kernels, ffn_forward(): pl.pallas_call(ffn_kernel, grid=(f // tile,), out_shape=(sds((t, d), BF16...  58.1 us
    pallas_call x1, Pallas kernels, gather_embeddings(): pl.pallas_call(functools.partial(gather_kernel, axis), out_shape=jax.Shap...  35.2 us
    pallas_call x1, Pallas kernels, down_backward(): pl.pallas_call(down_bwd_kernel, grid=(f // tile,), out_shape=(sds((n, f,...  24.8 us
    pallas_call x1, Pallas kernels, unpack(): pl.pallas_call(unpack_kernel, out_shape=(sds((ff, d), F32), sds((d, ff),...  23.2 us
    pallas_call x2, Pallas kernels, attention(): pl.pallas_call(functools.partial(attn_kernel, head ** (-0.5), head), grid...  16.9 us

profile of v3, /device:TPU:1, one launch (start us, length us, event | category | flops | bytes accessed | tf_op | source)
XLA Modules:
  0.0 468.7 jit_solution(2860902605098956358)
XLA Ops:
  0.6 1.4 reshape.90.b_ref
  2.1 1.4 stack.31.vec_ref
  3.5 13.0 %qkv_project.1 = (bf16[192,3072]{1,0:T(8,128)(2,1)}, bf16[1024,3072]{1,0:T(8,128)(2,1)}) custom-call(bf16[192,1024]{1,0:T(8,128)(2,1)} %bitcast.51, bf16[1024,1024]{1,0:T(8,128)(2,1)} %bitcast.43, bf16[3072,1024]{1,0:T(8,128)(2,1)} %bitcast.40, f32[1,3072]{1,0:T(1,128)} %reshape.90.b_ref), custom_call_target="tpu_custom_call" | custom-call | tf_op jit(solution)/shard_map/qkv_project/pallas_call | solution.py:581
  16.4 5.2 %attention.2 = (bf16[4,8,96,48]{3,2,1,0:T(8,128)(2,1)}, bf16[192,1024]{1,0:T(8,128)(2,1)}) custom-call(bf16[192,3072]{1,0:T(8,128)(2,1)} %get-tuple-element.54.qkv_ref.qkvq_ref, s32[4,1,48]{2,1,0:T(1,128)} %bitcast.59), custom_call_target="tpu_custom_call" | custom-call | tf_op jit(solution)/shard_map/attention/pallas_call | solution.py:622
  21.6 11.7 %attention.3 = (bf16[8,8,256,128]{3,2,1,0:T(8,128)(2,1)}, bf16[1024,1024]{1,0:T(8,128)(2,1)}) custom-call(bf16[1024,3072]{1,0:T(8,128)(2,1)} %get-tuple-element.56.qkv_ref.qkvp_ref, s32[8,1,128]{2,1,0:T(1,128)} %bitcast.56), custom_call_target="tpu_custom_call" | custom-call | tf_op jit(solution)/shard_map/attention/pallas_call | solution.py:622
  33.3 58.1 %ffn_forward.1 = (bf16[1216,1024]{1,0:T(8,128)(2,1)}, f32[192,1024]{1,0:T(8,128)}, f32[1024,1024]{1,0:T(8,128)}, bf16[1216,4096]{1,0:T(8,128)(2,1)}, f32[1216,40...) custom-call(bf16[192,1024]{1,0:T(8,128)(2,1)} %bitcast.52, bf16[1024,1024]{1,0:T(8,128)(2,1)} %bitcast.44, ...), custom_call_target="tpu_custom_call" | custom-call | tf_op jit(solution)/shard_map/ffn_forward/pallas_call | solution.py:712
  91.4 0.8 copy-done
  92.3 35.2 %gather_embeddings.1 = f32[4,4,4,24,1024]{4,3,2,1,0:T(8,128)S(1)} custom-call(f32[16,1024]{1,0:T(8,128)S(1)} %copy-done), custom_call_target="tpu_custom_call" | custom-call | tf_op jit(solution)/shard_map/gather_embeddings/pallas_call | solution.py:431
  127.5 0.0 copy-done.1
  127.5 11.3 %loss_and_grad.1 = (f32[8,128]{1,0:T(8,128)S(1)}, f32[16,1024]{1,0:T(8,128)S(1)}) custom-call(f32[64,24,1024]{2,1,0:T(8,128)S(1)} %bitcast.39, f32[16,1024]{1,0:T(8,128)S(1)} %copy-done.1), custom_call_target="tpu_custom_call" | custom-call | tf_op jit(solution)/shard_map/loss_and_grad/pallas_call | solution.py:520
  138.8 0.6 copy-done.2
  139.5 0.5 slice.27
  140.0 24.8 %down_backward.1 = (f32[4,4096,256]{2,1,0:T(8,128)}, f32[1216,1024]{1,0:T(8,128)}, bf16[1216,1024]{1,0:T(8,128)(2,1)}, f32[8,1024]{1,0:T(8,128)}) custom-call(f32[16,1024]{1,0:T(8,128)} %copy-done.2, f32[1216,1024]{1,0:T(8,128)} %get-tuple-element.61.r2_ref, s32[4,48]{1,0:T(4,128)} %mq_ref.3, s32[8,128]{1,0:T(8,128)} %bitcast.58, f32[8,1024]{1,0:T(8,128)} %stack.31.vec_ref, ...), custom_call_target="tpu_custom_call" | custom-call | tf_op jit(solution)/shard_map/down_backward/pallas_call | solution.py:749
  164.8 74.9 %up_backward.1 = (f32[20,1024,256]{2,1,0:T(8,128)}, f32[1,4096]{1,0:T(1,128)}, f32[192,1024]{1,0:T(8,128)}, f32[1024,1024]{1,0:T(8,128)}, bf16[192,1024]{1,0:T(8...) custom-call(f32[1216,1024]{1,0:T(8,128)} %get-tuple-element.63.dr2_hbm, ...), custom_call_target="tpu_custom_call" | custom-call | tf_op jit(solution)/shard_map/up_backward/pallas_call | solution.py:857
  239.8 92.3 %attn_qkv_backward.1 = (f32[4,3072,256]{2,1,0:T(8,128)}, f32[1,3072]{1,0:T(1,128)}, bf16[192,1024]{1,0:T(8,128)(2,1)}, bf16[1024,1024]{1,0:T(8,128)(2,1)}, f32[1...) custom-call(bf16[192,1024]{1,0:T(8,128)(2,1)} %get-tuple-element.70.lowq_ref, ...), custom_call_target="tpu_custom_call" | custom-call | tf_op jit(solution)/shard_map/attn_qkv_backward/pallas_call | solution.py:959
  332.1 109.2 %finish_sum.1 = (f32[32768,256]{1,0:T(8,128)S(1)}, f32[16,1024]{1,0:T(8,128)}, f32[6144,256]{1,0:T(8,128)}) custom-call(f32[160,256]{1,0:T(8,128)} %get-tuple-element.81.pieceb_ref, f32[12288,256]{1,0:T(8,128)} %bitcast.48, f32[8,1024]{1,0:T(8,128)} %get-tuple-element.83.vec1_ref, f32[8,1024]{1,0:T(8,128)} %get-tuple-element.84.vec2_ref, ...), custom_call_target="tpu_custom_call" | custom-call | tf_op jit(solution)/shard_map/finish_sum/pallas_call | solution.py:356
  441.3 0.0 copy-start.5
  441.3 23.2 %unpack.1 = (f32[4096,1024]{1,0:T(8,128)}, f32[1024,4096]{1,0:T(8,128)}, f32[1024,1024]{1,0:T(8,128)}, f32[3072,1024]{1,0:T(8,128)}) custom-call(f32[4,4096,256]{2,1,0:T(8,128)} %bitcast.46, f32[32768,256]{1,0:T(8,128)S(1)} %get-tuple-element.87.bc_ref), custom_call_target="tpu_custom_call" | custom-call | tf_op jit(solution)/shard_map/unpack/pallas_call | solution.py:1010
  464.5 0.6 copy.33
  465.1 0.6 fusion
  465.8 0.7 reshape.103
  466.4 0.0 copy-done.4
  466.4 0.7 copy.36
  467.2 1.3 copy.37
  (10 shorter events, 0.0 us)
Async XLA Ops:
  91.4 0.8 copy-start
  92.3 35.2 %copy-start.1 = (f32[16,1024]{1,0:T(8,128)S(1)}, f32[16,1024]{1,0:T(8,128)}, u32[]{:S(2)}) copy-start(f32[16,1024]{1,0:T(8,128)} %get-tuple-element.58.pooled_ref) | copy-start | bytes 196612
  138.8 0.6 copy-start.2
  441.3 23.2 %copy-start.5 = (f32[16,1024]{1,0:T(8,128)S(1)}, f32[16,1024]{1,0:T(8,128)}, u32[]{:S(2)}) copy-start(f32[16,1024]{1,0:T(8,128)} %get-tuple-element.89) | copy-start | bytes 196612
  441.3 25.1 %copy-start.4 = (bf16[192,1024]{1,0:T(8,128)(2,1)S(1)}, bf16[192,1024]{1,0:T(8,128)(2,1)}, u32[]{:S(2)}) copy-start(bf16[192,1024]{1,0:T(8,128)(2,1)} %get-tuple-element.78) | copy-start | bytes 1179652
  441.3 25.9 %copy-start.3 = (bf16[1024,1024]{1,0:T(8,128)(2,1)S(1)}, bf16[1024,1024]{1,0:T(8,128)(2,1)}, u32[]{:S(2)}) copy-start(bf16[1024,1024]{1,0:T(8,128)(2,1)} %get-tuple-element.79) | copy-start | bytes 6291460

commit v4 on v3

--- a/solution.py
+++ b/solution.py
@@ -76,8 +76,9 @@
     p.all = sum(p.piece)
     p.half = 64 * p.all
     p.base = core * p.half
-    p.peers = [p.partner] + [device_at(moved(coords, d, by), core) for d in AXES for by in (ONE, TWO, THREE)]
-    p.to = lambda k, s, step: device_at(moved(coords, p.dims[k][s], -p.sign[k] * (ONE + step)), core)
+    p.peers = [p.partner] + [device_at(moved(coords, d, by), core) for d in AXES for by in (ONE, THREE)]
+    p.across = [device_at(moved(coords, d, TWO), core) for d in AXES]
+    p.prv = [tuple(device_at(moved(coords, d, -p.sign[k]), core) for d in p.dims[k]) for k in COLOURS]
     return p
 
 
@@ -85,16 +86,24 @@
     return pl.ds(pl.multiple_of(at, 8), n)
 
 
-def chunk_row(p, k, step):
-    return 64 * p.lead[k] + wrap(p.pos[k][ZERO] - p.sign[k] * (ONE + step)) * (16 * p.piece[k])
-
-
-def sub_row(p, k, row, step):
-    return row + wrap(p.pos[k][ONE] - p.sign[k] * (ONE + step)) * (4 * p.piece[k])
-
-
-def piece_row(p, k, row, step):
-    return row + wrap(p.pos[k][TWO] - p.sign[k] * (ONE + step)) * p.piece[k]
+def place_of(p, k, ring, back):
+    return wrap(p.pos[k][ring] - p.sign[k] * back)
+
+
+def chunk_row(p, k, back):
+    return 64 * p.lead[k] + place_of(p, k, ZERO, back) * (16 * p.piece[k])
+
+
+def sub_row(p, k, row, back):
+    return row + place_of(p, k, ONE, back) * (4 * p.piece[k])
+
+
+def piece_row(p, k, row, back):
+    return row + place_of(p, k, TWO, back) * p.piece[k]
+
+
+GIVE = (TWO, ONE, THREE, ZERO)
+TAKE = (ZERO, ONE, THREE, TWO)
 
 
 def signal_peers(peers):
@@ -123,11 +132,11 @@
     far = p.half - p.base
 
     def turn_row(k, n):
-        return sub_row(p, k, chunk_row(p, k, n // RING), n % RING)
+        return sub_row(p, k, chunk_row(p, k, n // RING + ONE), GIVE[n % RING])
 
     def load(t):
         for k in COLOURS:
-            r, m = chunk_row(p, k, t), 16 * p.piece[k]
+            r, m = chunk_row(p, k, t + ONE), 16 * p.piece[k]
             copy(src.at[rows(p.base + r, m)], acc.at[rows(r, m)], load_sem(t))
 
     def swap(n):
@@ -169,28 +178,44 @@
                 at, m = rows(turn_row(k, n), 4 * p.piece[k]), pl.ds(4 * p.lead[k], 4 * p.piece[k])
                 rdma(acc.at[at], land1.at[t, i, m], p1_send(n), p1_recv(n), p.nxt[k][ZERO])
 
+    def pass_on(i, where, land, send, recv, ring):
+        if i == TWO:
+            drain(land.at[ZERO], recv(ZERO))
+        for k in COLOURS:
+            at, m = where(k, i)
+            if i == TWO:
+                acc[at] += land[ZERO, m]
+        for k in COLOURS:
+            at, m = where(k, i)
+            rdma(acc.at[at], land.at[i, m], send(i), recv(i), (p.prv if i == ONE else p.nxt)[k][ring])
+
+    def sub_at(k, i):
+        return rows(turn_row(k, 12 + i), 4 * p.piece[k]), pl.ds(4 * p.lead[k], 4 * p.piece[k])
+
+    def piece_at(k, i):
+        return rows(piece_row(p, k, turn_row(k, 15), GIVE[i]), p.piece[k]), pl.ds(p.lead[k], p.piece[k])
+
     def second(i):
-        for k in COLOURS:
-            at, m = rows(turn_row(k, 12 + i), 4 * p.piece[k]), pl.ds(4 * p.lead[k], 4 * p.piece[k])
-            rdma(acc.at[at], land2.at[i, m], p2_send(i), p2_recv(i), p.to(k, ONE, i))
+        pass_on(i, sub_at, land2, p2_send, p2_recv, ONE)
 
     def third():
-        for i in AXES:
+        for i in (ONE, TWO):
             drain(land2.at[i], p2_recv(i))
         for k in COLOURS:
-            at, m = rows(turn_row(k, 15), 4 * p.piece[k]), pl.ds(4 * p.lead[k], 4 * p.piece[k])
-            acc[at] += land2[ZERO, m] + land2[ONE, m] + land2[TWO, m]
-        for g in AXES:
-            for k in COLOURS:
-                at, m = rows(piece_row(p, k, turn_row(k, 15), g), p.piece[k]), pl.ds(p.lead[k], p.piece[k])
-                rdma(acc.at[at], land3.at[g, m], p3_send(g), p3_recv(g), p.to(k, TWO, g))
+            at, m = sub_at(k, THREE)
+            acc[at] += land2[ONE, m] + land2[TWO, m]
+        for i in (ZERO, ONE):
+            pass_on(i, piece_at, land3, p3_send, p3_recv, TWO)
+
+    def fourth():
+        pass_on(TWO, piece_at, land3, p3_send, p3_recv, TWO)
 
     def last():
-        for g in AXES:
-            drain(land3.at[g], p3_recv(g))
+        for i in (ONE, TWO):
+            drain(land3.at[i], p3_recv(i))
         for k in COLOURS:
-            at, m = rows(piece_row(p, k, turn_row(k, 15), THREE), p.piece[k]), pl.ds(p.lead[k], p.piece[k])
-            out[m] = acc[at] + (land3[ZERO, m] + land3[ONE, m] + land3[TWO, m])
+            at, m = piece_at(k, THREE)
+            out[m] = acc[at] + (land3[ONE, m] + land3[TWO, m])
 
     def finish():
         for n in TURNS:
@@ -208,7 +233,7 @@
                 f()
         return run
     steps = [begin] + [act(turn, n) for n in range(12)]
-    steps += [both(act(turn, 12 + i), act(second, i)) for i in AXES] + [act(turn, 15), third, last, finish]
+    steps += [both(act(turn, 12 + i), act(second, i)) for i in AXES] + [act(turn, 15), third, fourth, last, finish]
     return steps
 
 
@@ -223,18 +248,30 @@
     def many(n):
         return out.at[pl.ds(ZERO, n)]
 
-    def mine(k, c, s, g):
-        return p.base + piece_row(p, k, sub_row(p, k, chunk_row(p, k, c - ONE), s - ONE), g - ONE)
-
     def sub_at(k, c, s):
-        return rows(p.base + sub_row(p, k, chunk_row(p, k, c - ONE), s - ONE), 4 * p.piece[k])
+        return rows(p.base + sub_row(p, k, chunk_row(p, k, c), TAKE[s]), 4 * p.piece[k])
+
+    def piece_at(k, g):
+        return rows(p.base + piece_row(p, k, sub_row(p, k, chunk_row(p, k, ZERO), ZERO), TAKE[g]), p.piece[k])
+
+    def both_ways(at, send, recv, ring, srcs=out):
+        for k in COLOURS:
+            src = out.at[at(k)] if srcs is out else srcs.at[pl.ds(p.lead[k], p.piece[k])]
+            rdma(src, out.at[at(k)], send(ZERO), recv(ZERO), p.nxt[k][ring])
+            rdma(src, out.at[at(k)], send(ONE), recv(ONE), p.prv[k][ring])
+
+    def forward(at, send, recv, ring):
+        for k in COLOURS:
+            rdma(out.at[at(k)], out.at[at(k)], send(TWO), recv(TWO), p.nxt[k][ring])
 
     def third():
         for k in COLOURS:
-            src, at = piece.at[pl.ds(p.lead[k], p.piece[k])], out.at[rows(mine(k, ZERO, ZERO, ZERO), p.piece[k])]
-            copy(src, at, own_sem(ZERO))
-            for t in AXES:
-                rdma(src, at, a3_send(t), a3_recv(t), p.to(k, TWO, t))
+            copy(piece.at[pl.ds(p.lead[k], p.piece[k])], out.at[piece_at(k, ZERO)], own_sem(ZERO))
+        both_ways(lambda k: piece_at(k, ZERO), a3_send, a3_recv, TWO, piece)
+
+    def fourth():
+        drain(many(p.all), a3_recv(ZERO))
+        forward(lambda k: piece_at(k, ONE), a3_send, a3_recv, TWO)
 
     def hop1(c, s):
         for k in COLOURS:
@@ -244,14 +281,13 @@
 
     def second(s):
         if s == ZERO:
-            drain(many(p.all), own_sem(ZERO))
-            for t in AXES:
-                drain(many(p.all), a3_recv(t))
-            for t in AXES:
-                for k in COLOURS:
-                    rdma(out.at[sub_at(k, ZERO, ZERO)], out.at[sub_at(k, ZERO, ZERO)], a2_send(t), a2_recv(t), p.to(k, ONE, t))
+            for sem in (own_sem(ZERO), a3_recv(ONE), a3_recv(TWO)):
+                drain(many(p.all), sem)
+            both_ways(lambda k: sub_at(k, ZERO, ZERO), a2_send, a2_recv, ONE)
         else:
-            drain(many(n_sub), a2_recv(THREE - s))
+            drain(many(n_sub), a2_recv(s - ONE))
+        if s == ONE:
+            forward(lambda k: sub_at(k, ZERO, ONE), a2_send, a2_recv, ONE)
         hop1(ZERO, s)
 
     def first(c, s):
@@ -269,7 +305,7 @@
             drain(many(n_sub), push_recv(n))
 
     act = functools.partial
-    return ([third] + [act(second, s) for s in RINGS]
+    return ([third, fourth] + [act(second, s) for s in RINGS]
             + [act(first, c, s) for c in (ONE, TWO, THREE) for s in RINGS] + [finish])
 
 
@@ -320,7 +356,8 @@
     pb, pc = ring_plan(axis, units_b), ring_plan(axis, units_c)
     n_b, n_c = TWO * pb.half, TWO * pc.half
     b_out, c_out = bc_out.at[pl.ds(ZERO, n_b)], bc_out.at[pl.ds(n_b, n_c)]
-    signal_peers(pb.peers)
+    peers = pb.peers + pb.across
+    signal_peers(peers)
     width = small_ref.shape[ONE]
     small_ref[ALL] = jnp.zeros_like(small_ref)
     small_ref[ZERO:THREE, :] = vec1_ref[ZERO:THREE, :]
@@ -330,7 +367,7 @@
         for i in range(ref.shape[ONE] // width):
             small_ref[at:at + ONE, :] = ref[:, i * width:(i + ONE) * width]
             at += ONE
-    await_peers(pb.peers)
+    await_peers(peers)
     reduce_c = scatter_rounds(pc, c_ref, part, piecec, *sc)
     gather_b = gather_rounds(pb, pieceb_ref, b_out, gather_sem)
     gather_c = gather_rounds(pc, piecec, c_out, gather_sem2)
@@ -570,9 +607,16 @@
     return jnp.sum(x, axis=ZERO, keepdims=True)
 
 
-def qkv_kernel(xq_ref, xp_ref, w_ref, b_ref, oq_ref, op_ref):
-    for x_ref, o_ref in ((xq_ref, oq_ref), (xp_ref, op_ref)):
-        o_ref[ALL] = (mm(x_ref[ALL], w_ref[ALL], NT) + b_ref[ALL]).astype(BF16)
+def qkv_kernel(xq_ref, xp_ref, w_ref, b_ref, oq_ref, op_ref, x_ref):
+    tq = xq_ref.shape[ZERO]
+
+    @pl.when(pl.program_id(ZERO) == ZERO)
+    def _():
+        x_ref[:tq, :] = xq_ref[ALL]
+        x_ref[tq:, :] = xp_ref[ALL]
+    y = (mm(x_ref[ALL], w_ref[ALL], NT) + b_ref[ALL]).astype(BF16)
+    oq_ref[ALL] = y[:tq]
+    op_ref[ALL] = y[tq:]
 
 
 def qkv_project(xq, xp, w_t, b, tile=TILE):
@@ -583,6 +627,7 @@
         out_shape=(sds((tq, f), BF16), sds((tp, f), BF16)),
         in_specs=[whole(tq, d), whole(tp, d), down(tile, d), across(ONE, tile)],
         out_specs=(across(tq, tile), across(tp, tile)),
+        scratch_shapes=[pltpu.VMEM((tq + tp, d), BF16)],
         compiler_params=vmem(), name="qkv_project",
     )(xq, xp, w_t, b)
 
@@ -651,58 +696,65 @@
     return jnp.where(u >= 0.0, 1.0 - tail, tail), u * bell * 0.3989422804
 
 
-def sequences(mq_ref, mp_ref):
-    lo, out = ZERO, []
-    for first, ref in ((ZERO, mq_ref), (8, mp_ref)):
+def each_sequence(mq_ref, mp_ref, act):
+    for first, lo, ref in ((ZERO, ZERO, mq_ref), (8, mq_ref.shape[ZERO] * mq_ref.shape[ONE], mp_ref)):
         n, seq = ref.shape
-        for i in range(n):
-            size = row_sum(ref[i:i + ONE, :].astype(F32))
+
+        def one(i, _):
+            size = row_sum(ref[pl.ds(i, ONE), :].astype(F32))
             token = lax.broadcasted_iota(jnp.int32, (seq, ONE), ZERO).astype(F32)
-            out.append((first + i, pl.ds(lo, seq), jnp.where(token < size, 1.0 / size, 0.0)))
-            lo += seq
-    return out
-
-
-def row_blocks(n, size=256):
-    size = min(n, size)
-    return [pl.ds(a, size) for a in range(ZERO, n, size)]
-
-
-ROWS = 304
-
-
-def ffn_kernel(xq_ref, xp_ref, cq_ref, cp_ref, wo_ref, vec_ref, mq_ref, mp_ref, wu_ref, bu_ref, wd_ref,
-               h_ref, r1q_ref, r1p_ref, g_ref, gp_ref, r2_ref, pool_ref):
+            act(first + i, pl.ds(pl.multiple_of(lo + i * seq, 16), seq), jnp.where(token < size, 1.0 / size, 0.0))
+            return ZERO
+        lax.fori_loop(ZERO, n, one, ZERO)
+
+
+def each_block(lo, hi, act, size=304):
+    def one(i, _):
+        act(pl.ds(pl.multiple_of(lo + i * size, 16), size))
+        return ZERO
+    lax.fori_loop(ZERO, (hi - lo) // size, one, ZERO)
+
+
+def ffn_kernel(xq_ref, xp_ref, cq_ref, cp_ref, wo_ref, bo_ref, g1_ref, s1_ref, bd_ref, g2_ref, s2_ref, mq_ref, mp_ref,
+               wu_ref, bu_ref, wd_ref, h_hbm, r1_hbm, g_ref, gp_ref, r2_hbm, pool_ref, h_ref, r1_ref, r2_ref, sems):
     j = pl.program_id(ZERO)
     t, tq = h_ref.shape[ZERO], cq_ref.shape[ZERO]
-    b_out, g1, s1, b_down, g2, s2 = (vec_ref[i:i + ONE, :] for i in range(6))
+    saved = ((h_ref, h_hbm), (r1_ref, r1_hbm), (r2_ref, r2_hbm))
 
     @pl.when(j == ZERO)
     def _():
-        for x_ref, c_ref, r_ref, lo in ((xq_ref, cq_ref, r1q_ref, ZERO), (xp_ref, cp_ref, r1p_ref, tq)):
-            for at in row_blocks(c_ref.shape[ZERO]):
-                r1 = x_ref[at, :].astype(F32) + mm(c_ref[at, :], wo_ref[ALL]) + b_out
-                r_ref[at, :] = r1
-                h = (norm_rows(r1)[ZERO] * g1 + s1).astype(BF16)
-                to = pl.ds(lo + at.start, at.size)
+        for x_ref, c_ref, lo, size in ((xq_ref, cq_ref, ZERO, tq), (xp_ref, cp_ref, tq, 256)):
+            def block(at):
+                to = pl.ds(pl.multiple_of(lo + at.start, 16), size)
+                r1 = x_ref[at, :].astype(F32) + mm(c_ref[at, :], wo_ref[ALL]) + bo_ref[ALL]
+                r1_ref[to, :] = r1
+                h = (norm_rows(r1)[ZERO] * g1_ref[ALL] + s1_ref[ALL]).astype(BF16)
                 h_ref[to, :] = h
-                r2_ref[to, :] = h.astype(F32) + b_down
-
-    for a in range(ZERO, t, ROWS):
-        at = pl.ds(a, ROWS)
+                r2_ref[to, :] = h.astype(F32) + bd_ref[ALL]
+            each_block(ZERO, c_ref.shape[ZERO], block, size)
+        for i in range(TWO):
+            copy(*saved[i], sems.at[i])
+
+    def block(at):
         u = mm(h_ref[at, :], wu_ref[ALL]) + bu_ref[ALL]
         cdf, upd = gelu_parts(u)
         g = (u * cdf).astype(BF16)
         g_ref[at, :] = g
         gp_ref[at, :] = cdf + upd
         r2_ref[at, :] += mm(g, wd_ref[ALL])
+    each_block(ZERO, t, block, 608)
 
     @pl.when(j == pl.num_programs(ZERO) - ONE)
     def _():
+        copy(*saved[TWO], sems.at[TWO])
         pool_ref[ALL] = jnp.zeros_like(pool_ref)
-        for row, at, weight in sequences(mq_ref, mp_ref):
-            y = norm_rows(r2_ref[at, :])[ZERO] * g2 + s2
-            pool_ref[row:row + ONE, :] = col_sum(y * weight)
+
+        def pool(row, at, weight):
+            y = norm_rows(r2_ref[at, :])[ZERO] * g2_ref[ALL] + s2_ref[ALL]
+            pool_ref[pl.ds(row, ONE), :] = col_sum(y * weight)
+        each_sequence(mq_ref, mp_ref, pool)
+        for i in range(THREE):
+            drain(saved[i][ZERO], sems.at[i])
 
 
 def ffn_forward(xq, xp, ctx_q, ctx_p, w_out, vecs, mask_q, mask_p, w_up, b_up, w_down, tile=TILE):
@@ -711,13 +763,13 @@
     t = tq + tp
     return pl.pallas_call(
         ffn_kernel, grid=(f // tile,),
-        out_shape=(sds((t, d), BF16), sds((tq, d), F32), sds((tp, d), F32), sds((t, f), BF16), sds((t, f), F32),
-                   sds((t, d), F32), sds((16, d), F32)),
-        in_specs=[whole(tq, d), whole(tp, d), whole(tq, d), whole(tp, d), whole(d, d), whole(*vecs.shape),
+        out_shape=(sds((t, d), BF16), sds((t, d), F32), sds((t, f), BF16), sds((t, f), F32), sds((t, d), F32), sds((16, d), F32)),
+        in_specs=[whole(tq, d), whole(tp, d), whole(tq, d), whole(tp, d), whole(d, d), *(whole(ONE, d) for _ in vecs),
                   whole(*mask_q.shape), whole(*mask_p.shape), across(d, tile), across(ONE, tile), down(tile, d)],
-        out_specs=(whole(t, d), whole(tq, d), whole(tp, d), across(t, tile), across(t, tile), whole(t, d), whole(16, d)),
+        out_specs=(ANY, ANY, across(t, tile), across(t, tile), ANY, whole(16, d)),
+        scratch_shapes=[pltpu.VMEM((t, d), BF16), pltpu.VMEM((t, d), F32), pltpu.VMEM((t, d), F32), pltpu.SemaphoreType.DMA((THREE,))],
         compiler_params=vmem(), name="ffn_forward",
-    )(xq, xp, ctx_q, ctx_p, w_out, vecs, mask_q, mask_p, w_up, b_up, w_down)
+    )(xq, xp, ctx_q, ctx_p, w_out, *vecs, mask_q, mask_p, w_up, b_up, w_down)
 
 
 def store_blocks(ref, val):
@@ -725,39 +777,52 @@
         ref[c] = val[:, c * WIDTH:(c + ONE) * WIDTH]
 
 
-def down_bwd_kernel(dpool_ref, r2_ref, mq_ref, mp_ref, vec_ref, g_ref, dwd_ref, dr2_ref, dr2b_ref, dvec_ref):
-    @pl.when(pl.program_id(ZERO) == ZERO)
+def down_bwd_kernel(dpool_ref, r2_ref, mq_ref, mp_ref, g2_ref, g_ref, dwd_ref, dr2_hbm, dr2b_hbm, dvec_ref, dr2_ref, dr2b_ref, sems):
+    j = pl.program_id(ZERO)
+    saved = ((dr2_ref, dr2_hbm), (dr2b_ref, dr2b_hbm))
+
+    @pl.when(j == ZERO)
     def _():
         dvec_ref[ALL] = jnp.zeros_like(dvec_ref)
-        for row, at, weight in sequences(mq_ref, mp_ref):
+
+        def one(row, at, weight):
             hat, r = norm_rows(r2_ref[at, :])
-            dy = weight * dpool_ref[row:row + ONE, :]
-            dr2 = norm_back(dy * vec_ref[4:5, :], hat, r)
+            dy = weight * dpool_ref[pl.ds(row, ONE), :]
+            dr2 = norm_back(dy * g2_ref[ALL], hat, r)
             dr2_ref[at, :] = dr2
             dr2b_ref[at, :] = dr2.astype(BF16)
             dvec_ref[ZERO:ONE, :] += col_sum(dr2)
             dvec_ref[ONE:TWO, :] += col_sum(dy * hat)
             dvec_ref[TWO:THREE, :] += col_sum(dy)
+        each_sequence(mq_ref, mp_ref, one)
+        for i in range(TWO):
+            copy(*saved[i], sems.at[i])
 
     store_blocks(dwd_ref, mm(g_ref[ALL], dr2b_ref[ALL], TN))
 
-
-def down_backward(dpool, r2, mask_q, mask_p, vecs, g, tile=TILE):
+    @pl.when(j == pl.num_programs(ZERO) - ONE)
+    def _():
+        for i in range(TWO):
+            drain(saved[i][ZERO], sems.at[i])
+
+
+def down_backward(dpool, r2, mask_q, mask_p, gain, g, tile=TILE):
     t, d = r2.shape
     f = g.shape[ONE]
     n = d // WIDTH
     return pl.pallas_call(
         down_bwd_kernel, grid=(f // tile,),
         out_shape=(sds((n, f, WIDTH), F32), sds((t, d), F32), sds((t, d), BF16), sds((8, d), F32)),
-        in_specs=[whole(*dpool.shape), whole(t, d), whole(*mask_q.shape), whole(*mask_p.shape), whole(*vecs.shape), across(t, tile)],
-        out_specs=(pl.BlockSpec((n, tile, WIDTH), lambda j: (ZERO, j, ZERO)), whole(t, d), whole(t, d), whole(8, d)),
+        in_specs=[whole(*dpool.shape), whole(t, d), whole(*mask_q.shape), whole(*mask_p.shape), whole(ONE, d), across(t, tile)],
+        out_specs=(pl.BlockSpec((n, tile, WIDTH), lambda j: (ZERO, j, ZERO)), ANY, ANY, whole(8, d)),
+        scratch_shapes=[pltpu.VMEM((t, d), F32), pltpu.VMEM((t, d), BF16), pltpu.SemaphoreType.DMA((TWO,))],
         compiler_params=vmem(), name="down_backward",
-    )(dpool, r2, mask_q, mask_p, vecs, g)
-
-
-PACE_UP = (5.5, 2.3, 14.0, 6.0)
-PACE_B = (5.5, 2.8, 9.0, 5.0)
-PACE_A = (8.0, 3.3, 0.0, 0.0)
+    )(dpool, r2, mask_q, mask_p, gain, g)
+
+
+PACE_UP = (3.0, 2.5, 6.0, 4.0)
+PACE_B = (4.5, 2.6, 6.5, 4.5)
+PACE_A = (12.0, 3.0, 0.0, 0.0)
 def place(timed, slot_times):
     plan = [[] for _ in slot_times]
     for t, f in sorted(timed, key=lambda x: x[ZERO]):
@@ -769,13 +834,14 @@
     n = len(steps)
     times = [0.0] + [start + pace * i for i in range(n - TWO)] + [1e3]
     if before_last:
-        times[-THREE] = times[-4] + before_third
+        times[-4] = times[-5] + before_third
+        times[-THREE] = times[-4] + before_last
         times[-TWO] = times[-THREE] + before_last
     return list(zip(times, steps))
 
 
-def run_slot(plan, j, per, point):
-    for s in range(len(plan) // per):
+def run_slot(plan, j, per, steps, point):
+    for s in range(*steps):
         todo = plan[s * per + point]
         if todo:
             @pl.when(j == s)
@@ -788,29 +854,29 @@
     return pltpu.CompilerParams(collective_id=collective_id, has_side_effects=True, vmem_limit_bytes=mb * 1024 * 1024)
 
 
-def up_bwd_kernel(axis, steps, dr2_hbm, dr2b_ref, h_ref, gp_ref, wd_ref, wu_ref, r1q_ref, r1p_ref, vec_ref, cq_ref, cp_ref, a_ref,
-                  dw_ref, dbu_ref, dr1q_ref, dr1p_ref, lowq_ref, lowp_ref, dvec_ref, piece_ref, part_ref, ht_ref, sem, *scratch):
+def up_bwd_kernel(axis, steps, dr2_hbm, dr2b_ref, h_ref, gp_ref, wd_ref, wu_ref, r1_hbm, g1_ref, cq_hbm, cp_hbm, a_ref,
+                  dw_ref, dbu_ref, dr1q_hbm, dr1p_hbm, lowq_hbm, lowp_hbm, dvec_ref, piece_ref, part_ref,
+                  dr1_ref, low_ref, r1_ref, ctx_ref, ht_ref, in_sem, out_sem, *scratch):
     j = pl.program_id(ZERO)
-    tq = dr1q_ref.shape[ZERO]
-    tp = dr1p_ref.shape[ZERO]
+    t, tq, tp = dr1_ref.shape[ZERO], dr1q_hbm.shape[ZERO], dr1p_hbm.shape[ZERO]
     p = ring_plan(axis, UNITS_A)
     pace = 5.6
     timed = timeline(scatter_rounds(p, a_ref, part_ref, piece_ref, *scratch), *PACE_UP)
     points = THREE
     plan = place(timed, [pace * (s // points) + pace * (s % points) / points for s in range(points * (steps + TWO))])
-    parts = ((dr1q_ref, dr2_hbm.at[pl.ds(ZERO, tq)]), (dr1p_ref, dr2_hbm.at[pl.ds(tq, tp)]))
+    pause = functools.partial(run_slot, plan, j, points)
+    q_rows, p_rows = pl.ds(ZERO, tq), pl.ds(tq, tp)
+    late = ((r1_hbm, r1_ref), (cq_hbm, ctx_ref.at[q_rows]), (cp_hbm, ctx_ref.at[p_rows]))
+    results = ((dr1_ref.at[q_rows], dr1q_hbm), (dr1_ref.at[p_rows], dr1p_hbm), (low_ref.at[q_rows], lowq_hbm), (low_ref.at[p_rows], lowp_hbm))
 
     @pl.when(j == ZERO)
     def _():
         signal_peers(p.peers)
-        for ref, src in parts:
-            copy(src, ref, sem.at[ZERO])
+        copy(dr2_hbm, dr1_ref, in_sem.at[ZERO])
         ht_ref[ALL] = h_ref[ALL].T
-        for ref, src in parts:
-            drain(ref, sem.at[ZERO])
-        await_peers(p.peers)
-
-    run_slot(plan, j, points, ZERO)
+        drain(dr1_ref, in_sem.at[ZERO])
+        for i in range(THREE):
+            copy(*late[i], in_sem.at[ONE + i])
 
     @pl.when(j < steps)
     def _():
@@ -818,84 +884,110 @@
         dpre = dg * gp_ref[ALL]
         dbu_ref[ALL] = col_sum(dpre)
         dpre = dpre.astype(BF16)
-        run_slot(plan, j, points, ONE)
+
+        @pl.when(j == ZERO)
+        def _():
+            await_peers(p.peers)
+        pause((ZERO, steps), ZERO)
         store_blocks(dw_ref, mm(ht_ref[ALL], dpre))
-        run_slot(plan, j, points, TWO)
-        dr1q_ref[ALL] += mm(dpre[:tq], wu_ref[ALL], NT)
-        dr1p_ref[ALL] += mm(dpre[tq:], wu_ref[ALL], NT)
+        pause((ZERO, steps), ONE)
+        dr1_ref[ALL] += mm(dpre, wu_ref[ALL], NT)
+        pause((ZERO, steps), TWO)
+
+    def norm_backward(at):
+        dy = dr1_ref[at, :].astype(BF16).astype(F32)
+        hat, r = norm_rows(r1_ref[at, :])
+        dr1 = norm_back(dy * g1_ref[ALL], hat, r)
+        dr1_ref[at, :] = dr1
+        low_ref[at, :] = dr1.astype(BF16)
+        dvec_ref[ZERO:ONE, :] += col_sum(dr1)
+        dvec_ref[ONE:TWO, :] += col_sum(dy * hat)
+        dvec_ref[TWO:THREE, :] += col_sum(dy)
 
     @pl.when(j == steps)
     def _():
         dvec_ref[ALL] = jnp.zeros_like(dvec_ref)
-        for d_ref, r_ref, low_ref in ((dr1q_ref, r1q_ref, lowq_ref), (dr1p_ref, r1p_ref, lowp_ref)):
-            for at in row_blocks(d_ref.shape[ZERO]):
-                dy = d_ref[at, :].astype(BF16).astype(F32)
-                hat, r = norm_rows(r_ref[at, :])
-                dr1 = norm_back(dy * vec_ref[ONE:TWO, :], hat, r)
-                d_ref[at, :] = dr1
-                low_ref[at, :] = dr1.astype(BF16)
-                dvec_ref[ZERO:ONE, :] += col_sum(dr1)
-                dvec_ref[ONE:TWO, :] += col_sum(dy * hat)
-                dvec_ref[TWO:THREE, :] += col_sum(dy)
+        for i in range(THREE):
+            drain(late[i][ONE], in_sem.at[ONE + i])
+        each_block(ZERO, t, norm_backward)
+        pause((steps, steps + ONE), ZERO)
+        for i in range(4):
+            copy(*results[i], out_sem.at[i])
 
     @pl.when(j >= steps)
     def _():
-        half = dr1q_ref.shape[ONE] // TWO
+        half = dr1_ref.shape[ONE] // TWO
         at = pl.ds(pl.multiple_of(jnp.maximum(j - steps, ZERO) * half, half), half)
-        run_slot(plan, j, points, ONE)
-        store_blocks(dw_ref, mm(cq_ref[ALL], lowq_ref[:, at], TN) + mm(cp_ref[ALL], lowp_ref[:, at], TN))
-        run_slot(plan, j, points, TWO)
-
-
-def up_backward(axis, dr2, dr2b, h, gp, w_down, w_up, r1_q, r1_p, vecs, ctx_q, ctx_p, part_a, collective_id, tile=TILE):
+        pause((steps + ONE, steps + TWO), ZERO)
+        pause((steps, steps + TWO), ONE)
+        store_blocks(dw_ref, mm(ctx_ref[ALL], low_ref[:, at], TN))
+        pause((steps, steps + TWO), TWO)
+
+    @pl.when(j == steps + ONE)
+    def _():
+        for i in range(4):
+            drain(results[i][ZERO], out_sem.at[i])
+
+
+def up_backward(axis, dr2, dr2b, h, gp, w_down, w_up, r1, gain, ctx_q, ctx_p, part_a, collective_id, tile=TILE):
     t, d = h.shape
     f = w_up.shape[ONE]
-    tq, tp = r1_q.shape[ZERO], r1_p.shape[ZERO]
+    tq, tp = ctx_q.shape[ZERO], ctx_p.shape[ZERO]
     n, total, steps = tile // WIDTH, part_a.shape[ZERO], f // tile
     cut = lambda j: jnp.minimum(j, steps - ONE)
     wide = lambda rows: pl.BlockSpec((rows, tile), lambda j: (ZERO, cut(j)))
+    dma, vm = pltpu.SemaphoreType.DMA, pltpu.VMEM
     return pl.pallas_call(
         functools.partial(up_bwd_kernel, axis, steps), grid=(steps + TWO,),
         out_shape=(sds(((f + d) // WIDTH, d, WIDTH), F32), sds((ONE, f), F32), sds((tq, d), F32), sds((tp, d), F32),
                    sds((tq, d), BF16), sds((tp, d), BF16), sds((8, d), F32),
                    sds((total // 128, WIDTH), F32), sds((total // TWO, WIDTH), F32)),
         in_specs=[ANY, whole(t, d), whole(t, d), wide(t), pl.BlockSpec((tile, d), lambda j: (cut(j), ZERO)), wide(d),
-                  whole(tq, d), whole(tp, d), whole(*vecs.shape), whole(tq, d), whole(tp, d), ANY],
-        out_specs=(pl.BlockSpec((n, d, WIDTH), lambda j: (j, ZERO, ZERO)), wide(ONE), whole(tq, d), whole(tp, d), whole(tq, d), whole(tp, d),
+                  ANY, whole(ONE, d), ANY, ANY, ANY],
+        out_specs=(pl.BlockSpec((n, d, WIDTH), lambda j: (j, ZERO, ZERO)), wide(ONE), ANY, ANY, ANY, ANY,
                    whole(8, d), whole(total // 128, WIDTH), ANY),
-        scratch_shapes=[pltpu.VMEM((d, t), BF16), pltpu.SemaphoreType.DMA((ONE,))] + scatter_scratch(UNITS_A),
+        scratch_shapes=[vm((t, d), F32), vm((t, d), BF16), vm((t, d), F32), vm((t, d), BF16), vm((d, t), BF16), dma((4,)), dma((4,))]
+        + scatter_scratch(UNITS_A),
         compiler_params=host(collective_id, 63), name="up_backward",
-    )(dr2, dr2b, h, gp, w_down, w_up, r1_q, r1_p, vecs, ctx_q, ctx_p, part_a)
-
-
-def attn_bwd_body(scale, head, low_ref, wo_ref, qkv_ref, probs_ref, out_ref, pause):
-    d = low_ref.shape[ONE]
+    )(dr2, dr2b, h, gp, w_down, w_up, r1, gain, ctx_q, ctx_p, part_a)
+
+
+def attn_bwd_body(scale, head, group, low_ref, wo_ref, qkv_ref, probs_ref, out_ref, dctx_ref, pause, enter=lambda: None):
+    rows_here, d = low_ref.shape
     pair = TWO * head
-    dctx = mm(low_ref[ALL], wo_ref[ALL], NT).astype(BF16)
-    for g in range(d // pair):
-        if g == d // (TWO * pair):
-            pause(ONE)
-        at = pl.ds(g * pair, pair)
+    dctx_ref[:rows_here, :] = mm(low_ref[ALL], wo_ref[ALL], NT).astype(BF16)
+    enter()
+    pause(ZERO)
+
+    def one(g):
+        at, k_at, v_at = (pl.ds(pl.multiple_of(part * d + g * pair, pair), pair) for part in range(THREE))
         q = split_heads(qkv_ref[:, at], head)
-        k = qkv_ref[:, pl.ds(d + g * pair, pair)]
-        v = qkv_ref[:, pl.ds(TWO * d + g * pair, pair)]
+        k = qkv_ref[:, k_at]
+        v = qkv_ref[:, v_at]
         p = probs_ref[ZERO, g]
-        dc = split_heads(dctx[:, g * pair:(g + ONE) * pair], head)
+        dc = split_heads(dctx_ref[:rows_here, at], head)
         dp = mm(dc, v, NT)
         pf = p.astype(F32)
         ds = (pf * (dp - row_sum(dp * pf)) * scale).astype(BF16)
         out_ref[:, at] = join_heads(mm(ds, k), head).astype(BF16)
-        out_ref[:, pl.ds(d + g * pair, pair)] = mm(ds, q, TN).astype(BF16)
-        out_ref[:, pl.ds(TWO * d + g * pair, pair)] = mm(p, dc, TN).astype(BF16)
+        out_ref[:, k_at] = mm(ds, q, TN).astype(BF16)
+        out_ref[:, v_at] = mm(p, dc, TN).astype(BF16)
+
+    def some(i, _):
+        for h in range(group):
+            one(i * group + h)
+        return ZERO
+    lax.fori_loop(ZERO, d // (pair * group), some, ZERO)
+    pause(ONE)
 
 
 def attn_qkv_kernel(axis, scale, head, nq, n_pass, lowq_ref, lowp_ref, wo_ref, qkvq_ref, qkvp_ref, probq_ref, probp_ref,
                     xq_ref, xp_ref, w_ref, dr1q_hbm, dr1p_hbm, b_ref, piecea_ref,
-                    dw_ref, db_ref, dhq_ref, dhp_ref, pieceb_ref, part_ref, a_ref, dq_ref, dp_ref, accq_ref, accp_ref, sem, gsem, *scratch):
+                    dw_ref, db_ref, dhq_ref, dhp_ref, pieceb_ref, part_ref, a_ref, dq_ref, dp_ref, accq_ref, accp_ref, dctx_ref, sem, gsem, *scratch):
     j = pl.program_id(ZERO)
-    first, last = nq + n_pass, pl.num_programs(ZERO) - ONE
     tile = w_ref.shape[ZERO]
     per = dq_ref.shape[TWO] // tile
+    first, last = nq + n_pass, nq + n_pass + per - ONE
     pa, pb = ring_plan(axis, UNITS_A), ring_plan(axis, UNITS_B)
     points = TWO
     steps = [3.2] * nq + [3.3] * n_pass + [4.3] * per
@@ -911,16 +1003,21 @@
         signal_peers(pa.peers)
         for src, dst in loads:
             copy(src, dst, sem.at[ZERO])
-        await_peers(pa.peers)
-    pause(ZERO)
+
+    def enter():
+        @pl.when(j == ZERO)
+        def _():
+            await_peers(pa.peers)
 
     @pl.when(j < nq)
     def _():
-        attn_bwd_body(scale, head, lowq_ref, wo_ref, qkvq_ref, probq_ref, dq_ref.at[jnp.minimum(j, nq - ONE)], pause)
+        attn_bwd_body(scale, head, 4, lowq_ref, wo_ref, qkvq_ref, probq_ref, dq_ref.at[jnp.minimum(j, nq - ONE)], dctx_ref,
+                      functools.partial(pause, (ZERO, nq)), enter)
 
     @pl.when((j >= nq) & (j < first))
     def _():
-        attn_bwd_body(scale, head, lowp_ref, wo_ref, qkvp_ref, probp_ref, dp_ref.at[jnp.clip(j - nq, ZERO, n_pass - ONE)], pause)
+        attn_bwd_body(scale, head, 4, lowp_ref, wo_ref, qkvp_ref, probp_ref, dp_ref.at[jnp.clip(j - nq, ZERO, n_pass - ONE)], dctx_ref,
+                      functools.partial(pause, (nq, first)))
 
     @pl.when(j == first - ONE)
     def _():
@@ -929,12 +1026,13 @@
 
     @pl.when(j >= first)
     def _():
+        pause((first, last + ONE), ZERO)
         at = pl.ds(pl.multiple_of(jnp.maximum(j - first, ZERO) * tile, tile), tile)
         dq = dq_ref[:, :, at].reshape(-ONE, tile)
         dp = dp_ref[:, :, at].reshape(-ONE, tile)
         store_blocks(dw_ref, mm(dq, xq_ref[ALL], TN) + mm(dp, xp_ref[ALL], TN))
         db_ref[ALL] = col_sum(dq.astype(F32)) + col_sum(dp.astype(F32))
-        pause(ONE)
+        pause((first, last + ONE), ONE)
         accq_ref[ALL] += mm(dq, w_ref[ALL])
         accp_ref[ALL] += mm(dp, w_ref[ALL])
 
@@ -965,7 +1063,8 @@
         out_specs=(pl.BlockSpec((cols, tile, WIDTH), lambda j: (ZERO, jt(j), ZERO)), pl.BlockSpec((ONE, tile), lambda j: (ZERO, jt(j))),
                    whole(tq, d), whole(tp, d), whole(total // 128, WIDTH), ANY, ANY),
         scratch_shapes=[pltpu.VMEM((nq, lq, f), BF16), pltpu.VMEM((n_pass, lp, f), BF16), pltpu.VMEM((tq, d), F32),
-                        pltpu.VMEM((tp, d), F32), pltpu.SemaphoreType.DMA((ONE,)), pltpu.SemaphoreType.DMA((GATHER_SEMS,))]
+                        pltpu.VMEM((tp, d), F32), pltpu.VMEM((lp, d), BF16), pltpu.SemaphoreType.DMA((ONE,)),
+                        pltpu.SemaphoreType.DMA((GATHER_SEMS,))]
         + scatter_scratch(UNITS_B),
         compiler_params=host(collective_id, 63), name="attn_qkv_backward",
     )(low_q, low_p, w_out, qkv_q, qkv_p, probs_q, probs_p, xq, xp, w_t, dr1_q, dr1_p, part_b, piece_a)
@@ -1028,27 +1127,26 @@
         p_mask = p_mask.reshape(n_pass, p_len)
         wqkv_t = w_qkv.transpose(ONE, TWO, THREE, ZERO).reshape(-ONE, d)
         wo = w_out.reshape(-ONE, d)
-        none = jnp.zeros_like(b_out)
-        vecs = jnp.stack([b_out, ln1_gain, ln1_shift, b_down, ln2_gain, ln2_shift, none, none])
+        vecs = [v.reshape(ONE, d) for v in (b_out, ln1_gain, ln1_shift, b_down, ln2_gain, ln2_shift)]
 
         qkv_q, qkv_p = qkv_project(xq, xp, wqkv_t, b_qkv.reshape(ONE, -ONE))
         probs_q, ctx_q = attention(qkv_q, q_mask, head)
         probs_p, ctx_p = attention(qkv_p, p_mask, head)
-        h, r1_q, r1_p, g, gp, r2, pooled = ffn_forward(
+        h, r1, g, gp, r2, pooled = ffn_forward(
             xq, xp, ctx_q, ctx_p, wo, vecs, q_mask, p_mask, w_up, b_up.reshape(ONE, -ONE), w_down)
         everyone = gather_embeddings(pooled, axis, ONE)
         mean_loss, d_pooled = loss_and_grad(everyone, pooled, axis, nq * n_dev)
-        dwd, dr2, dr2b, dvec2 = down_backward(d_pooled, r2, q_mask, p_mask, vecs, g)
+        dwd, dr2, dr2b, dvec2 = down_backward(d_pooled, r2, q_mask, p_mask, vecs[4], g)
         dwb, dbu, dr1_q, dr1_p, low_q, low_p, dvec1, piece_a, _ = up_backward(
-            axis, dr2, dr2b, h, gp, w_down, w_up, r1_q, r1_p, vecs, ctx_q, ctx_p, dwd.reshape(-ONE, WIDTH), TWO)
+            axis, dr2, dr2b, h, gp, w_down, w_up, r1, vecs[ONE], ctx_q, ctx_p, dwd.reshape(-ONE, WIDTH), TWO)
         dwq, dbq, dh_q, dh_p, piece_b, _, a = attn_qkv_backward(
             axis, low_q, low_p, wo, qkv_q, qkv_p, probs_q, probs_p, xq, xp, wqkv_t, dr1_q, dr1_p, dwb.reshape(-ONE, WIDTH), piece_a, head, THREE)
         bc, small = finish_sum(axis, UNITS_B, UNITS_C, piece_b, dwq.reshape(-ONE, WIDTH), dvec1, dvec2, dbq, dbu, 4)
         d_down, d_up, d_out, d_qkv = unpack(a.reshape(dwd.shape), bc, d, three * d)
-        vec = [small[i] for i in range(6)]
+        vec, bias = small[:8], small[8:]
         return (mean_loss, dh_q.reshape(q_hidden.shape), dh_p.reshape(p_hidden.shape),
-                d_qkv.reshape(three, heads, head, d).transpose(THREE, ZERO, ONE, TWO), small[8:8 + three].reshape(b_qkv.shape),
-                d_out.reshape(w_out.shape), vec[ZERO], vec[ONE], vec[TWO], d_up, small[8 + three:-ONE].reshape(-ONE),
+                d_qkv.reshape(three, heads, head, d).transpose(THREE, ZERO, ONE, TWO), bias[:three].reshape(b_qkv.shape),
+                d_out.reshape(w_out.shape), vec[ZERO], vec[ONE], vec[TWO], d_up, bias[three:-ONE].reshape(-ONE),
                 d_down, vec[THREE], vec[4], vec[5])
 
     in_specs = (P(axis),) * 4 + (P(),) * 12

time: 473 us -> 445 us (0.941)
  Pallas kernels: 459 us -> 435 us
    pallas_call x1, Pallas kernels: 74.9 us -> 60.3 us  [up_backward(): pl.pallas_call(functools.partial(up_bwd_kernel, axis, steps), grid=(steps...]
    pallas_call x1, Pallas kernels: 109 us -> 102 us  [finish_sum(): pl.pallas_call(functools.partial(finish_kernel, axis, units_b, units_c),...]
where the time goes in v4:
time: 445 us; the launch traced here: 444 us
  Pallas kernels  435 us (98%)
  local copies, waits for them, and re-layouts  7.41 us (2%)
    pallas_call x1, Pallas kernels, finish_sum(): pl.pallas_call(functools.partial(finish_kernel, axis, units_b, units_c),...  102 us
    pallas_call x1, Pallas kernels, attn_qkv_backward(): pl.pallas_call(functools.partial(attn_qkv_kernel, axis, head ** (-0.5), h...  94.7 us
    pallas_call x1, Pallas kernels, up_backward(): pl.pallas_call(functools.partial(up_bwd_kernel, axis, steps), grid=(steps...  60.3 us
    pallas_call x1, Pallas kernels, ffn_forward(): pl.pallas_call(ffn_kernel, grid=(f // tile,), out_shape=(sds((t, d), BF16...  55.7 us
    pallas_call x1, Pallas kernels, gather_embeddings(): pl.pallas_call(functools.partial(gather_kernel, axis), out_shape=jax.Shap...  35.2 us
    pallas_call x1, Pallas kernels, down_backward(): pl.pallas_call(down_bwd_kernel, grid=(f // tile,), out_shape=(sds((n, f,...  23.7 us
    pallas_call x1, Pallas kernels, unpack(): pl.pallas_call(unpack_kernel, out_shape=(sds((ff, d), F32), sds((d, ff),...  23.2 us
    pallas_call x2, Pallas kernels, attention(): pl.pallas_call(functools.partial(attn_kernel, head ** (-0.5), head), grid...  16.9 us

profile of v4, /device:TPU:1, one launch (start us, length us, event | category | flops | bytes accessed | tf_op | source)
XLA Modules:
  0.0 443.5 jit_solution(12766758696206140759)
XLA Ops:
  0.6 1.4 reshape.108.b_ref
  2.1 12.5 %qkv_project.1 = (bf16[192,3072]{1,0:T(8,128)(2,1)}, bf16[1024,3072]{1,0:T(8,128)(2,1)}) custom-call(bf16[192,1024]{1,0:T(8,128)(2,1)} %bitcast.51, bf16[1024,1024]{1,0:T(8,128)(2,1)} %bitcast.43, bf16[3072,1024]{1,0:T(8,128)(2,1)} %bitcast.40, f32[1,3072]{1,0:T(1,128)} %reshape.108.b_ref), custom_call_target="tpu_custom_call" | custom-call | tf_op jit(solution)/shard_map/qkv_project/pallas_call | solution.py:625
  14.5 5.2 %attention.2 = (bf16[4,8,96,48]{3,2,1,0:T(8,128)(2,1)}, bf16[192,1024]{1,0:T(8,128)(2,1)}) custom-call(bf16[192,3072]{1,0:T(8,128)(2,1)} %get-tuple-element.53.qkv_ref.qkvq_ref, s32[4,1,48]{2,1,0:T(1,128)} %bitcast.59), custom_call_target="tpu_custom_call" | custom-call | tf_op jit(solution)/shard_map/attention/pallas_call | solution.py:667
  19.7 11.7 %attention.3 = (bf16[8,8,256,128]{3,2,1,0:T(8,128)(2,1)}, bf16[1024,1024]{1,0:T(8,128)(2,1)}) custom-call(bf16[1024,3072]{1,0:T(8,128)(2,1)} %get-tuple-element.55.qkv_ref.qkvp_ref, s32[8,1,128]{2,1,0:T(1,128)} %bitcast.56), custom_call_target="tpu_custom_call" | custom-call | tf_op jit(solution)/shard_map/attention/pallas_call | solution.py:667
  31.4 55.7 %ffn_forward.1 = (bf16[1216,1024]{1,0:T(8,128)(2,1)}, f32[1216,1024]{1,0:T(8,128)}, bf16[1216,4096]{1,0:T(8,128)(2,1)}, f32[1216,4096]{1,0:T(8,128)}, f32[1216,1024]{1,0:T(8,128)}, /*index=5*/f32[16,1024]{1,0:T(8,128)}) custom-call(bf16[192,1024]{1,0:T(8,128)(2,1)} %bitcast.52, bf16[1024,1024]{1,0:T(8,128)(2,1)} %bitcast.44, ...), custom_call_target="tpu_custom_call" | custom-call | tf_op jit(solution)/shard_map/ffn_forward/pallas_call | solution.py:764
  87.2 0.0 copy-start
  87.2 0.8 copy-done
  88.0 35.2 %gather_embeddings.1 = f32[4,4,4,24,1024]{4,3,2,1,0:T(8,128)S(1)} custom-call(f32[16,1024]{1,0:T(8,128)S(1)} %copy-done), custom_call_target="tpu_custom_call" | custom-call | tf_op jit(solution)/shard_map/gather_embeddings/pallas_call | solution.py:468
  123.2 0.0 copy-done.1
  123.2 11.2 %loss_and_grad.1 = (f32[8,128]{1,0:T(8,128)S(1)}, f32[16,1024]{1,0:T(8,128)S(1)}) custom-call(f32[64,24,1024]{2,1,0:T(8,128)S(1)} %bitcast.39, f32[16,1024]{1,0:T(8,128)S(1)} %copy-done.1), custom_call_target="tpu_custom_call" | custom-call | tf_op jit(solution)/shard_map/loss_and_grad/pallas_call | solution.py:557
  134.4 0.6 copy-done.2
  135.0 0.5 slice.37
  135.5 23.7 %down_backward.1 = (f32[4,4096,256]{2,1,0:T(8,128)}, f32[1216,1024]{1,0:T(8,128)}, bf16[1216,1024]{1,0:T(8,128)(2,1)}, f32[8,1024]{1,0:T(8,128)}) custom-call(f32[16,1024]{1,0:T(8,128)} %copy-done.2, f32[1216,1024]{1,0:T(8,128)} %get-tuple-element.60.r2_ref, s32[4,48]{1,0:T(4,128)} %mq_ref.3, s32[8,128]{1,0:T(8,128)} %bitcast.58, f32[1,1024]{1,0:T(1,128)} %bitcast.62, ...), custom_call_target="tpu_custom_call" | custom-call | tf_op jit(solution)/shard_map/down_backward/pallas_call | solution.py:813
  159.2 60.3 %up_backward.1 = (f32[20,1024,256]{2,1,0:T(8,128)}, f32[1,4096]{1,0:T(1,128)}, f32[192,1024]{1,0:T(8,128)}, f32[1024,1024]{1,0:T(8,128)}, bf16[192,1024]{1,0:T(8...) custom-call(f32[1216,1024]{1,0:T(8,128)} %get-tuple-element.62.dr2_hbm, ...), custom_call_target="tpu_custom_call" | custom-call | tf_op jit(solution)/shard_map/up_backward/pallas_call | solution.py:940
  219.5 94.7 %attn_qkv_backward.1 = (f32[4,3072,256]{2,1,0:T(8,128)}, f32[1,3072]{1,0:T(1,128)}, bf16[192,1024]{1,0:T(8,128)(2,1)}, bf16[1024,1024]{1,0:T(8,128)(2,1)}, f32[1...) custom-call(bf16[192,1024]{1,0:T(8,128)(2,1)} %get-tuple-element.68.lowq_ref, ...), custom_call_target="tpu_custom_call" | custom-call | tf_op jit(solution)/shard_map/attn_qkv_backward/pallas_call | solution.py:1057
  314.3 102.0 %finish_sum.1 = (f32[32768,256]{1,0:T(8,128)S(1)}, f32[16,1024]{1,0:T(8,128)}, f32[6144,256]{1,0:T(8,128)}) custom-call(f32[160,256]{1,0:T(8,128)} %get-tuple-element.79.pieceb_ref, f32[12288,256]{1,0:T(8,128)} %bitcast.48, f32[8,1024]{1,0:T(8,128)} %get-tuple-element.81.vec1_ref, f32[8,1024]{1,0:T(8,128)} %get-tuple-element.82.vec2_ref, ...), custom_call_target="tpu_custom_call" | custom-call | tf_op jit(solution)/shard_map/finish_sum/pallas_call | solution.py:393
  416.3 0.0 copy-start.5
  416.3 23.2 %unpack.1 = (f32[4096,1024]{1,0:T(8,128)}, f32[1024,4096]{1,0:T(8,128)}, f32[1024,1024]{1,0:T(8,128)}, f32[3072,1024]{1,0:T(8,128)}) custom-call(f32[4,4096,256]{2,1,0:T(8,128)} %bitcast.46, f32[32768,256]{1,0:T(8,128)S(1)} %get-tuple-element.85.bc_ref), custom_call_target="tpu_custom_call" | custom-call | tf_op jit(solution)/shard_map/unpack/pallas_call | solution.py:1109
  439.5 0.6 copy.33
  440.1 0.6 fusion
  440.8 0.7 reshape.127
  441.4 0.0 copy-done.4
  441.4 0.7 copy.36
  442.2 1.3 copy.37
  (8 shorter events, 0.0 us)
Async XLA Ops:
  87.2 0.8 copy-start
  88.0 35.2 %copy-start.1 = (f32[16,1024]{1,0:T(8,128)S(1)}, f32[16,1024]{1,0:T(8,128)}, u32[]{:S(2)}) copy-start(f32[16,1024]{1,0:T(8,128)} %get-tuple-element.57.pooled_ref) | copy-start | bytes 196612
  134.4 0.6 copy-start.2
  416.3 23.2 %copy-start.5 = (f32[16,1024]{1,0:T(8,128)S(1)}, f32[16,1024]{1,0:T(8,128)}, u32[]{:S(2)}) copy-start(f32[16,1024]{1,0:T(8,128)} %get-tuple-element.87) | copy-start | bytes 196612
  416.3 25.1 %copy-start.4 = (bf16[192,1024]{1,0:T(8,128)(2,1)S(1)}, bf16[192,1024]{1,0:T(8,128)(2,1)}, u32[]{:S(2)}) copy-start(bf16[192,1024]{1,0:T(8,128)(2,1)} %get-tuple-element.76) | copy-start | bytes 1179652
  416.3 25.9 %copy-start.3 = (bf16[1024,1024]{1,0:T(8,128)(2,1)S(1)}, bf16[1024,1024]{1,0:T(8,128)(2,1)}, u32[]{:S(2)}) copy-start(bf16[1024,1024]{1,0:T(8,128)(2,1)} %get-tuple-element.77) | copy-start | bytes 6291460

commit v5 on v4

--- a/solution.py
+++ b/solution.py
@@ -350,14 +350,16 @@
     return plan
 
 
-def finish_kernel(axis, units_b, units_c, pieceb_ref, c_ref, vec1_ref, vec2_ref, bq_ref, bu_ref, bc_out, small_out, part,
-                  small_ref, piecec, *scratch):
+def finish_kernel(axis, units_b, units_c, pieceb_ref, c_ref, a_ref, vec1_ref, vec2_ref, bq_ref, bu_ref, bc_out, small_out, part,
+                  small_ref, piecec, a_sem, *scratch):
     sc, (gather_sem, gather_sem2, small_land, small_sem) = scratch[:6], scratch[6:]
     pb, pc = ring_plan(axis, units_b), ring_plan(axis, units_c)
     n_b, n_c = TWO * pb.half, TWO * pc.half
     b_out, c_out = bc_out.at[pl.ds(ZERO, n_b)], bc_out.at[pl.ds(n_b, n_c)]
+    a_here = bc_out.at[pl.ds(n_b + n_c, bc_out.shape[ZERO] - n_b - n_c)]
     peers = pb.peers + pb.across
     signal_peers(peers)
+    copy(a_ref.at[pl.ds(ZERO, a_here.shape[ZERO])], a_here, a_sem.at[ZERO])
     width = small_ref.shape[ONE]
     small_ref[ALL] = jnp.zeros_like(small_ref)
     small_ref[ZERO:THREE, :] = vec1_ref[ZERO:THREE, :]
@@ -382,9 +384,10 @@
             f()
     for rounds in (reduce_c, gather_b, gather_c):
         rounds[-ONE]()
-
-
-def finish_sum(axis, units_b, units_c, piece_b, c, vec1, vec2, bq, bu, collective_id):
+    drain(a_here, a_sem.at[ZERO])
+
+
+def finish_sum(axis, units_b, units_c, piece_b, c, a, keep, vec1, vec2, bq, bu, collective_id):
     sds = jax.ShapeDtypeStruct
     dma = pltpu.SemaphoreType.DMA
     vm = pl.BlockSpec(memory_space=pltpu.VMEM)
@@ -392,13 +395,13 @@
     small = (16, vec1.shape[ONE])
     outs = pl.pallas_call(
         functools.partial(finish_kernel, axis, units_b, units_c),
-        out_shape=(pltpu.VMEM((piece_b.shape[ZERO] * 128 + n, WIDTH), F32), sds(small, F32), sds((n // TWO, WIDTH), F32)),
-        in_specs=[vm, ANY, vm, vm, vm, vm], out_specs=(vm, vm, ANY),
-        scratch_shapes=[pltpu.VMEM(small, F32), pltpu.VMEM((n // 128, WIDTH), F32)] + scatter_scratch(units_c)
+        out_shape=(pltpu.VMEM((piece_b.shape[ZERO] * 128 + n + keep, WIDTH), F32), sds(small, F32), sds((n // TWO, WIDTH), F32)),
+        in_specs=[vm, ANY, ANY, vm, vm, vm, vm], out_specs=(vm, vm, ANY),
+        scratch_shapes=[pltpu.VMEM(small, F32), pltpu.VMEM((n // 128, WIDTH), F32), dma((ONE,))] + scatter_scratch(units_c)
         + [dma((GATHER_SEMS,)), dma((GATHER_SEMS,))] + small_scratch(small),
-        compiler_params=pltpu.CompilerParams(collective_id=collective_id, has_side_effects=True, vmem_limit_bytes=22 * 1024 * 1024),
+        compiler_params=pltpu.CompilerParams(collective_id=collective_id, has_side_effects=True, vmem_limit_bytes=17 * 1024 * 1024),
         name="finish_sum",
-    )(piece_b, c, vec1, vec2, bq, bu)
+    )(piece_b, c, a, vec1, vec2, bq, bu)
     return outs[:TWO]
 
 
@@ -742,7 +745,7 @@
         g_ref[at, :] = g
         gp_ref[at, :] = cdf + upd
         r2_ref[at, :] += mm(g, wd_ref[ALL])
-    each_block(ZERO, t, block, 608)
+    each_block(ZERO, t, block)
 
     @pl.when(j == pl.num_programs(ZERO) - ONE)
     def _():
@@ -757,7 +760,7 @@
             drain(saved[i][ZERO], sems.at[i])
 
 
-def ffn_forward(xq, xp, ctx_q, ctx_p, w_out, vecs, mask_q, mask_p, w_up, b_up, w_down, tile=TILE):
+def ffn_forward(xq, xp, ctx_q, ctx_p, w_out, vecs, mask_q, mask_p, w_up, b_up, w_down, tile=TWO * TILE):
     tq, d = xq.shape
     tp, f = xp.shape[ZERO], w_up.shape[ONE]
     t = tq + tp
@@ -806,7 +809,7 @@
             drain(saved[i][ZERO], sems.at[i])
 
 
-def down_backward(dpool, r2, mask_q, mask_p, gain, g, tile=TILE):
+def down_backward(dpool, r2, mask_q, mask_p, gain, g, tile=TWO * TILE):
     t, d = r2.shape
     f = g.shape[ONE]
     n = d // WIDTH
@@ -821,8 +824,8 @@
 
 
 PACE_UP = (3.0, 2.5, 6.0, 4.0)
-PACE_B = (4.5, 2.6, 6.5, 4.5)
-PACE_A = (12.0, 3.0, 0.0, 0.0)
+PACE_B = (4.5, 2.8, 5.5, 4.5)
+PACE_A = (9.0, 3.2, 0.0, 0.0)
 def place(timed, slot_times):
     plan = [[] for _ in slot_times]
     for t, f in sorted(timed, key=lambda x: x[ZERO]):
@@ -1011,12 +1014,12 @@
 
     @pl.when(j < nq)
     def _():
-        attn_bwd_body(scale, head, 4, lowq_ref, wo_ref, qkvq_ref, probq_ref, dq_ref.at[jnp.minimum(j, nq - ONE)], dctx_ref,
+        attn_bwd_body(scale, head, ONE, lowq_ref, wo_ref, qkvq_ref, probq_ref, dq_ref.at[jnp.minimum(j, nq - ONE)], dctx_ref,
                       functools.partial(pause, (ZERO, nq)), enter)
 
     @pl.when((j >= nq) & (j < first))
     def _():
-        attn_bwd_body(scale, head, 4, lowp_ref, wo_ref, qkvp_ref, probp_ref, dp_ref.at[jnp.clip(j - nq, ZERO, n_pass - ONE)], dctx_ref,
+        attn_bwd_body(scale, head, TWO, lowp_ref, wo_ref, qkvp_ref, probp_ref, dp_ref.at[jnp.clip(j - nq, ZERO, n_pass - ONE)], dctx_ref,
                       functools.partial(pause, (nq, first)))
 
     @pl.when(j == first - ONE)
@@ -1070,48 +1073,47 @@
     )(low_q, low_p, w_out, qkv_q, qkv_p, probs_q, probs_p, xq, xp, w_t, dr1_q, dr1_p, part_b, piece_a)
 
 
-def unpack_kernel(a_hbm, bc_ref, down_ref, up_ref, out_ref, qkv_ref, stage, sems, in_sem, out_sem):
-    n_up = up_ref.shape[ONE] // WIDTH
-    slots, _, rows_each, _ = stage.shape
-
+def unpack_kernel(a_hbm, sums_ref, down_ref, up_ref, out_ref, qkv_ref, stage, sem, in_sem, out_sem):
     def cols(i):
         return pl.ds(i * WIDTH, WIDTH)
 
+    slots, rows_each, _ = stage.shape
+    n, ff, f = up_ref.shape[ZERO], down_ref.shape[ZERO], qkv_ref.shape[ZERO]
+    kept = sums_ref.shape[ZERO] - (up_ref.shape[ONE] + out_ref.shape[ONE]) // WIDTH * n - qkv_ref.shape[ONE] // WIDTH * f
+    todo = [(kept + i * rows_each) for i in range((down_ref.shape[ONE] // WIDTH * ff - kept) // rows_each)]
+
     def load(i):
-        copy(a_hbm.at[:, pl.ds(i * rows_each, rows_each)], stage.at[i % slots], in_sem.at[i % slots])
-
-    total = down_ref.shape[ZERO] // rows_each
+        copy(a_hbm.at[pl.ds(todo[i], rows_each)], stage.at[i % slots], in_sem.at[i % slots])
+
     for i in range(slots):
         load(i)
-    n, m, k = up_ref.shape[ZERO], qkv_ref.shape[ZERO], n_up + out_ref.shape[ONE] // WIDTH
-    for i in range(k):
-        copy(bc_ref.at[pl.ds(i * n, n)], up_ref.at[:, cols(i)] if i < n_up else out_ref.at[:, cols(i - n_up)], sems.at[ZERO])
-    for i in range(qkv_ref.shape[ONE] // WIDTH):
-        copy(bc_ref.at[pl.ds(k * n + i * m, m)], qkv_ref.at[:, cols(i)], sems.at[ZERO])
-    for i in range(total):
+    at = ZERO
+    for ref, size in ((up_ref, n), (out_ref, n), (qkv_ref, f), (down_ref, ff)):
+        for i in range(ref.shape[ONE] // WIDTH):
+            if at < sums_ref.shape[ZERO]:
+                copy(sums_ref.at[pl.ds(at, size)], ref.at[:, cols(i)], sem.at[ZERO])
+            at += size
+    for i, row in enumerate(todo):
         slot = i % slots
         drain(stage.at[slot], in_sem.at[slot])
-        for k in range(stage.shape[ONE]):
-            copy(stage.at[slot, k], down_ref.at[pl.ds(i * rows_each, rows_each), cols(k)], out_sem.at[slot])
-        if i >= ONE and i - ONE + slots < total:
-            drain(stage.at[(i - ONE) % slots], out_sem.at[(i - ONE) % slots])
+        copy(stage.at[slot], down_ref.at[pl.ds(row % ff, rows_each), cols(row // ff)], out_sem.at[slot])
+        if i >= ONE and i - ONE + slots < len(todo):
+            drain(stage.at[slot], out_sem.at[(i - ONE) % slots])
             load(i - ONE + slots)
-    for i in range(max(total - slots, ZERO), total):
-        drain(stage.at[i % slots], out_sem.at[i % slots])
-    drain(bc_ref, sems.at[ZERO])
-
-
-def unpack(a, bc, d, f):
-    ff = a.shape[ONE]
-    vm = pl.BlockSpec(memory_space=pltpu.VMEM)
+    for i in range(max(len(todo) - slots, ZERO), len(todo)):
+        drain(stage.at[ZERO], out_sem.at[i % slots])
+    drain(sums_ref, sem.at[ZERO])
+
+
+def unpack(a, sums, d, ff, f):
     slots = 4
     dma = pltpu.SemaphoreType.DMA
     return pl.pallas_call(
         unpack_kernel, out_shape=(sds((ff, d), F32), sds((d, ff), F32), sds((d, d), F32), sds((f, d), F32)),
-        in_specs=[ANY, vm], out_specs=(ANY,) * 4,
-        scratch_shapes=[pltpu.VMEM((slots, d // WIDTH, TILE, WIDTH), F32), dma((ONE,)), dma((slots,)), dma((slots,))],
-        compiler_params=vmem(12), name="unpack",
-    )(a, pltpu.with_memory_space_constraint(bc, pltpu.VMEM))
+        in_specs=[ANY, pl.BlockSpec(memory_space=pltpu.VMEM)], out_specs=(ANY,) * 4,
+        scratch_shapes=[pltpu.VMEM((slots, TWO * TILE, WIDTH), F32), dma((ONE,)), dma((slots,)), dma((slots,))],
+        compiler_params=vmem(8), name="unpack",
+    )(a, pltpu.with_memory_space_constraint(sums, pltpu.VMEM))
 
 
 def solution(mesh):
@@ -1141,8 +1143,9 @@
             axis, dr2, dr2b, h, gp, w_down, w_up, r1, vecs[ONE], ctx_q, ctx_p, dwd.reshape(-ONE, WIDTH), TWO)
         dwq, dbq, dh_q, dh_p, piece_b, _, a = attn_qkv_backward(
             axis, low_q, low_p, wo, qkv_q, qkv_p, probs_q, probs_p, xq, xp, wqkv_t, dr1_q, dr1_p, dwb.reshape(-ONE, WIDTH), piece_a, head, THREE)
-        bc, small = finish_sum(axis, UNITS_B, UNITS_C, piece_b, dwq.reshape(-ONE, WIDTH), dvec1, dvec2, dbq, dbu, 4)
-        d_down, d_up, d_out, d_qkv = unpack(a.reshape(dwd.shape), bc, d, three * d)
+        sums, small = finish_sum(axis, UNITS_B, UNITS_C, piece_b, dwq.reshape(-ONE, WIDTH), a, THREE * w_down.shape[ZERO],
+                                 dvec1, dvec2, dbq, dbu, 4)
+        d_down, d_up, d_out, d_qkv = unpack(a, sums, d, w_down.shape[ZERO], three * d)
         vec, bias = small[:8], small[8:]
         return (mean_loss, dh_q.reshape(q_hidden.shape), dh_p.reshape(p_hidden.shape),
                 d_qkv.reshape(three, heads, head, d).transpose(THREE, ZERO, ONE, TWO), bias[:three].reshape(b_qkv.shape),

time: 445 us -> 439 us (0.987)
  Pallas kernels: 435 us -> 430 us
    pallas_call x1, Pallas kernels: 23.2 us -> 17.8 us  [unpack(): pl.pallas_call(unpack_kernel, out_shape=(sds((ff, d), F32), sds((d, ff),...]
where the time goes in v5:
time: 439 us; the launch traced here: 438 us
  Pallas kernels  430 us (98%)
  local copies, waits for them, and re-layouts  7.41 us (2%)
    pallas_call x1, Pallas kernels, finish_sum(): pl.pallas_call(functools.partial(finish_kernel, axis, units_b, units_c),...  104 us
    pallas_call x1, Pallas kernels, attn_qkv_backward(): pl.pallas_call(functools.partial(attn_qkv_kernel, axis, head ** (-0.5), h...  96 us
    pallas_call x1, Pallas kernels, up_backward(): pl.pallas_call(functools.partial(up_bwd_kernel, axis, steps), grid=(steps...  60.3 us
    pallas_call x1, Pallas kernels, ffn_forward(): pl.pallas_call(ffn_kernel, grid=(f // tile,), out_shape=(sds((t, d), BF16...  53.7 us
    pallas_call x1, Pallas kernels, gather_embeddings(): pl.pallas_call(functools.partial(gather_kernel, axis), out_shape=jax.Shap...  35.2 us
    pallas_call x1, Pallas kernels, down_backward(): pl.pallas_call(down_bwd_kernel, grid=(f // tile,), out_shape=(sds((n, f,...  22.3 us
    pallas_call x1, Pallas kernels, unpack(): pl.pallas_call(unpack_kernel, out_shape=(sds((ff, d), F32), sds((d, ff),...  17.8 us
    pallas_call x2, Pallas kernels, attention(): pl.pallas_call(functools.partial(attn_kernel, head ** (-0.5), head), grid...  16.9 us

profile of v5, /device:TPU:1, one launch (start us, length us, event | category | flops | bytes accessed | tf_op | source)
XLA Modules:
  0.0 438.1 jit_solution(11257339777047162971)
XLA Ops:
  0.6 1.4 reshape.105.b_ref
  2.1 12.5 %qkv_project.1 = (bf16[192,3072]{1,0:T(8,128)(2,1)}, bf16[1024,3072]{1,0:T(8,128)(2,1)}) custom-call(bf16[192,1024]{1,0:T(8,128)(2,1)} %bitcast.49, bf16[1024,1024]{1,0:T(8,128)(2,1)} %bitcast.42, bf16[3072,1024]{1,0:T(8,128)(2,1)} %bitcast.39, f32[1,3072]{1,0:T(1,128)} %reshape.105.b_ref), custom_call_target="tpu_custom_call" | custom-call | tf_op jit(solution)/shard_map/qkv_project/pallas_call | solution.py:628
  14.5 5.2 %attention.2 = (bf16[4,8,96,48]{3,2,1,0:T(8,128)(2,1)}, bf16[192,1024]{1,0:T(8,128)(2,1)}) custom-call(bf16[192,3072]{1,0:T(8,128)(2,1)} %get-tuple-element.53.qkv_ref.qkvq_ref, s32[4,1,48]{2,1,0:T(1,128)} %bitcast.57), custom_call_target="tpu_custom_call" | custom-call | tf_op jit(solution)/shard_map/attention/pallas_call | solution.py:670
  19.7 11.7 %attention.3 = (bf16[8,8,256,128]{3,2,1,0:T(8,128)(2,1)}, bf16[1024,1024]{1,0:T(8,128)(2,1)}) custom-call(bf16[1024,3072]{1,0:T(8,128)(2,1)} %get-tuple-element.55.qkv_ref.qkvp_ref, s32[8,1,128]{2,1,0:T(1,128)} %bitcast.54), custom_call_target="tpu_custom_call" | custom-call | tf_op jit(solution)/shard_map/attention/pallas_call | solution.py:670
  31.4 53.7 %ffn_forward.1 = (bf16[1216,1024]{1,0:T(8,128)(2,1)}, f32[1216,1024]{1,0:T(8,128)}, bf16[1216,4096]{1,0:T(8,128)(2,1)}, f32[1216,4096]{1,0:T(8,128)}, f32[1216,1024]{1,0:T(8,128)}, /*index=5*/f32[16,1024]{1,0:T(8,128)}) custom-call(bf16[192,1024]{1,0:T(8,128)(2,1)} %bitcast.50, bf16[1024,1024]{1,0:T(8,128)(2,1)} %bitcast.43, ...), custom_call_target="tpu_custom_call" | custom-call | tf_op jit(solution)/shard_map/ffn_forward/pallas_call | solution.py:767
  85.2 0.0 copy-start
  85.2 0.8 copy-done
  86.0 35.2 %gather_embeddings.1 = f32[4,4,4,24,1024]{4,3,2,1,0:T(8,128)S(1)} custom-call(f32[16,1024]{1,0:T(8,128)S(1)} %copy-done), custom_call_target="tpu_custom_call" | custom-call | tf_op jit(solution)/shard_map/gather_embeddings/pallas_call | solution.py:471
  121.2 0.0 copy-done.1
  121.2 11.2 %loss_and_grad.1 = (f32[8,128]{1,0:T(8,128)S(1)}, f32[16,1024]{1,0:T(8,128)S(1)}) custom-call(f32[64,24,1024]{2,1,0:T(8,128)S(1)} %bitcast.38, f32[16,1024]{1,0:T(8,128)S(1)} %copy-done.1), custom_call_target="tpu_custom_call" | custom-call | tf_op jit(solution)/shard_map/loss_and_grad/pallas_call | solution.py:560
  132.4 0.6 copy-done.2
  133.0 0.5 slice.37
  133.6 22.3 %down_backward.1 = (f32[4,4096,256]{2,1,0:T(8,128)}, f32[1216,1024]{1,0:T(8,128)}, bf16[1216,1024]{1,0:T(8,128)(2,1)}, f32[8,1024]{1,0:T(8,128)}) custom-call(f32[16,1024]{1,0:T(8,128)} %copy-done.2, f32[1216,1024]{1,0:T(8,128)} %get-tuple-element.60.r2_ref, s32[4,48]{1,0:T(4,128)} %mq_ref.3, s32[8,128]{1,0:T(8,128)} %bitcast.56, f32[1,1024]{1,0:T(1,128)} %bitcast.60, ...), custom_call_target="tpu_custom_call" | custom-call | tf_op jit(solution)/shard_map/down_backward/pallas_call | solution.py:816
  155.9 60.3 %up_backward.1 = (f32[20,1024,256]{2,1,0:T(8,128)}, f32[1,4096]{1,0:T(1,128)}, f32[192,1024]{1,0:T(8,128)}, f32[1024,1024]{1,0:T(8,128)}, bf16[192,1024]{1,0:T(8...) custom-call(f32[1216,1024]{1,0:T(8,128)} %get-tuple-element.62.dr2_hbm, ...), custom_call_target="tpu_custom_call" | custom-call | tf_op jit(solution)/shard_map/up_backward/pallas_call | solution.py:943
  216.3 96.0 %attn_qkv_backward.1 = (f32[4,3072,256]{2,1,0:T(8,128)}, f32[1,3072]{1,0:T(1,128)}, bf16[192,1024]{1,0:T(8,128)(2,1)}, bf16[1024,1024]{1,0:T(8,128)(2,1)}, f32[1...) custom-call(bf16[192,1024]{1,0:T(8,128)(2,1)} %get-tuple-element.68.lowq_ref, ...), custom_call_target="tpu_custom_call" | custom-call | tf_op jit(solution)/shard_map/attn_qkv_backward/pallas_call | solution.py:1060
  312.3 103.9 %finish_sum.1 = (f32[45056,256]{1,0:T(8,128)S(1)}, f32[16,1024]{1,0:T(8,128)}, f32[6144,256]{1,0:T(8,128)}) custom-call(f32[160,256]{1,0:T(8,128)} %get-tuple-element.79.pieceb_ref, f32[12288,256]{1,0:T(8,128)} %bitcast.46, f32[16384,256]{1,0:T(8,128)} %get-tuple-element.78.a_ref.a_hbm, f32[8,1024]{1,0:T(8,128)} %get-tuple-element.81.vec1_ref, ...), custom_call_target="tpu_custom_call" | custom-call | tf_op jit(solution)/shard_map/finish_sum/pallas_call | solution.py:396
  416.3 17.8 %unpack.1 = (f32[4096,1024]{1,0:T(8,128)}, f32[1024,4096]{1,0:T(8,128)}, f32[1024,1024]{1,0:T(8,128)}, f32[3072,1024]{1,0:T(8,128)}) custom-call(f32[16384,256]{1,0:T(8,128)} %get-tuple-element.78.a_ref.a_hbm, f32[45056,256]{1,0:T(8,128)S(1)} %get-tuple-element.85.sums_ref), custom_call_target="tpu_custom_call" | custom-call | tf_op jit(solution)/shard_map/unpack/pallas_call | solution.py:1111
  434.1 0.0 copy-done.5
  434.1 0.6 copy.33
  434.7 0.6 fusion
  435.3 0.7 reshape.123
  436.0 0.7 copy.36
  436.8 0.0 copy-done.3
  436.8 1.3 copy.37
  (8 shorter events, 0.0 us)
Async XLA Ops:
  85.2 0.8 copy-start
  86.0 35.2 %copy-start.1 = (f32[16,1024]{1,0:T(8,128)S(1)}, f32[16,1024]{1,0:T(8,128)}, u32[]{:S(2)}) copy-start(f32[16,1024]{1,0:T(8,128)} %get-tuple-element.57.pooled_ref) | copy-start | bytes 196612
  132.4 0.6 copy-start.2
  416.2 17.8 %copy-start.5 = (f32[16,1024]{1,0:T(8,128)S(1)}, f32[16,1024]{1,0:T(8,128)}, u32[]{:S(2)}) copy-start(f32[16,1024]{1,0:T(8,128)} %get-tuple-element.87) | copy-start | bytes 196612
  416.3 19.8 %copy-start.4 = (bf16[192,1024]{1,0:T(8,128)(2,1)S(1)}, bf16[192,1024]{1,0:T(8,128)(2,1)}, u32[]{:S(2)}) copy-start(bf16[192,1024]{1,0:T(8,128)(2,1)} %get-tuple-element.76) | copy-start | bytes 1179652
  416.3 20.5 %copy-start.3 = (bf16[1024,1024]{1,0:T(8,128)(2,1)S(1)}, bf16[1024,1024]{1,0:T(8,128)(2,1)}, u32[]{:S(2)}) copy-start(bf16[1024,1024]{1,0:T(8,128)(2,1)} %get-tuple-element.77) | copy-start | bytes 6291460

commit v6 on v5

--- a/solution.py
+++ b/solution.py
@@ -359,7 +359,6 @@
     a_here = bc_out.at[pl.ds(n_b + n_c, bc_out.shape[ZERO] - n_b - n_c)]
     peers = pb.peers + pb.across
     signal_peers(peers)
-    copy(a_ref.at[pl.ds(ZERO, a_here.shape[ZERO])], a_here, a_sem.at[ZERO])
     width = small_ref.shape[ONE]
     small_ref[ALL] = jnp.zeros_like(small_ref)
     small_ref[ZERO:THREE, :] = vec1_ref[ZERO:THREE, :]
@@ -378,6 +377,8 @@
     fill = spread(gather_b[:-ONE], len(main) - 4)
     for i, f in enumerate(main):
         f()
+        if i == 16:
+            copy(a_ref.at[pl.ds(ZERO, a_here.shape[ZERO])], a_here, a_sem.at[ZERO])
         if i % THREE == ONE and i // THREE < len(smalls):
             smalls[i // THREE]()
         for f in fill[i] if i < len(fill) else ():
@@ -726,7 +727,7 @@
 
     @pl.when(j == ZERO)
     def _():
-        for x_ref, c_ref, lo, size in ((xq_ref, cq_ref, ZERO, tq), (xp_ref, cp_ref, tq, 256)):
+        for x_ref, c_ref, lo, size in ((xq_ref, cq_ref, ZERO, tq), (xp_ref, cp_ref, tq, 128)):
             def block(at):
                 to = pl.ds(pl.multiple_of(lo + at.start, 16), size)
                 r1 = x_ref[at, :].astype(F32) + mm(c_ref[at, :], wo_ref[ALL]) + bo_ref[ALL]
@@ -1014,7 +1015,7 @@
 
     @pl.when(j < nq)
     def _():
-        attn_bwd_body(scale, head, ONE, lowq_ref, wo_ref, qkvq_ref, probq_ref, dq_ref.at[jnp.minimum(j, nq - ONE)], dctx_ref,
+        attn_bwd_body(scale, head, TWO, lowq_ref, wo_ref, qkvq_ref, probq_ref, dq_ref.at[jnp.minimum(j, nq - ONE)], dctx_ref,
                       functools.partial(pause, (ZERO, nq)), enter)
 
     @pl.when((j >= nq) & (j < first))

time: 439 us -> 437 us (level)
  no operation moved by 1% of the time
where the time goes in v6:
time: 437 us; the launch traced here: 436 us
  Pallas kernels  428 us (98%)
  local copies, waits for them, and re-layouts  7.41 us (2%)
    pallas_call x1, Pallas kernels, finish_sum(): pl.pallas_call(functools.partial(finish_kernel, axis, units_b, units_c),...  102 us
    pallas_call x1, Pallas kernels, attn_qkv_backward(): pl.pallas_call(functools.partial(attn_qkv_kernel, axis, head ** (-0.5), h...  94.4 us
    pallas_call x1, Pallas kernels, up_backward(): pl.pallas_call(functools.partial(up_bwd_kernel, axis, steps), grid=(steps...  60.3 us
    pallas_call x1, Pallas kernels, ffn_forward(): pl.pallas_call(ffn_kernel, grid=(f // tile,), out_shape=(sds((t, d), BF16...  55.2 us
    pallas_call x1, Pallas kernels, gather_embeddings(): pl.pallas_call(functools.partial(gather_kernel, axis), out_shape=jax.Shap...  35.2 us
    pallas_call x1, Pallas kernels, down_backward(): pl.pallas_call(down_bwd_kernel, grid=(f // tile,), out_shape=(sds((n, f,...  22.3 us
    pallas_call x1, Pallas kernels, unpack(): pl.pallas_call(unpack_kernel, out_shape=(sds((ff, d), F32), sds((d, ff),...  17.8 us
    pallas_call x2, Pallas kernels, attention(): pl.pallas_call(functools.partial(attn_kernel, head ** (-0.5), head), grid...  16.9 us

profile of v6, /device:TPU:1, one launch (start us, length us, event | category | flops | bytes accessed | tf_op | source)
XLA Modules:
  0.0 436.2 jit_solution(18152539401342637084)
XLA Ops:
  0.6 1.4 reshape.105.b_ref
  2.1 12.5 %qkv_project.1 = (bf16[192,3072]{1,0:T(8,128)(2,1)}, bf16[1024,3072]{1,0:T(8,128)(2,1)}) custom-call(bf16[192,1024]{1,0:T(8,128)(2,1)} %bitcast.49, bf16[1024,1024]{1,0:T(8,128)(2,1)} %bitcast.42, bf16[3072,1024]{1,0:T(8,128)(2,1)} %bitcast.39, f32[1,3072]{1,0:T(1,128)} %reshape.105.b_ref), custom_call_target="tpu_custom_call" | custom-call | tf_op jit(solution)/shard_map/qkv_project/pallas_call | solution.py:629
  14.5 5.2 %attention.2 = (bf16[4,8,96,48]{3,2,1,0:T(8,128)(2,1)}, bf16[192,1024]{1,0:T(8,128)(2,1)}) custom-call(bf16[192,3072]{1,0:T(8,128)(2,1)} %get-tuple-element.53.qkv_ref.qkvq_ref, s32[4,1,48]{2,1,0:T(1,128)} %bitcast.57), custom_call_target="tpu_custom_call" | custom-call | tf_op jit(solution)/shard_map/attention/pallas_call | solution.py:671
  19.7 11.7 %attention.3 = (bf16[8,8,256,128]{3,2,1,0:T(8,128)(2,1)}, bf16[1024,1024]{1,0:T(8,128)(2,1)}) custom-call(bf16[1024,3072]{1,0:T(8,128)(2,1)} %get-tuple-element.55.qkv_ref.qkvp_ref, s32[8,1,128]{2,1,0:T(1,128)} %bitcast.54), custom_call_target="tpu_custom_call" | custom-call | tf_op jit(solution)/shard_map/attention/pallas_call | solution.py:671
  31.4 55.2 %ffn_forward.1 = (bf16[1216,1024]{1,0:T(8,128)(2,1)}, f32[1216,1024]{1,0:T(8,128)}, bf16[1216,4096]{1,0:T(8,128)(2,1)}, f32[1216,4096]{1,0:T(8,128)}, f32[1216,1024]{1,0:T(8,128)}, /*index=5*/f32[16,1024]{1,0:T(8,128)}) custom-call(bf16[192,1024]{1,0:T(8,128)(2,1)} %bitcast.50, bf16[1024,1024]{1,0:T(8,128)(2,1)} %bitcast.43, ...), custom_call_target="tpu_custom_call" | custom-call | tf_op jit(solution)/shard_map/ffn_forward/pallas_call | solution.py:768
  86.6 0.0 copy-start
  86.6 0.8 copy-done
  87.4 35.2 %gather_embeddings.1 = f32[4,4,4,24,1024]{4,3,2,1,0:T(8,128)S(1)} custom-call(f32[16,1024]{1,0:T(8,128)S(1)} %copy-done), custom_call_target="tpu_custom_call" | custom-call | tf_op jit(solution)/shard_map/gather_embeddings/pallas_call | solution.py:472
  122.6 0.0 copy-done.1
  122.7 11.2 %loss_and_grad.1 = (f32[8,128]{1,0:T(8,128)S(1)}, f32[16,1024]{1,0:T(8,128)S(1)}) custom-call(f32[64,24,1024]{2,1,0:T(8,128)S(1)} %bitcast.38, f32[16,1024]{1,0:T(8,128)S(1)} %copy-done.1), custom_call_target="tpu_custom_call" | custom-call | tf_op jit(solution)/shard_map/loss_and_grad/pallas_call | solution.py:561
  133.8 0.6 copy-done.2
  134.5 0.5 slice.37
  135.0 22.3 %down_backward.1 = (f32[4,4096,256]{2,1,0:T(8,128)}, f32[1216,1024]{1,0:T(8,128)}, bf16[1216,1024]{1,0:T(8,128)(2,1)}, f32[8,1024]{1,0:T(8,128)}) custom-call(f32[16,1024]{1,0:T(8,128)} %copy-done.2, f32[1216,1024]{1,0:T(8,128)} %get-tuple-element.60.r2_ref, s32[4,48]{1,0:T(4,128)} %mq_ref.3, s32[8,128]{1,0:T(8,128)} %bitcast.56, f32[1,1024]{1,0:T(1,128)} %bitcast.60, ...), custom_call_target="tpu_custom_call" | custom-call | tf_op jit(solution)/shard_map/down_backward/pallas_call | solution.py:817
  157.3 60.3 %up_backward.1 = (f32[20,1024,256]{2,1,0:T(8,128)}, f32[1,4096]{1,0:T(1,128)}, f32[192,1024]{1,0:T(8,128)}, f32[1024,1024]{1,0:T(8,128)}, bf16[192,1024]{1,0:T(8...) custom-call(f32[1216,1024]{1,0:T(8,128)} %get-tuple-element.62.dr2_hbm, ...), custom_call_target="tpu_custom_call" | custom-call | tf_op jit(solution)/shard_map/up_backward/pallas_call | solution.py:944
  217.7 94.4 %attn_qkv_backward.1 = (f32[4,3072,256]{2,1,0:T(8,128)}, f32[1,3072]{1,0:T(1,128)}, bf16[192,1024]{1,0:T(8,128)(2,1)}, bf16[1024,1024]{1,0:T(8,128)(2,1)}, f32[1...) custom-call(bf16[192,1024]{1,0:T(8,128)(2,1)} %get-tuple-element.68.lowq_ref, ...), custom_call_target="tpu_custom_call" | custom-call | tf_op jit(solution)/shard_map/attn_qkv_backward/pallas_call | solution.py:1061
  312.1 102.3 %finish_sum.1 = (f32[45056,256]{1,0:T(8,128)S(1)}, f32[16,1024]{1,0:T(8,128)}, f32[6144,256]{1,0:T(8,128)}) custom-call(f32[160,256]{1,0:T(8,128)} %get-tuple-element.79.pieceb_ref, f32[12288,256]{1,0:T(8,128)} %bitcast.46, f32[16384,256]{1,0:T(8,128)} %get-tuple-element.78.a_ref.a_hbm, f32[8,1024]{1,0:T(8,128)} %get-tuple-element.81.vec1_ref, ...), custom_call_target="tpu_custom_call" | custom-call | tf_op jit(solution)/shard_map/finish_sum/pallas_call | solution.py:397
  414.3 0.0 copy-start.5
  414.4 0.0 copy-start.4
  414.4 17.8 %unpack.1 = (f32[4096,1024]{1,0:T(8,128)}, f32[1024,4096]{1,0:T(8,128)}, f32[1024,1024]{1,0:T(8,128)}, f32[3072,1024]{1,0:T(8,128)}) custom-call(f32[16384,256]{1,0:T(8,128)} %get-tuple-element.78.a_ref.a_hbm, f32[45056,256]{1,0:T(8,128)S(1)} %get-tuple-element.85.sums_ref), custom_call_target="tpu_custom_call" | custom-call | tf_op jit(solution)/shard_map/unpack/pallas_call | solution.py:1112
  432.2 0.6 copy.33
  432.8 0.6 fusion
  433.4 0.7 reshape.123
  434.1 0.7 copy.36
  434.9 1.3 copy.37
  (8 shorter events, 0.0 us)
Async XLA Ops:
  86.6 0.8 copy-start
  87.4 35.2 %copy-start.1 = (f32[16,1024]{1,0:T(8,128)S(1)}, f32[16,1024]{1,0:T(8,128)}, u32[]{:S(2)}) copy-start(f32[16,1024]{1,0:T(8,128)} %get-tuple-element.57.pooled_ref) | copy-start | bytes 196612
  133.8 0.6 copy-start.2
  414.3 17.8 %copy-start.5 = (f32[16,1024]{1,0:T(8,128)S(1)}, f32[16,1024]{1,0:T(8,128)}, u32[]{:S(2)}) copy-start(f32[16,1024]{1,0:T(8,128)} %get-tuple-element.87) | copy-start | bytes 196612
  414.4 19.8 %copy-start.4 = (bf16[192,1024]{1,0:T(8,128)(2,1)S(1)}, bf16[192,1024]{1,0:T(8,128)(2,1)}, u32[]{:S(2)}) copy-start(bf16[192,1024]{1,0:T(8,128)(2,1)} %get-tuple-element.76) | copy-start | bytes 1179652
  414.4 20.5 %copy-start.3 = (bf16[1024,1024]{1,0:T(8,128)(2,1)S(1)}, bf16[1024,1024]{1,0:T(8,128)(2,1)}, u32[]{:S(2)}) copy-start(bf16[1024,1024]{1,0:T(8,128)(2,1)} %get-tuple-element.77) | copy-start | bytes 6291460

commit v7 on v6

--- a/solution.py
+++ b/solution.py
@@ -727,7 +727,7 @@
 
     @pl.when(j == ZERO)
     def _():
-        for x_ref, c_ref, lo, size in ((xq_ref, cq_ref, ZERO, tq), (xp_ref, cp_ref, tq, 128)):
+        for x_ref, c_ref, lo, size in ((xq_ref, cq_ref, ZERO, tq), (xp_ref, cp_ref, tq, 256)):
             def block(at):
                 to = pl.ds(pl.multiple_of(lo + at.start, 16), size)
                 r1 = x_ref[at, :].astype(F32) + mm(c_ref[at, :], wo_ref[ALL]) + bo_ref[ALL]
@@ -810,7 +810,7 @@
             drain(saved[i][ZERO], sems.at[i])
 
 
-def down_backward(dpool, r2, mask_q, mask_p, gain, g, tile=TWO * TILE):
+def down_backward(dpool, r2, mask_q, mask_p, gain, g, tile=TILE):
     t, d = r2.shape
     f = g.shape[ONE]
     n = d // WIDTH
@@ -825,8 +825,8 @@
 
 
 PACE_UP = (3.0, 2.5, 6.0, 4.0)
-PACE_B = (4.5, 2.8, 5.5, 4.5)
-PACE_A = (9.0, 3.2, 0.0, 0.0)
+PACE_B = (4.5, 3.0, 5.0, 4.0)
+PACE_A = (6.0, 3.4, 0.0, 0.0)
 def place(timed, slot_times):
     plan = [[] for _ in slot_times]
     for t, f in sorted(timed, key=lambda x: x[ZERO]):

time: 437 us -> 438 us (level)
  no operation moved by 1% of the time
where the time goes in v7:
time: 438 us; the launch traced here: 437 us
  Pallas kernels  429 us (98%)
  local copies, waits for them, and re-layouts  7.41 us (2%)
    pallas_call x1, Pallas kernels, finish_sum(): pl.pallas_call(functools.partial(finish_kernel, axis, units_b, units_c),...  102 us
    pallas_call x1, Pallas kernels, attn_qkv_backward(): pl.pallas_call(functools.partial(attn_qkv_kernel, axis, head ** (-0.5), h...  95.4 us
    pallas_call x1, Pallas kernels, up_backward(): pl.pallas_call(functools.partial(up_bwd_kernel, axis, steps), grid=(steps...  60.3 us
    pallas_call x1, Pallas kernels, ffn_forward(): pl.pallas_call(ffn_kernel, grid=(f // tile,), out_shape=(sds((t, d), BF16...  53.7 us
    pallas_call x1, Pallas kernels, gather_embeddings(): pl.pallas_call(functools.partial(gather_kernel, axis), out_shape=jax.Shap...  35.2 us
    pallas_call x1, Pallas kernels, down_backward(): pl.pallas_call(down_bwd_kernel, grid=(f // tile,), out_shape=(sds((n, f,...  23.7 us
    pallas_call x1, Pallas kernels, unpack(): pl.pallas_call(unpack_kernel, out_shape=(sds((ff, d), F32), sds((d, ff),...  17.8 us
    pallas_call x2, Pallas kernels, attention(): pl.pallas_call(functools.partial(attn_kernel, head ** (-0.5), head), grid...  16.9 us

profile of v7, /device:TPU:1, one launch (start us, length us, event | category | flops | bytes accessed | tf_op | source)
XLA Modules:
  0.0 436.9 jit_solution(5837992708276050946)
XLA Ops:
  0.6 1.4 reshape.105.b_ref
  2.1 12.5 %qkv_project.1 = (bf16[192,3072]{1,0:T(8,128)(2,1)}, bf16[1024,3072]{1,0:T(8,128)(2,1)}) custom-call(bf16[192,1024]{1,0:T(8,128)(2,1)} %bitcast.49, bf16[1024,1024]{1,0:T(8,128)(2,1)} %bitcast.42, bf16[3072,1024]{1,0:T(8,128)(2,1)} %bitcast.39, f32[1,3072]{1,0:T(1,128)} %reshape.105.b_ref), custom_call_target="tpu_custom_call" | custom-call | tf_op jit(solution)/shard_map/qkv_project/pallas_call | solution.py:629
  14.5 5.2 %attention.2 = (bf16[4,8,96,48]{3,2,1,0:T(8,128)(2,1)}, bf16[192,1024]{1,0:T(8,128)(2,1)}) custom-call(bf16[192,3072]{1,0:T(8,128)(2,1)} %get-tuple-element.53.qkv_ref.qkvq_ref, s32[4,1,48]{2,1,0:T(1,128)} %bitcast.57), custom_call_target="tpu_custom_call" | custom-call | tf_op jit(solution)/shard_map/attention/pallas_call | solution.py:671
  19.7 11.7 %attention.3 = (bf16[8,8,256,128]{3,2,1,0:T(8,128)(2,1)}, bf16[1024,1024]{1,0:T(8,128)(2,1)}) custom-call(bf16[1024,3072]{1,0:T(8,128)(2,1)} %get-tuple-element.55.qkv_ref.qkvp_ref, s32[8,1,128]{2,1,0:T(1,128)} %bitcast.54), custom_call_target="tpu_custom_call" | custom-call | tf_op jit(solution)/shard_map/attention/pallas_call | solution.py:671
  31.4 53.7 %ffn_forward.1 = (bf16[1216,1024]{1,0:T(8,128)(2,1)}, f32[1216,1024]{1,0:T(8,128)}, bf16[1216,4096]{1,0:T(8,128)(2,1)}, f32[1216,4096]{1,0:T(8,128)}, f32[1216,1024]{1,0:T(8,128)}, /*index=5*/f32[16,1024]{1,0:T(8,128)}) custom-call(bf16[192,1024]{1,0:T(8,128)(2,1)} %bitcast.50, bf16[1024,1024]{1,0:T(8,128)(2,1)} %bitcast.43, ...), custom_call_target="tpu_custom_call" | custom-call | tf_op jit(solution)/shard_map/ffn_forward/pallas_call | solution.py:768
  85.2 0.0 copy-start
  85.2 0.8 copy-done
  86.0 35.2 %gather_embeddings.1 = f32[4,4,4,24,1024]{4,3,2,1,0:T(8,128)S(1)} custom-call(f32[16,1024]{1,0:T(8,128)S(1)} %copy-done), custom_call_target="tpu_custom_call" | custom-call | tf_op jit(solution)/shard_map/gather_embeddings/pallas_call | solution.py:472
  121.2 0.0 copy-done.1
  121.2 11.2 %loss_and_grad.1 = (f32[8,128]{1,0:T(8,128)S(1)}, f32[16,1024]{1,0:T(8,128)S(1)}) custom-call(f32[64,24,1024]{2,1,0:T(8,128)S(1)} %bitcast.38, f32[16,1024]{1,0:T(8,128)S(1)} %copy-done.1), custom_call_target="tpu_custom_call" | custom-call | tf_op jit(solution)/shard_map/loss_and_grad/pallas_call | solution.py:561
  132.4 0.6 copy-done.2
  133.0 0.5 slice.37
  133.6 23.7 %down_backward.1 = (f32[4,4096,256]{2,1,0:T(8,128)}, f32[1216,1024]{1,0:T(8,128)}, bf16[1216,1024]{1,0:T(8,128)(2,1)}, f32[8,1024]{1,0:T(8,128)}) custom-call(f32[16,1024]{1,0:T(8,128)} %copy-done.2, f32[1216,1024]{1,0:T(8,128)} %get-tuple-element.60.r2_ref, s32[4,48]{1,0:T(4,128)} %mq_ref.3, s32[8,128]{1,0:T(8,128)} %bitcast.56, f32[1,1024]{1,0:T(1,128)} %bitcast.60, ...), custom_call_target="tpu_custom_call" | custom-call | tf_op jit(solution)/shard_map/down_backward/pallas_call | solution.py:817
  157.2 60.3 %up_backward.1 = (f32[20,1024,256]{2,1,0:T(8,128)}, f32[1,4096]{1,0:T(1,128)}, f32[192,1024]{1,0:T(8,128)}, f32[1024,1024]{1,0:T(8,128)}, bf16[192,1024]{1,0:T(8...) custom-call(f32[1216,1024]{1,0:T(8,128)} %get-tuple-element.62.dr2_hbm, ...), custom_call_target="tpu_custom_call" | custom-call | tf_op jit(solution)/shard_map/up_backward/pallas_call | solution.py:944
  217.6 95.4 %attn_qkv_backward.1 = (f32[4,3072,256]{2,1,0:T(8,128)}, f32[1,3072]{1,0:T(1,128)}, bf16[192,1024]{1,0:T(8,128)(2,1)}, bf16[1024,1024]{1,0:T(8,128)(2,1)}, f32[1...) custom-call(bf16[192,1024]{1,0:T(8,128)(2,1)} %get-tuple-element.68.lowq_ref, ...), custom_call_target="tpu_custom_call" | custom-call | tf_op jit(solution)/shard_map/attn_qkv_backward/pallas_call | solution.py:1061
  313.0 102.1 %finish_sum.1 = (f32[45056,256]{1,0:T(8,128)S(1)}, f32[16,1024]{1,0:T(8,128)}, f32[6144,256]{1,0:T(8,128)}) custom-call(f32[160,256]{1,0:T(8,128)} %get-tuple-element.79.pieceb_ref, f32[12288,256]{1,0:T(8,128)} %bitcast.46, f32[16384,256]{1,0:T(8,128)} %get-tuple-element.78.a_ref.a_hbm, f32[8,1024]{1,0:T(8,128)} %get-tuple-element.81.vec1_ref, ...), custom_call_target="tpu_custom_call" | custom-call | tf_op jit(solution)/shard_map/finish_sum/pallas_call | solution.py:397
  415.1 0.0 copy-start.5
  415.1 0.0 copy-start.4
  415.1 17.8 %unpack.1 = (f32[4096,1024]{1,0:T(8,128)}, f32[1024,4096]{1,0:T(8,128)}, f32[1024,1024]{1,0:T(8,128)}, f32[3072,1024]{1,0:T(8,128)}) custom-call(f32[16384,256]{1,0:T(8,128)} %get-tuple-element.78.a_ref.a_hbm, f32[45056,256]{1,0:T(8,128)S(1)} %get-tuple-element.85.sums_ref), custom_call_target="tpu_custom_call" | custom-call | tf_op jit(solution)/shard_map/unpack/pallas_call | solution.py:1112
  432.9 0.6 copy.33
  433.5 0.6 fusion
  434.2 0.7 reshape.123
  434.9 0.7 copy.36
  435.6 1.3 copy.37
  (8 shorter events, 0.0 us)
Async XLA Ops:
  85.2 0.8 copy-start
  86.0 35.2 %copy-start.1 = (f32[16,1024]{1,0:T(8,128)S(1)}, f32[16,1024]{1,0:T(8,128)}, u32[]{:S(2)}) copy-start(f32[16,1024]{1,0:T(8,128)} %get-tuple-element.57.pooled_ref) | copy-start | bytes 196612
  132.4 0.6 copy-start.2
  415.1 17.8 %copy-start.5 = (f32[16,1024]{1,0:T(8,128)S(1)}, f32[16,1024]{1,0:T(8,128)}, u32[]{:S(2)}) copy-start(f32[16,1024]{1,0:T(8,128)} %get-tuple-element.87) | copy-start | bytes 196612
  415.1 19.8 %copy-start.4 = (bf16[192,1024]{1,0:T(8,128)(2,1)S(1)}, bf16[192,1024]{1,0:T(8,128)(2,1)}, u32[]{:S(2)}) copy-start(bf16[192,1024]{1,0:T(8,128)(2,1)} %get-tuple-element.76) | copy-start | bytes 1179652
  415.1 20.5 %copy-start.3 = (bf16[1024,1024]{1,0:T(8,128)(2,1)S(1)}, bf16[1024,1024]{1,0:T(8,128)(2,1)}, u32[]{:S(2)}) copy-start(bf16[1024,1024]{1,0:T(8,128)(2,1)} %get-tuple-element.77) | copy-start | bytes 6291460
